TPU v7x, 32 devices: a whole 2x2x4 slice. The times are simulated.
32 devices in a mesh: ctx: 16 (over z, y, core), head: 2 (over x).
Axes of the slice: x: 2, y: 2, z: 4, core: 2. Of those that a mesh axis runs over, the one named last changes fastest.
Arguments:
- queries: bfloat16 [8192, 16, 128], P('ctx', 'head'), may hold values from -130 to 130, as said below
- values: bfloat16 [8192, 16, 128], P('ctx', 'head'), may hold values from -6 to 6
- codes: int32 [8192, 16], P('ctx', 'head'), may hold values from 0 to 511
- codebook: bfloat16 [16, 512, 128], P('head'), may hold values from -8 to 8, as said below
- out_weight: bfloat16 [2048, 2048], P('head'), may hold values from -0.1875 to 0.1875
Outputs:
- mixed: bfloat16 [8192, 2048], P('ctx', 'head')
Inputs may be any that keep to these rules, and one draw needn't show every extreme that they name: `queries`: every entry has magnitude at most 130. `codebook`: every entry has magnitude at most 8.
All inputs are finite; a program needn't handle non-finite values.
Results may differ from a plain program's by a relative error of at most 0.0066.
Values may be sent and summed in bfloat16 or wider, within the bound.
No kernel may reach another device: no remote copies, remote signals or barrier semaphores. Data moves between devices by JAX's collectives and lax.ppermute only.
A program may use at most 128 MiB of HBM per device.

v0:
```python
import jax
import jax.numpy as jnp
from jax import lax
from jax.sharding import PartitionSpec as P

BLOCK = 512


def from_behind(value, axis, steps):
    count = lax.axis_size(axis)
    first, last = (max(0, -steps), min(count, count - steps))
    return lax.ppermute(value, axis, [(source, source + steps) for source in range(first, last)])


def prefix(x, axis, combine, identity):
    devices, here = (lax.axis_size(axis), lax.axis_index(axis))
    everything = jax.tree.map(lambda part: lax.all_gather(part, axis), x)
    start = jax.tree.map(
        lambda part, zero: jnp.broadcast_to(jnp.asarray(zero, part.dtype), part.shape), x, identity
    )

    def turn(k, before):
        reached = k < here
        new = combine(before, jax.tree.map(lambda part: part[k], everything))
        return jax.tree.map(lambda a, b: jnp.where(reached, a, b), new, before)

    return lax.fori_loop(0, devices, turn, start)


def attend(query, cur_keys, cur_values, prev_keys, prev_values, live, book, cache_sum, cache_count):
    scale = query.shape[-1] ** (-0.5)
    code_scores = jnp.dot(query, book.T, preferred_element_type=jnp.float32) * scale
    cur_scores = jnp.dot(query, cur_keys.T, preferred_element_type=jnp.float32) * scale
    prev_scores = jnp.dot(query, prev_keys.T, preferred_element_type=jnp.float32) * scale
    rows = lax.broadcasted_iota(jnp.int32, cur_scores.shape, 0)
    cols = lax.broadcasted_iota(jnp.int32, cur_scores.shape, 1)
    causal = rows >= cols
    present = (cache_count > 0.0)[None, :]
    top = jnp.max(jnp.where(causal, cur_scores, -jnp.inf), axis=1)
    top = jnp.maximum(top, jnp.max(jnp.where(live, prev_scores, -jnp.inf), axis=1))
    top = jnp.maximum(top, jnp.max(jnp.where(present, code_scores, -jnp.inf), axis=1))
    top = top[:, None]
    cur_weight = jnp.where(causal, jnp.exp(cur_scores - top), 0.0)
    prev_weight = jnp.where(live, jnp.exp(prev_scores - top), 0.0)
    code_weight = jnp.where(present, jnp.exp(code_scores - top), 0.0)
    denom = (
        jnp.sum(cur_weight, axis=1)
        + jnp.sum(prev_weight, axis=1)
        + jnp.sum(code_weight * cache_count[None, :], axis=1)
    )
    numer = jnp.dot(cur_weight.astype(jnp.bfloat16), cur_values, preferred_element_type=jnp.float32)
    numer = numer + jnp.dot(
        prev_weight.astype(jnp.bfloat16), prev_values, preferred_element_type=jnp.float32
    )
    numer = numer + jnp.dot(code_weight, cache_sum, precision=lax.Precision.HIGHEST)
    return (numer / denom[:, None]).astype(jnp.bfloat16)


def add_totals(earlier, later):
    return (earlier[0] + later[0], earlier[1] + later[1])


def on_device(queries, values, codes, codebook, out_weight):
    tokens, local_heads, width = queries.shape
    ncodes = codebook.shape[1]
    nblocks = tokens // BLOCK
    keys = jax.vmap(lambda book, index: book[index], in_axes=(0, 1), out_axes=1)(codebook, codes)
    table = lax.broadcasted_iota(jnp.int32, (1, 1, ncodes), 2)
    onehot = (
        (codes[:, :, None] == table)
        .astype(jnp.bfloat16)
        .reshape(nblocks, BLOCK, local_heads, ncodes)
    )
    block_sums = jnp.einsum(
        "bths,bthd->bhsd",
        onehot,
        values.reshape(nblocks, BLOCK, local_heads, width),
        preferred_element_type=jnp.float32,
    )
    block_counts = jnp.sum(onehot.astype(jnp.float32), axis=1)
    last_sum, last_count = (block_sums[nblocks - 1], block_counts[nblocks - 1])
    rest_sum = jnp.sum(block_sums[: nblocks - 1], axis=0)
    rest_count = jnp.sum(block_counts[: nblocks - 1], axis=0)
    prev_keys, prev_values = from_behind((keys, values), "ctx", 1)
    zero_sum = jnp.zeros_like(last_sum)
    zero_count = jnp.zeros_like(last_count)
    total_sum, total_count = prefix(
        (rest_sum + last_sum, rest_count + last_count), "ctx", add_totals, (zero_sum, zero_count)
    )
    pend_sum, pend_count = from_behind((last_sum, last_count), "ctx", 1)
    cache_sum = total_sum - pend_sum
    cache_count = total_count - pend_count
    live = lax.axis_index("ctx") > 0
    attended = jax.vmap(attend, in_axes=(1, 1, 1, 1, 1, None, 0, 0, 0), out_axes=1)(
        queries, keys, values, prev_keys, prev_values, live, codebook, cache_sum, cache_count
    )
    attended_all = attended.reshape(tokens, local_heads * width)
    columns = lax.all_to_all(out_weight, "head", split_axis=1, concat_axis=0, tiled=True)
    summed = jnp.dot(
        lax.all_gather(attended_all, "head", axis=1, tiled=True),
        columns,
        preferred_element_type=jnp.float32,
    )
    return summed.astype(jnp.bfloat16)


def solution(mesh):
    return jax.shard_map(
        on_device,
        mesh=mesh,
        in_specs=(
            P("ctx", "head", None),
            P("ctx", "head", None),
            P("ctx", "head"),
            P("head", None, None),
            P("head", None),
        ),
        out_specs=P("ctx", "head"),
        check_vma=False,
    )
```

profile of v0, /device:TPU:0, one launch (start us, length us, event | category | flops | bytes accessed | tf_op | source)
XLA Modules:
  0.0 355.7 jit_solution(16759261698368009623)
XLA Ops:
  6.5 2.5 copy.66
  9.0 4.0 %fusion.3 = f32[8,512,128]{2,1,0:T(8,128)} fusion(bf16[512,8,128]{0,2,1:T(8,128)(2,1)} %copy.66, s32[512,8]{0,1:T(8,128)} %param.9), kind=kOutput, calls=%fused_computation.18 | convolution fusion | flops 538968064 | bytes 3162112 | tf_op jit(solution)/shard_map/bths,bthd->bhsd/dot_general | solution.py:74
  13.1 40.2 %gather_fusion = bf16[4096,128]{1,0:T(8,128)(2,1)} fusion(bf16[8,512,128]{2,1,0:T(8,128)(2,1)S(1)} %copy-done, s32[4096]{0:T(1024)S(1)} %bitcast.65), kind=kCustom, calls=%fused_computation | custom fusion | bytes 2129920 | tf_op jit(solution)/shard_map/vmap()/gather | solution.py:67
  53.3 3.4 collective-permute-start
  56.6 4.5 %collective-permute-start.2 = (bf16[512,8,128]{0,2,1:T(8,128)(2,1)}, bf16[512,8,128]{0,2,1:T(8,128)(2,1)}, u32[]{:S(2)}, u32[]{:S(2)}) collective-permute-start(bf16[512,8,128]{0,2,1:T(8,128)(2,1)} %copy.66), channel_id=1, source_target_pairs={{0,2},{2,4},{4,6},{6,8},{8,10},{10,12},{12,14},{14,16},{16,18},{18... | collective-permute-start | bytes 3145736 | tf_op jit(solution)/shard_map/ppermute | solution.py:12
  61.2 2.6 collective-permute-start.3
  66.8 6.5 %copy.70 = bf16[1024,2048]{0,1:T(8,128)(2,1)} copy(bf16[1024,2048]{1,0:T(8,128)(2,1)} %param.11) | data formatting | bytes 8388608 | tf_op args[4]
  73.2 5.6 %all-to-all-start = ((bf16[1024,2,1024]{0,2,1:T(8,128)(2,1)}), bf16[1024,2,1024]{0,2,1:T(8,128)(2,1)}, u32[]{:S(2)}, u32[]{:S(2)}) async-start(bf16[1024,2,1024]{0,2,1:T(8,128)(2,1)} %bitcast.70), calls=%async_computation | async-start | bytes 8388608 | tf_op jit(solution)/shard_map/all_to_all | solution.py:98
  79.0 132.5 %all-gather.1 = f32[128,512]{1,0:T(8,128)} all-gather(f32[8,512]{1,0:T(8,128)S(1)} %convert_reduce_fusion), channel_id=3, replica_groups=mesh['ctx'=16,'head'=2] {'ctx'}, dimensions={0}, use_global_device_ids=true | all-gather | bytes 278528 | tf_op jit(solution)/shard_map/all_gather | solution.py:17
  211.5 6.2 %fusion = (f32[8,512]{1,0:T(8,128)S(1)}, f32[8,512,512]{2,1,0:T(8,128)}) fusion(pred[512,512]{0,1:T(8,128)(4,1)S(1)} %iota_compare_fusion.3, bf16[8,512,128]{2,1,0:T(8,128)(2,1)} %bitcast.2, bf16[512,8,128]{2,1,0:T(8,128)(2,1)} %param.7), kind=kOutput, calls=%fused_computation.7 | convolution fusion | flops 543158272 | bytes 10764288 | tf_op jit(solution)/shard_map/vmap()/dot_general | solution.py:33
  217.7 5.7 %select_reduce_fusion.1 = (f32[8,512]{1,0:T(8,128)S(1)}, f32[8,512,512]{1,2,0:T(8,128)}) fusion(pred[]{:T(512)S(6)} %gt.6, bf16[512,8,128]{2,1,0:T(8,128)(2,1)S(1)} %copy-done.2, bf16[512,8,128]{2,0,1:T(8,128)(2,1)} %collective-permute-done), kind=kOutput, calls=%fused_computation.17 | convolution fusion | flops 543158272 | bytes 10502145 | tf_op jit(solution)/shard_map/vmap()/dot_general | solution.py:34
  223.4 3.9 %all-gather.7.cloned.1.call-done = f32[128,512,128]{2,1,0:T(8,128)} async-done(((f32[8,512,128]{2,1,0:T(8,128)}), f32[128,512,128]{2,1,0:T(8,128)}) %all-gather.7.cloned.1.call-update) | async-done | bytes 33554448 | tf_op jit(solution)/shard_map/all_gather | solution.py:17
  227.3 48.6 %while.16 = (s32[]{:T(128)}, f32[8,512,128]{2,1,0:T(8,128)S(1)}, f32[8,512]{1,0:T(8,128)S(1)}, s32[]{:T(128)}, f32[16,8,512,128]{3,2,1,0:T(8,128)}, /*index=5*/f32[16,8,512]{2,1,0:T(8,128)}, s32[]{:T(128)}, s32[]{:T(128)}) while((s32[]{:T(128)}, f32[8,512,128]{2,1,0:T(8,128)S(1)}, f32[8,512]{1,0:T(8,128)S(1)}, s32[]{:T(128)}, ...), condition=%wide.region_4.5_spmd.clone, body=%wide.region_3.4_spmd.clone.sunk | while | flops 1585156 | bytes 6340723 | solution.py:27
  227.3 2.3 add_select_fusion.4
  230.4 2.3 add_select_fusion.4
  233.4 2.3 add_select_fusion.4
  242.5 2.3 add_select_fusion.4
  245.5 2.3 add_select_fusion.4
  248.6 2.3 add_select_fusion.4
  251.6 2.3 add_select_fusion.4
  260.7 2.3 add_select_fusion.4
  263.8 2.3 add_select_fusion.4
  266.8 2.3 add_select_fusion.4
  269.8 2.3 add_select_fusion.4
  275.9 3.5 select_reduce_fusion
  279.5 7.9 %fusion.6 = (f32[8,512]{1,0:T(8,128)S(1)}, f32[8,512]{1,0:T(8,128)S(1)}) fusion(f32[8,512,512]{2,1,0:T(8,128)} %get-tuple-element.157, f32[8,512]{1,0:T(8,128)S(1)} %maximum_maximum_fusion, pred[512,512]{0,1:T(8,128)(4,1)S(1)} %iota_compare_fusion.3, f32[8,512]{1,0:T(8,128)S(1)} %get-tuple-element.153, f32[8,512,512]{1,2,0:T(8,128)S(1)} %get-tuple-element.155, ...), kind=kLoop, calls=%fused_computation.21 | loop fusion | flops 18866176 | bytes 17108992 | tf_op jit(solution)/shard_map/vmap()/reduce_sum | solution.py:47
  289.6 3.3 fusion.8
  292.9 3.2 fusion.10
  296.1 9.2 %fusion.24 = bf16[512,8,128]{0,2,1:T(8,128)(2,1)} fusion(f32[8,512,128]{1,2,0:T(8,128)S(1)} %fusion.8, f32[8,512,128]{1,2,0:T(8,128)S(1)} %fusion.10, f32[512,8]{0,1:T(8,128)S(1)} %add_bitcast_fusion, f32[8,512,128]{2,1,0:T(8,128)S(1)} %get-tuple-element.116, f32[8,512,128]{2,1,0:T(8,128)} %collective-permute-done.3, ...), kind=kOutput, calls=%fused_computation.39 | convolution fusion | flops 3230138368 | bytes 17862656 | tf_op jit(solution)/shard_map/vmap()/dot_general | solution.py:55
  305.3 6.3 %copy.71 = bf16[2,1024,1024]{2,1,0:T(8,128)(2,1)} copy(bf16[2,1024,1024]{1,2,0:T(8,128)(2,1)} %bitcast.13) | data formatting | bytes 8388608 | tf_op jit(solution)/shard_map/all_to_all | solution.py:98
  311.6 31.1 %all-gather.5.cloned.1.call-done = bf16[512,2048]{0,1:T(8,128)(2,1)} async-done(((bf16[512,1024]{0,1:T(8,128)(2,1)}), bf16[512,2048]{0,1:T(8,128)(2,1)}) %all-gather.5.cloned.1.call-update) | async-done | bytes 2097168 | tf_op jit(solution)/shard_map/all_gather | solution.py:100
  342.8 6.1 %convolution_convert_fusion = bf16[512,1024]{1,0:T(8,128)(2,1)} fusion(bf16[512,2048]{0,1:T(8,128)(2,1)} %all-gather.5.cloned.1.call-done, bf16[2048,1024]{1,0:T(8,128)(2,1)} %bitcast.71), kind=kOutput, calls=%fused_computation.41 | convolution fusion | flops 2148007936 | bytes 7340032 | tf_op jit(solution)/shard_map/dot_general | solution.py:99
  (60 shorter events, 28.5 us)
Async XLA Ops:
  6.5 6.6 %copy-start = (bf16[8,512,128]{2,1,0:T(8,128)(2,1)S(1)}, bf16[8,512,128]{2,1,0:T(8,128)(2,1)}, u32[]{:S(2)}) copy-start(bf16[8,512,128]{2,1,0:T(8,128)(2,1)} %param.10) | copy-start | bytes 3145732
  6.5 6.5 %copy-start.3 = (s32[512,8]{0,1:T(8,128)S(1)}, s32[512,8]{0,1:T(8,128)}, u32[]{:S(2)}) copy-start(s32[512,8]{0,1:T(8,128)} %param.9) | copy-start | bytes 49156
  6.5 220.8 %all-gather.7.cloned.1.call-start = ((), (), s32[]{:S(2)}) async-start(), calls=%async_computation.2 | async-start | bytes 35651584 | tf_op jit(solution)/shard_map/all_gather | solution.py:17
  53.3 164.5 %collective-permute-start = (bf16[512,8,128]{2,0,1:T(8,128)(2,1)}, bf16[512,8,128]{2,0,1:T(8,128)(2,1)}, u32[]{:S(2)}, u32[]{:S(2)}) collective-permute-start(bf16[512,8,128]{2,0,1:T(8,128)(2,1)} %bitcast.4), channel_id=1, source_target_pairs={{0,2},{2,4},{4,6},{6,8},{8,10},{10,12},{12,14},{14,16},{16,18},{18... | collective-permute-start | bytes 3145736 | tf_op jit(solution)/shard_map/ppermute | solution.py:12
  56.6 236.2 %collective-permute-start.2 = (bf16[512,8,128]{0,2,1:T(8,128)(2,1)}, bf16[512,8,128]{0,2,1:T(8,128)(2,1)}, u32[]{:S(2)}, u32[]{:S(2)}) collective-permute-start(bf16[512,8,128]{0,2,1:T(8,128)(2,1)} %copy.66), channel_id=1, source_target_pairs={{0,2},{2,4},{4,6},{6,8},{8,10},{10,12},{12,14},{14,16},{16,18},{18... | collective-permute-start | bytes 3145736 | tf_op jit(solution)/shard_map/ppermute | solution.py:12
  61.2 234.9 %collective-permute-start.3 = (f32[8,512,128]{2,1,0:T(8,128)}, f32[8,512,128]{2,1,0:T(8,128)}, u32[]{:S(2)}, u32[]{:S(2)}) collective-permute-start(f32[8,512,128]{2,1,0:T(8,128)} %fusion.3), channel_id=1, source_target_pairs={{0,2},{2,4},{4,6},{6,8},{8,10},{10,12},{12,14},{14,16},{16,18},{18... | collective-permute-start | bytes 6291464 | tf_op jit(solution)/shard_map/ppermute | solution.py:12
  64.9 211.0 %collective-permute-start.1 = (f32[8,512]{1,0:T(8,128)S(1)}, f32[8,512]{1,0:T(8,128)S(1)}, u32[]{:S(2)}, u32[]{:S(2)}) collective-permute-start(f32[8,512]{1,0:T(8,128)S(1)} %convert_reduce_fusion), channel_id=1, source_target_pairs={{0,2},{2,4},{4,6},{6,8},{8,10},{10,12},{12,14},{14,16},{16,18},{18... | collective-permute-start | bytes 49160 | tf_op jit(solution)/shard_map/ppermute | solution.py:12
  73.2 232.1 %all-to-all-start = ((bf16[1024,2,1024]{0,2,1:T(8,128)(2,1)}), bf16[1024,2,1024]{0,2,1:T(8,128)(2,1)}, u32[]{:S(2)}, u32[]{:S(2)}) async-start(bf16[1024,2,1024]{0,2,1:T(8,128)(2,1)} %bitcast.70), calls=%async_computation | async-start | bytes 8388608 | tf_op jit(solution)/shard_map/all_to_all | solution.py:98
  78.8 263.9 %all-gather.5.cloned.1.call-start = ((), (), s32[]{:S(2)}) async-start(), calls=%async_computation.1 | async-start | bytes 3145728 | tf_op jit(solution)/shard_map/all_gather | solution.py:100
  78.9 138.8 %copy-start.2 = (bf16[512,8,128]{2,1,0:T(8,128)(2,1)S(1)}, bf16[512,8,128]{2,1,0:T(8,128)(2,1)}, u32[]{:S(2)}) copy-start(bf16[512,8,128]{2,1,0:T(8,128)(2,1)} %param.7) | copy-start | bytes 3145732
  275.9 11.5 %slice-start.2 = ((s8[8388608]{0:T(1024)(128)(4,1)}), s8[4194304]{0:T(1024)(128)(4,1)S(1)}, s32[]{:S(2)}) async-start(s8[8388608]{0:T(1024)(128)(4,1)} %bitcast.68), calls=%async_computation.5 | async-start | bytes 8388608
  275.9 13.7 %slice-start = ((s8[8388608]{0:T(1024)(128)(4,1)}), s8[4194304]{0:T(1024)(128)(4,1)S(1)}, s32[]{:S(2)}) async-start(s8[8388608]{0:T(1024)(128)(4,1)} %bitcast.66), calls=%async_computation.3 | async-start | bytes 8388608
  279.4 7.9 %slice-start.3 = ((s8[8388608]{0:T(1024)(128)(4,1)}), s8[4194304]{0:T(1024)(128)(4,1)S(1)}, s32[]{:S(2)}) async-start(s8[8388608]{0:T(1024)(128)(4,1)} %bitcast.68), calls=%async_computation.6 | async-start | bytes 8388608
  279.4 10.1 %slice-start.1 = ((s8[8388608]{0:T(1024)(128)(4,1)}), s8[4194304]{0:T(1024)(128)(4,1)S(1)}, s32[]{:S(2)}) async-start(s8[8388608]{0:T(1024)(128)(4,1)} %bitcast.66), calls=%async_computation.4 | async-start | bytes 8388608
  305.3 43.6 %copy-start.1 = (bf16[8,512,128]{2,1,0:T(8,128)(2,1)S(1)}, bf16[8,512,128]{2,1,0:T(8,128)(2,1)}, u32[]{:S(2)}) copy-start(bf16[8,512,128]{2,1,0:T(8,128)(2,1)} %param.10) | copy-start | bytes 3145732
Sparse Core Ops, SparseCore 0:
  13.2 214.1 all-gather.6
  305.4 37.2 all-gather.4
where the time goes:
time: 358 us; the launch traced here: 356 us
  blocking collectives  132 us (37%)
  other arithmetic  59.6 us (17%)
  local copies, waits for them, and re-layouts  55.6 us (16%)
  matrix products  41.2 us (12%)
  waiting for transfers between devices  35.1 us (10%)
  starting transfers between devices  18 us (5%)
  between operations  13.7 us (4%)
    all_gather x1, blocking collectives, prefix(): everything = jax.tree.map(lambda part: lax.all_gather(part, axis), x)  132 us
    select_n x32, other arithmetic, turn(): return jax.tree.map(lambda a, b: jnp.where(reached, a, b), new, before)  48.5 us
    gather x1, local copies, waits for them, and re-layouts, on_device(): book[index]  40.2 us
    all_gather x1, waiting for transfers between devices, on_device(): lax.all_gather(attended_all, 'head', axis=1, tiled=True)  31.1 us
    ppermute x4, starting transfers between devices, from_behind(): lax.ppermute(value, axis, [(source, source + steps) for source in range(f...  12.4 us
    dot_general x1, matrix products, attend(): jnp.dot(code_weight, cache_sum, precision=lax.Precision.HIGHEST)  9.17 us
    unnamed x20, local copies, waits for them, and re-layouts  9.13 us
    reduce_sum x1, other arithmetic, attend(): jnp.sum(cur_weight, axis=1) + jnp.sum(prev_weight, axis=1)  7.9 us
  transfers between devices with their start and end apart: 7, of which 2 were waited for; matrix products, arithmetic and copies ran while one was open for 40% of the time, Pallas kernels for 0%

commit v1 on v0

v1 whole, which is shorter than its diff:
```python
import functools
import math

import jax
import jax.numpy as jnp
from jax import lax
from jax.experimental import pallas as pl
from jax.experimental.pallas import tpu as pltpu
from jax.sharding import PartitionSpec as P

BLOCK = 512
LANES = 128
GROUPS = 4
NEVER = -1e30
F32 = jnp.float32
BF16 = jnp.bfloat16


def dot(a, b, contract=((1,), (0,))):
    return lax.dot_general(a, b, (contract, ((), ())), preferred_element_type=F32)


class Layout:
    def __init__(self, devices, heads, ncodes):
        self.groups = math.gcd(GROUPS, heads)
        self.heads = heads // self.groups
        self.each = ncodes // LANES
        self.units = self.heads * self.each
        self.per = self.units // 4
        self.shift = int(math.log2(256 // devices + 1))
        self.digits = 1
        while (1 << (self.shift * self.digits)) <= BLOCK:
            self.digits += 1
        self.sums = self.per * LANES
        self.tail = -(-self.digits * self.per // 16) * 16
        self.rows = self.sums + self.tail
        assert ncodes % LANES == 0 and self.units % 4 == 0 and devices % 4 == 0


def sums_kernel(lay, pos_ref, codes_ref, values_ref, *refs):
    outs, buf = (refs[:-1], refs[-1])
    core, row = (pos_ref[0], pos_ref[1])
    heads, tokens = codes_ref.shape
    ncodes = lay.each * LANES
    by_head = jnp.swapaxes(values_ref[...], 0, 1)
    table = lax.broadcasted_iota(jnp.int32, (ncodes, tokens), 0)
    line = lax.broadcasted_iota(jnp.int32, (lay.tail, LANES), 0)
    ones = jnp.ones((8, tokens), BF16)
    mask = (1 << lay.shift) - 1
    for g in range(lay.groups):
        tails = [jnp.zeros((lay.tail, LANES), F32) for _ in range(4)]
        for k in range(lay.heads):
            h = g * lay.heads + k
            onehot = (table == codes_ref[h : h + 1, :]).astype(BF16)
            sums = dot(onehot, by_head[h]).astype(BF16)
            count = dot(ones, onehot, ((1,), (1,)))[0:1].astype(jnp.int32)
            for j in range(lay.each):
                piece, at = divmod(k * lay.each + j, lay.per)
                a, b = (piece // 2 ^ core, piece % 2 ^ row)
                buf[a, b, at * LANES : (at + 1) * LANES, :] = sums[j * LANES : (j + 1) * LANES]
                part = count[:, j * LANES : (j + 1) * LANES]
                for d in range(lay.digits):
                    digit = ((part >> (lay.shift * d)) & mask).astype(F32)
                    tails[piece] = jnp.where(line == d * lay.per + at, digit, tails[piece])
        for piece in range(4):
            buf[piece // 2 ^ core, piece % 2 ^ row, lay.sums :, :] = tails[piece].astype(BF16)
        outs[2 * g][...] = buf[0]
        outs[2 * g + 1][...] = buf[1]


def block_sums(lay, pos, codes, values):
    tokens, heads, width = values.shape
    piece = jax.ShapeDtypeStruct((2, lay.rows, LANES), BF16)
    vmem = pl.BlockSpec(memory_space=pltpu.VMEM)
    outs = pl.pallas_call(
        functools.partial(sums_kernel, lay),
        out_shape=[piece] * (2 * lay.groups),
        in_specs=[pl.BlockSpec(memory_space=pltpu.SMEM), vmem, vmem],
        out_specs=[vmem] * (2 * lay.groups),
        scratch_shapes=[pltpu.VMEM((2, 2, lay.rows, LANES), BF16)],
        cost_estimate=pl.CostEstimate(
            flops=2 * heads * tokens * lay.each * LANES * width * 2, bytes_accessed=4 * tokens * heads * width, transcendentals=0
        ),
        name="block_sums",
    )(pos, codes, values)
    return [(outs[2 * g], outs[2 * g + 1]) for g in range(lay.groups)]


def window_kernel(factor, codes_ref, queries_ref, values_ref, book_ref, qt_ref, num_ref, ml_ref, vt_ref):
    heads, tokens = codes_ref.shape
    ncodes = book_ref.shape[1]
    tile = tokens // 2
    qt_ref[...] = jnp.swapaxes(queries_ref[...], 0, 1)
    vt_ref[...] = jnp.swapaxes(values_ref[...], 0, 1)
    table = lax.broadcasted_iota(jnp.int32, (ncodes, tokens), 0)
    lane = lax.broadcasted_iota(jnp.int32, (tile, LANES), 1)
    causal = lax.broadcasted_iota(jnp.int32, (tile, tile), 0) >= lax.broadcasted_iota(jnp.int32, (tile, tile), 1)

    def one(h, carry):
        onehot = (table == codes_ref[pl.ds(h, 1), :]).astype(BF16)
        keys = dot(book_ref[h], onehot, ((0,), (0,))).astype(BF16)
        value = vt_ref[h]
        for r in range(2):
            rows = slice(r * tile, (r + 1) * tile)
            query = qt_ref[h, rows, :]
            score = jnp.where(causal, dot(query, keys[:, rows]), NEVER)
            top = jnp.max(score, axis=1, keepdims=True)
            if r:
                early = dot(query, keys[:, :tile])
                top = jnp.maximum(top, jnp.max(early, axis=1, keepdims=True))
            weight = jnp.exp2((score - top) * factor)
            den = jnp.sum(weight, axis=1, keepdims=True)
            num = dot(weight.astype(BF16), value[rows])
            if r:
                weight = jnp.exp2((early - top) * factor)
                den += jnp.sum(weight, axis=1, keepdims=True)
                num += dot(weight.astype(BF16), value[:tile])
            num_ref[h, rows, :] = num
            ml_ref[h, rows, :] = jnp.where(lane < LANES // 2, top, den)
        return carry

    lax.fori_loop(0, heads, one, 0)


def window(codes, queries, values, book):
    tokens, heads, width = queries.shape
    vmem = pl.BlockSpec(memory_space=pltpu.VMEM)
    factor = width ** (-0.5) * math.log2(math.e)
    flops = 2 * heads * tokens * tokens * width * 3
    return pl.pallas_call(
        functools.partial(window_kernel, factor),
        out_shape=[
            jax.ShapeDtypeStruct((heads, tokens, width), BF16),
            jax.ShapeDtypeStruct((heads, tokens, width), F32),
            jax.ShapeDtypeStruct((heads, tokens, LANES), F32),
        ],
        in_specs=[vmem] * 4,
        out_specs=[vmem] * 3,
        scratch_shapes=[pltpu.VMEM((heads, tokens, width), BF16)],
        cost_estimate=pl.CostEstimate(flops=flops * 4, bytes_accessed=9 * tokens * heads * width, transcendentals=0),
        name="window",
    )(codes, queries, values, book)


def codes_kernel(lay, factor, pos_ref, qt_ref, book_ref, num_ref, ml_ref, mine_ref, theirs_ref, out_ref):
    core, row = (pos_ref[0], pos_ref[1])
    width = qt_ref.shape[2]

    def piece(p, rows):
        b = p % 2 ^ row
        return jnp.where(p // 2 == core, mine_ref[b, rows, :].astype(F32), theirs_ref[b, rows, :].astype(F32))

    tails = [piece(p, slice(lay.sums, lay.rows)) for p in range(4)]
    for k in range(lay.heads):
        sums, counts = ([], [])
        for j in range(lay.each):
            p, at = divmod(k * lay.each + j, lay.per)
            sums.append(piece(p, slice(at * LANES, (at + 1) * LANES)).astype(BF16))
            count = 0.0
            for d in range(lay.digits):
                line = d * lay.per + at
                count = count + tails[p][line : line + 1] * float(1 << (lay.shift * d))
            counts.append(count)
        cache = jnp.concatenate(sums, axis=0)
        count = jnp.concatenate(counts, axis=1)
        score = dot(qt_ref[k], book_ref[k], ((1,), (1,)))
        score = score + jnp.where(count > 0.5, 0.0, NEVER)
        early = ml_ref[k, :, 0:1]
        top = jnp.maximum(early, jnp.max(score, axis=1, keepdims=True))
        weight = jnp.exp2((score - top) * factor)
        keep = jnp.exp2((early - top) * factor)
        den = keep * ml_ref[k, :, LANES // 2 : LANES // 2 + 1] + jnp.sum(weight * count, axis=1, keepdims=True)
        num = keep * num_ref[k] + dot(weight.astype(BF16), cache)
        out_ref[:, k * width : (k + 1) * width] = (num / den).astype(BF16)


def attend(lay, g, pos, qt, book, num, ml, mine, theirs):
    heads, tokens, width = qt.shape
    ncodes = book.shape[1]
    vmem = pl.BlockSpec(memory_space=pltpu.VMEM)
    factor = width ** (-0.5) * math.log2(math.e)
    part = lambda n: pl.BlockSpec((lay.heads, n, width), lambda i: (g, 0, 0))
    whole = lambda x: pl.BlockSpec(x.shape, lambda i: (0,) * x.ndim)
    out = jax.ShapeDtypeStruct((tokens, lay.heads * width), BF16)
    return pl.pallas_call(
        functools.partial(codes_kernel, lay, factor),
        out_shape=out,
        grid=(1,),
        in_specs=[pl.BlockSpec(memory_space=pltpu.SMEM), part(tokens), part(ncodes), part(tokens), part(tokens), whole(mine), whole(theirs)],
        out_specs=whole(out),
        cost_estimate=pl.CostEstimate(
            flops=2 * lay.heads * tokens * ncodes * width * 8, bytes_accessed=14 * tokens * lay.heads * width, transcendentals=0
        ),
        name="attend",
    )(pos, qt, book, num, ml, mine, theirs)


def swap(x, axis, k):
    return lax.ppermute(x, axis, [(i, i ^ k) for i in range(lax.axis_size(axis))])


def ahead(x, axis, k):
    return lax.ppermute(x, axis, [(i, i + k) for i in range(lax.axis_size(axis) - k)])


def add(a, b):
    return (a.astype(F32) + b.astype(F32)).astype(BF16)


def earlier_totals(x, axis, stride):
    count = lax.axis_size(axis) // stride
    if count <= 4:
        parts = [ahead(x, axis, stride * d) for d in range(1, count)]
        total = sum((part.astype(F32) for part in parts), jnp.zeros(x.shape, F32))
        return total.astype(BF16)
    total = ahead(x, axis, stride)
    upto, d = (add(x, total), 2)
    while d < count:
        part = ahead(upto, axis, stride * d)
        total, upto, d = (add(total, part), add(upto, part), 2 * d)
    return total


def prefix(keep, give, core, row):
    got = swap(give, "ctx", 1)
    low1 = jnp.where(core == 1, got, keep)
    mine, send = (add(keep[0], got[0]), add(keep[1], got[1]))
    got = swap(send, "ctx", 2)
    low2 = jnp.where(row == 1, got, mine)
    before = earlier_totals(add(mine, got), "ctx", 4)
    with_low = add(before, low2)
    got = swap(jnp.where(row == 1, before, with_low), "ctx", 2)
    before = jnp.stack([jnp.where(row == 1, with_low, before), got])
    with_low = add(before, low1)
    got = swap(jnp.where(core == 1, before, with_low), "ctx", 1)
    return jnp.where(core == 1, with_low, before), got


def on_device(queries, values, codes, codebook, out_weight):
    tokens, heads, width = queries.shape
    assert tokens == BLOCK
    devices = lax.axis_size("ctx")
    here, side = (lax.axis_index("ctx"), lax.axis_index("head"))
    sides = lax.axis_size("head")
    core, row = (here & 1, here >> 1 & 1)
    pos = jnp.stack([core, row]).astype(jnp.int32)
    lay = Layout(devices, heads, codebook.shape[1])
    codes = codes.T

    rows, columns = (out_weight.shape[0], out_weight.shape[1] // sides)
    half = rows // 2
    weights = {0: lax.dynamic_slice(out_weight, (0, side * columns), (rows, columns))}
    for k in range(1, sides):
        block = lax.dynamic_slice(out_weight, (core * half, (side ^ k) * columns), (half, columns))
        mine = swap(block, "head", k)
        other = swap(mine, "ctx", 1)
        first = core == 0
        weights[k] = jnp.stack([jnp.where(first, mine, other), jnp.where(first, other, mine)]).reshape(rows, columns)

    pieces = block_sums(lay, pos, codes, values)
    qt, num, ml = window(codes, queries, values, codebook)
    wide = lay.heads * width
    total = jnp.zeros((tokens, columns), F32)
    for g, (keep, give) in enumerate(pieces):
        mine, theirs = prefix(keep, give, core, row)
        attended = attend(lay, g, pos, qt, codebook, num, ml, mine, theirs)
        for k in range(sides):
            part = attended if k == 0 else swap(attended, "head", k)
            total = total + dot(part, weights[k][g * wide : (g + 1) * wide])
    return total.astype(BF16)


def solution(mesh):
    return jax.shard_map(
        on_device,
        mesh=mesh,
        in_specs=(
            P("ctx", "head", None),
            P("ctx", "head", None),
            P("ctx", "head"),
            P("head", None, None),
            P("head", None),
        ),
        out_specs=P("ctx", "head"),
        check_vma=False,
    )
```

time: 358 us -> 105 us (0.29)
  blocking collectives: 132 us -> 0 us
  other arithmetic: 59.6 us -> 4.46 us
  local copies, waits for them, and re-layouts: 55.6 us -> 3.98 us
  Pallas kernels: 0 us -> 38.7 us
  waiting for transfers between devices: 35.1 us -> 1.48 us
  matrix products: 41.2 us -> 9.2 us
  starting transfers between devices: 18 us -> 46.1 us
  between operations: 13.7 us -> 0.44 us
    all_gather x1 -> x0, blocking collectives: 132 us -> none  [prefix(): everything = jax.tree.map(lambda part: lax.all_gather(part, axis), x)]
    select_n x32 -> x4, other arithmetic: 48.5 us -> 2.97 us  [prefix(): got = swap(jnp.where(core == 1, before, with_low), 'ctx', 1)]
    gather x1 -> x0, local copies, waits for them, and re-layouts: 40.2 us -> none  [on_device(): book[index]]
    pallas_call x0 -> x6, Pallas kernels: none -> 38.7 us  [the longest x4 22 us: attend(): pl.pallas_call(functools.partial(codes_kernel, lay, factor), out_shape=ou...]
    all_gather x2 -> x0, waiting for transfers between devices: 35 us -> none  [the longest x1 31.1 us: on_device(): lax.all_gather(attended_all, 'head', axis=1, tiled=True)]
    ppermute x4 -> x34, starting transfers between devices: 12.4 us -> 46.1 us  [the longest x12 28.8 us: ahead(): lax.ppermute(x, axis, [(i, i + k) for i in range(lax.axis_size(axis) - k)])]
    dot_general x8, matrix products: 41.2 us -> 9.2 us  [dot(): lax.dot_general(a, b, (contract, ((), ())), preferred_element_type=F32)]
    reduce_sum x3 -> x0, other arithmetic: 11 us -> none  [the longest x1 7.9 us: attend(): jnp.sum(cur_weight, axis=1) + jnp.sum(prev_weight, axis=1)]
  transfers between devices with their start and end apart: 7 -> 34, of which waited for: 2 -> 3; matrix products, arithmetic and copies ran while one was open for 40% -> 11% of each run, Pallas kernels for 0% -> 37%
where the time goes in v1:
time: 105 us; the launch traced here: 104 us
  starting transfers between devices  46.1 us (44%)
  Pallas kernels  38.7 us (37%)
  matrix products  9.2 us (9%)
  other arithmetic  4.46 us (4%)
  local copies, waits for them, and re-layouts  3.98 us (4%)
  waiting for transfers between devices  1.48 us (1%)
    ppermute x12, starting transfers between devices, ahead(): lax.ppermute(x, axis, [(i, i + k) for i in range(lax.axis_size(axis) - k)])  28.8 us
    pallas_call x4, Pallas kernels, attend(): pl.pallas_call(functools.partial(codes_kernel, lay, factor), out_shape=ou...  22 us
    ppermute x22, starting transfers between devices, swap(): lax.ppermute(x, axis, [(i, i ^ k) for i in range(lax.axis_size(axis))])  17.2 us
    pallas_call x1, Pallas kernels, window(): pl.pallas_call(functools.partial(window_kernel, factor), out_shape=[jax.S...  12.3 us
    dot_general x8, matrix products, dot(): lax.dot_general(a, b, (contract, ((), ())), preferred_element_type=F32)  9.2 us
    pallas_call x1, Pallas kernels, block_sums(): pl.pallas_call(functools.partial(sums_kernel, lay), out_shape=[piece] * (...  4.42 us
    select_n x4, other arithmetic, prefix(): got = swap(jnp.where(core == 1, before, with_low), 'ctx', 1)  2.97 us
    unnamed x24, local copies, waits for them, and re-layouts  2.69 us
  transfers between devices with their start and end apart: 34, of which 3 were waited for; matrix products, arithmetic and copies ran while one was open for 11% of the time, Pallas kernels for 37%

profile of v1, /device:TPU:0, one launch (start us, length us, event | category | flops | bytes accessed | tf_op | source)
XLA Modules:
  0.0 104.3 jit_solution(4731154345063158654)
XLA Ops:
  0.0 1.3 %dynamic_slice.7 = bf16[512,1024]{1,0:T(8,128)(2,1)S(1)} dynamic-slice(bf16[1024,2048]{1,0:T(8,128)(2,1)} %param.9, s32[]{:T(128)S(6)} %select_n.135, s32[]{:T(128)S(6)} %select_n.136), dynamic_slice_sizes={512,1024} | dynamic-slice | bytes 2097156 | tf_op jit(solution)/shard_map/dynamic_slice | solution.py:254
  1.3 3.0 %collective-permute-start.8 = (bf16[512,1024]{1,0:T(8,128)(2,1)S(1)}, bf16[512,1024]{1,0:T(8,128)(2,1)S(1)}, u32[]{:S(2)}, u32[]{:S(2)}) collective-permute-start(bf16[512,1024]{1,0:T(8,128)(2,1)S(1)} %dynamic_slice.7), channel_id=1, source_target_pairs={{0,1},{1,0},{2,3},{3,2},{4,5},{5,4},{6,7},{7,6},{8,9},{9,8},{10,11... | collective-permute-start | bytes 3145736 | tf_op jit(solution)/shard_map/ppermute | solution.py:199
  5.0 4.4 %block_sums.1 = (bf16[2,272,128]{2,1,0:T(8,128)(2,1)}, bf16[2,272,128]{2,1,0:T(8,128)(2,1)}, bf16[2,272,128]{2,1,0:T(8,128)(2,1)}, bf16[2,272,128]{2,1,0:T(8,128...) custom-call(s32[2]{0:T(128)} %pad_add_fusion.pos_ref, ...), custom_call_target="tpu_custom_call" | custom-call | flops 1073741824 | bytes 2097152 | tf_op jit(solution)/shard_map/block_sums/pallas_call | solution.py:75
  10.5 12.3 %window.1 = (bf16[8,512,128]{2,1,0:T(8,128)(2,1)}, f32[8,512,128]{2,1,0:T(8,128)}, f32[8,512,128]{2,1,0:T(8,128)}) custom-call(s32[8,512]{1,0:T(8,128)} %bitcast.77, bf16[512,8,128]{2,1,0:T(8,128)(2,1)} %queries_ref.1, bf16[512,8,128]{2,1,0:T(8,128)(2,1)} %values_ref.3, bf16[8,512,128]{2,1,0:T(8,128)(2,1)} %book_ref.9), custom_call_target="tpu_custom_call" | custom-call | flops 6442450944 | bytes 4718592 | tf_op jit(solution)/shard_map/window/pallas_call | solution.py:130
  22.8 1.6 %collective-permute-start.1 = (bf16[272,128]{1,0:T(8,128)(2,1)S(1)}, bf16[272,128]{1,0:T(8,128)(2,1)S(1)}, u32[]{:S(2)}, u32[]{:S(2)}) collective-permute-start(bf16[272,128]{1,0:T(8,128)(2,1)S(1)} %fusion.39), channel_id=1, source_target_pairs={{0,4},{2,6},{4,0},{6,2},{8,12},{10,14},{12,8},{14,10},{16,20},{18,... | collective-permute-start | bytes 208904 | tf_op jit(solution)/shard_map/ppermute | solution.py:199
  25.0 1.6 %collective-permute-start.19 = (bf16[272,128]{1,0:T(8,128)(2,1)S(1)}, bf16[272,128]{1,0:T(8,128)(2,1)S(1)}, u32[]{:S(2)}, u32[]{:S(2)}) collective-permute-start(bf16[272,128]{1,0:T(8,128)(2,1)S(1)} %fusion.43), channel_id=1, source_target_pairs={{0,4},{2,6},{4,0},{6,2},{8,12},{10,14},{12,8},{14,10},{16,20},{18,... | collective-permute-start | bytes 208904 | tf_op jit(solution)/shard_map/ppermute | solution.py:199
  27.4 5.5 %collective-permute-start.4 = (bf16[272,128]{1,0:T(8,128)(2,1)S(1)}, bf16[272,128]{1,0:T(8,128)(2,1)S(1)}, u32[]{:S(2)}, u32[]{:S(2)}) collective-permute-start(bf16[272,128]{1,0:T(8,128)(2,1)S(1)} %add_convert_fusion.22), channel_id=1, source_target_pairs={{0,24},{2,26},{4,28},{6,30},{1,25},{3,27},{5,29},{7,31}} | collective-permute-start | bytes 208904 | tf_op jit(solution)/shard_map/ppermute | solution.py:203
  32.9 1.3 %collective-permute-start.3 = (bf16[272,128]{1,0:T(8,128)(2,1)S(1)}, bf16[272,128]{1,0:T(8,128)(2,1)S(1)}, u32[]{:S(2)}, u32[]{:S(2)}) collective-permute-start(bf16[272,128]{1,0:T(8,128)(2,1)S(1)} %add_convert_fusion.22), channel_id=1, source_target_pairs={{0,16},{2,18},{4,20},{6,22},{8,24},{10,26},{12,28},{14,30},{1,17},... | collective-permute-start | bytes 208904 | tf_op jit(solution)/shard_map/ppermute | solution.py:203
  34.3 3.3 %collective-permute-start.2 = (bf16[272,128]{1,0:T(8,128)(2,1)S(1)}, bf16[272,128]{1,0:T(8,128)(2,1)S(1)}, u32[]{:S(2)}, u32[]{:S(2)}) collective-permute-start(bf16[272,128]{1,0:T(8,128)(2,1)S(1)} %add_convert_fusion.22), channel_id=1, source_target_pairs={{0,8},{2,10},{4,12},{6,14},{8,16},{10,18},{12,20},{14,22},{16,24},... | collective-permute-start | bytes 208904 | tf_op jit(solution)/shard_map/ppermute | solution.py:203
  37.6 1.3 %collective-permute-start.14 = (bf16[272,128]{1,0:T(8,128)(2,1)S(1)}, bf16[272,128]{1,0:T(8,128)(2,1)S(1)}, u32[]{:S(2)}, u32[]{:S(2)}) collective-permute-start(bf16[272,128]{1,0:T(8,128)(2,1)S(1)} %add_convert_fusion.17), channel_id=1, source_target_pairs={{0,24},{2,26},{4,28},{6,30},{1,25},{3,27},{5,29},{7,31}} | collective-permute-start | bytes 208904 | tf_op jit(solution)/shard_map/ppermute | solution.py:203
  39.0 1.3 %collective-permute-start.13 = (bf16[272,128]{1,0:T(8,128)(2,1)S(1)}, bf16[272,128]{1,0:T(8,128)(2,1)S(1)}, u32[]{:S(2)}, u32[]{:S(2)}) collective-permute-start(bf16[272,128]{1,0:T(8,128)(2,1)S(1)} %add_convert_fusion.17), channel_id=1, source_target_pairs={{0,16},{2,18},{4,20},{6,22},{8,24},{10,26},{12,28},{14,30},{1,17},... | collective-permute-start | bytes 208904 | tf_op jit(solution)/shard_map/ppermute | solution.py:203
  40.3 3.4 %collective-permute-start.12 = (bf16[272,128]{1,0:T(8,128)(2,1)S(1)}, bf16[272,128]{1,0:T(8,128)(2,1)S(1)}, u32[]{:S(2)}, u32[]{:S(2)}) collective-permute-start(bf16[272,128]{1,0:T(8,128)(2,1)S(1)} %add_convert_fusion.17), channel_id=1, source_target_pairs={{0,8},{2,10},{4,12},{6,14},{8,16},{10,18},{12,20},{14,22},{16,24},... | collective-permute-start | bytes 208904 | tf_op jit(solution)/shard_map/ppermute | solution.py:203
  43.7 1.9 %collective-permute-start.22 = (bf16[272,128]{1,0:T(8,128)(2,1)S(1)}, bf16[272,128]{1,0:T(8,128)(2,1)S(1)}, u32[]{:S(2)}, u32[]{:S(2)}) collective-permute-start(bf16[272,128]{1,0:T(8,128)(2,1)S(1)} %add_convert_fusion.12), channel_id=1, source_target_pairs={{0,24},{2,26},{4,28},{6,30},{1,25},{3,27},{5,29},{7,31}} | collective-permute-start | bytes 208904 | tf_op jit(solution)/shard_map/ppermute | solution.py:203
  45.7 1.8 %collective-permute-start.21 = (bf16[272,128]{1,0:T(8,128)(2,1)S(1)}, bf16[272,128]{1,0:T(8,128)(2,1)S(1)}, u32[]{:S(2)}, u32[]{:S(2)}) collective-permute-start(bf16[272,128]{1,0:T(8,128)(2,1)S(1)} %add_convert_fusion.12), channel_id=1, source_target_pairs={{0,16},{2,18},{4,20},{6,22},{8,24},{10,26},{12,28},{14,30},{1,17},... | collective-permute-start | bytes 208904 | tf_op jit(solution)/shard_map/ppermute | solution.py:203
  47.6 1.9 %collective-permute-start.20 = (bf16[272,128]{1,0:T(8,128)(2,1)S(1)}, bf16[272,128]{1,0:T(8,128)(2,1)S(1)}, u32[]{:S(2)}, u32[]{:S(2)}) collective-permute-start(bf16[272,128]{1,0:T(8,128)(2,1)S(1)} %add_convert_fusion.12), channel_id=1, source_target_pairs={{0,8},{2,10},{4,12},{6,14},{8,16},{10,18},{12,20},{14,22},{16,24},... | collective-permute-start | bytes 208904 | tf_op jit(solution)/shard_map/ppermute | solution.py:203
  49.5 2.3 %collective-permute-start.30 = (bf16[272,128]{1,0:T(8,128)(2,1)S(1)}, bf16[272,128]{1,0:T(8,128)(2,1)S(1)}, u32[]{:S(2)}, u32[]{:S(2)}) collective-permute-start(bf16[272,128]{1,0:T(8,128)(2,1)S(1)} %add_convert_fusion.7), channel_id=1, source_target_pairs={{0,24},{2,26},{4,28},{6,30},{1,25},{3,27},{5,29},{7,31}} | collective-permute-start | bytes 208904 | tf_op jit(solution)/shard_map/ppermute | solution.py:203
  51.9 1.8 %collective-permute-start.29 = (bf16[272,128]{1,0:T(8,128)(2,1)S(1)}, bf16[272,128]{1,0:T(8,128)(2,1)S(1)}, u32[]{:S(2)}, u32[]{:S(2)}) collective-permute-start(bf16[272,128]{1,0:T(8,128)(2,1)S(1)} %add_convert_fusion.7), channel_id=1, source_target_pairs={{0,16},{2,18},{4,20},{6,22},{8,24},{10,26},{12,28},{14,30},{1,17},... | collective-permute-start | bytes 208904 | tf_op jit(solution)/shard_map/ppermute | solution.py:203
  53.8 2.9 %collective-permute-start.28 = (bf16[272,128]{1,0:T(8,128)(2,1)S(1)}, bf16[272,128]{1,0:T(8,128)(2,1)S(1)}, u32[]{:S(2)}, u32[]{:S(2)}) collective-permute-start(bf16[272,128]{1,0:T(8,128)(2,1)S(1)} %add_convert_fusion.7), channel_id=1, source_target_pairs={{0,8},{2,10},{4,12},{6,14},{8,16},{10,18},{12,20},{14,22},{16,24},... | collective-permute-start | bytes 208904 | tf_op jit(solution)/shard_map/ppermute | solution.py:203
  56.8 1.7 %collective-permute-start.5 = (bf16[272,128]{1,0:T(8,128)(2,1)S(1)}, bf16[272,128]{1,0:T(8,128)(2,1)S(1)}, u32[]{:S(2)}, u32[]{:S(2)}) collective-permute-start(bf16[272,128]{1,0:T(8,128)(2,1)S(1)} %get-tuple-element.30), channel_id=1, source_target_pairs={{0,4},{2,6},{4,0},{6,2},{8,12},{10,14},{12,8},{14,10},{16,20},{18,... | collective-permute-start | bytes 208904 | tf_op jit(solution)/shard_map/ppermute | solution.py:199
  59.0 1.6 %collective-permute-start.23 = (bf16[272,128]{1,0:T(8,128)(2,1)S(1)}, bf16[272,128]{1,0:T(8,128)(2,1)S(1)}, u32[]{:S(2)}, u32[]{:S(2)}) collective-permute-start(bf16[272,128]{1,0:T(8,128)(2,1)S(1)} %get-tuple-element.34), channel_id=1, source_target_pairs={{0,4},{2,6},{4,0},{6,2},{8,12},{10,14},{12,8},{14,10},{16,20},{18,... | collective-permute-start | bytes 208904 | tf_op jit(solution)/shard_map/ppermute | solution.py:199
  61.9 1.0 collective-permute-done.15
  66.5 5.5 %attend.4 = bf16[512,256]{1,0:T(8,128)(2,1)} custom-call(s32[2]{0:T(128)} %pad_add_fusion.pos_ref, bf16[8,512,128]{2,1,0:T(8,128)(2,1)} %get-tuple-element.16.qt_ref, bf16[8,512,128]{2,1,0:T(8,128)(2,1)} %book_ref.9, f32[8,512,128]{2,1,0:T(8,128)} %get-tuple-element.17.num_ref, f32[8,512,128]{2,1,0:T(8,128)} %get-tuple-element.18.ml_ref, ...), custom_call_target="tpu_custom_call" | custom-call | flops 1073741824 | bytes 1835008 | tf_op jit(solution)/shard_map/attend/pallas_call | solution.py:185
  73.2 5.5 %attend.5 = bf16[512,256]{1,0:T(8,128)(2,1)} custom-call(s32[2]{0:T(128)} %pad_add_fusion.pos_ref, bf16[8,512,128]{2,1,0:T(8,128)(2,1)} %get-tuple-element.16.qt_ref, bf16[8,512,128]{2,1,0:T(8,128)(2,1)} %book_ref.9, f32[8,512,128]{2,1,0:T(8,128)} %get-tuple-element.17.num_ref, f32[8,512,128]{2,1,0:T(8,128)} %get-tuple-element.18.ml_ref, ...), custom_call_target="tpu_custom_call" | custom-call | flops 1073741824 | bytes 1835008 | tf_op jit(solution)/shard_map/attend/pallas_call | solution.py:185
  78.7 1.5 %collective-permute-start.17 = (bf16[512,256]{1,0:T(8,128)(2,1)}, bf16[512,256]{1,0:T(8,128)(2,1)S(1)}, u32[]{:S(2)}, u32[]{:S(2)}) collective-permute-start(bf16[512,256]{1,0:T(8,128)(2,1)} %attend.5), channel_id=1, source_target_pairs={{0,1},{1,0},{2,3},{3,2},{4,5},{5,4},{6,7},{7,6},{8,9},{9,8},{10,11... | collective-permute-start | bytes 786440 | tf_op jit(solution)/shard_map/ppermute | solution.py:199
  80.9 5.5 %attend.6 = bf16[512,256]{1,0:T(8,128)(2,1)} custom-call(s32[2]{0:T(128)} %pad_add_fusion.pos_ref, bf16[8,512,128]{2,1,0:T(8,128)(2,1)} %get-tuple-element.16.qt_ref, bf16[8,512,128]{2,1,0:T(8,128)(2,1)} %book_ref.9, f32[8,512,128]{2,1,0:T(8,128)} %get-tuple-element.17.num_ref, f32[8,512,128]{2,1,0:T(8,128)} %get-tuple-element.18.ml_ref, ...), custom_call_target="tpu_custom_call" | custom-call | flops 1073741824 | bytes 1835008 | tf_op jit(solution)/shard_map/attend/pallas_call | solution.py:185
  87.6 5.5 %attend.7 = bf16[512,256]{1,0:T(8,128)(2,1)} custom-call(s32[2]{0:T(128)} %pad_add_fusion.pos_ref, bf16[8,512,128]{2,1,0:T(8,128)(2,1)} %get-tuple-element.16.qt_ref, bf16[8,512,128]{2,1,0:T(8,128)(2,1)} %book_ref.9, f32[8,512,128]{2,1,0:T(8,128)} %get-tuple-element.17.num_ref, f32[8,512,128]{2,1,0:T(8,128)} %get-tuple-element.18.ml_ref, ...), custom_call_target="tpu_custom_call" | custom-call | flops 1073741824 | bytes 1835008 | tf_op jit(solution)/shard_map/attend/pallas_call | solution.py:185
  93.1 1.5 %collective-permute-start.33 = (bf16[512,256]{1,0:T(8,128)(2,1)}, bf16[512,256]{1,0:T(8,128)(2,1)S(1)}, u32[]{:S(2)}, u32[]{:S(2)}) collective-permute-start(bf16[512,256]{1,0:T(8,128)(2,1)} %attend.7), channel_id=1, source_target_pairs={{0,1},{1,0},{2,3},{3,2},{4,5},{5,4},{6,7},{7,6},{8,9},{9,8},{10,11... | collective-permute-start | bytes 786440 | tf_op jit(solution)/shard_map/ppermute | solution.py:199
  94.6 1.5 %fusion.16 = f32[512,1024]{1,0:T(8,128)S(1)} fusion(bf16[512,256]{1,0:T(8,128)(2,1)S(1)} %copy-done, bf16[1024,2048]{1,0:T(8,128)(2,1)} %param.9, s32[]{:T(128)S(6)} %select_n.133), kind=kOutput, calls=%fused_computation.18 | convolution fusion | flops 268435456 | bytes 2883588 | tf_op jit(solution)/shard_map/dot_general | solution.py:20
  96.1 1.5 %fusion.12 = f32[512,1024]{1,0:T(8,128)S(1)} fusion(bf16[512,256]{1,0:T(8,128)(2,1)S(1)} %copy-done.1, bf16[1024,2048]{1,0:T(8,128)(2,1)} %param.9, s32[]{:T(128)S(6)} %add.161, s32[]{:T(128)S(6)} %select_n.133), kind=kOutput, calls=%fused_computation.14 | convolution fusion | flops 268435456 | bytes 2883592 | tf_op jit(solution)/shard_map/dot_general | solution.py:20
  97.7 1.5 %fusion.8 = f32[512,1024]{1,0:T(8,128)S(1)} fusion(bf16[512,256]{1,0:T(8,128)(2,1)S(1)} %copy-done.3, bf16[1024,2048]{1,0:T(8,128)(2,1)} %param.9, s32[]{:T(128)S(6)} %add.162, s32[]{:T(128)S(6)} %select_n.133), kind=kOutput, calls=%fused_computation.10 | convolution fusion | flops 268435456 | bytes 2883592 | tf_op jit(solution)/shard_map/dot_general | solution.py:20
  99.2 1.5 %fusion.4 = f32[512,1024]{1,0:T(8,128)S(1)} fusion(bf16[512,256]{1,0:T(8,128)(2,1)S(1)} %copy-done.2, bf16[1024,2048]{1,0:T(8,128)(2,1)} %param.9, s32[]{:T(128)S(6)} %add.163, s32[]{:T(128)S(6)} %select_n.133), kind=kOutput, calls=%fused_computation.6 | convolution fusion | flops 268435456 | bytes 2883592 | tf_op jit(solution)/shard_map/dot_general | solution.py:20
  102.5 1.9 %add_convert_fusion = bf16[512,1024]{1,0:T(8,128)(2,1)} fusion(f32[512,1024]{1,0:T(8,128)S(1)} %fusion.4, f32[512,1024]{1,0:T(8,128)S(1)} %fusion.6, f32[512,1024]{1,0:T(8,128)S(1)} %fusion.8, f32[512,1024]{1,0:T(8,128)S(1)} %fusion.10, f32[512,1024]{1,0:T(8,128)S(1)} %fusion.12, f32[512,1024]{1,0:T(8,128)S(1)} %fusion.16, f32[512,1024]{1,0:T(8,128)S(1)} %fusion.14, ...), kind=kOutput, calls=%fused_computation.1 | convolution fusion | flops 272629760 | bytes 16515072 | tf_op jit(solution)/shard_map/dot_general | solution.py:20
  (94 shorter events, 13.6 us)
Async XLA Ops:
  1.3 93.3 %collective-permute-start.8 = (bf16[512,1024]{1,0:T(8,128)(2,1)S(1)}, bf16[512,1024]{1,0:T(8,128)(2,1)S(1)}, u32[]{:S(2)}, u32[]{:S(2)}) collective-permute-start(bf16[512,1024]{1,0:T(8,128)(2,1)S(1)} %dynamic_slice.7), channel_id=1, source_target_pairs={{0,1},{1,0},{2,3},{3,2},{4,5},{5,4},{6,7},{7,6},{8,9},{9,8},{10,11... | collective-permute-start | bytes 3145736 | tf_op jit(solution)/shard_map/ppermute | solution.py:199
  9.4 13.4 %collective-permute-start = (bf16[2,272,128]{2,1,0:T(8,128)(2,1)}, bf16[2,272,128]{2,1,0:T(8,128)(2,1)S(1)}, u32[]{:S(2)}, u32[]{:S(2)}) collective-permute-start(bf16[2,272,128]{2,1,0:T(8,128)(2,1)} %get-tuple-element.20), channel_id=1, source_target_pairs={{0,2},{2,0},{4,6},{6,4},{8,10},{10,8},{12,14},{14,12},{16,18},{18,... | collective-permute-start | bytes 417800 | tf_op jit(solution)/shard_map/ppermute | solution.py:199
  9.4 15.0 %collective-permute-start.10 = (bf16[2,272,128]{2,1,0:T(8,128)(2,1)}, bf16[2,272,128]{2,1,0:T(8,128)(2,1)S(1)}, u32[]{:S(2)}, u32[]{:S(2)}) collective-permute-start(bf16[2,272,128]{2,1,0:T(8,128)(2,1)} %get-tuple-element.22), channel_id=1, source_target_pairs={{0,2},{2,0},{4,6},{6,4},{8,10},{10,8},{12,14},{14,12},{16,18},{18,... | collective-permute-start | bytes 417800 | tf_op jit(solution)/shard_map/ppermute | solution.py:199
  9.9 15.1 %collective-permute-start.18 = (bf16[2,272,128]{2,1,0:T(8,128)(2,1)}, bf16[2,272,128]{2,1,0:T(8,128)(2,1)S(1)}, u32[]{:S(2)}, u32[]{:S(2)}) collective-permute-start(bf16[2,272,128]{2,1,0:T(8,128)(2,1)} %get-tuple-element.24), channel_id=1, source_target_pairs={{0,2},{2,0},{4,6},{6,4},{8,10},{10,8},{12,14},{14,12},{16,18},{18,... | collective-permute-start | bytes 417800 | tf_op jit(solution)/shard_map/ppermute | solution.py:199
  10.0 16.7 %collective-permute-start.26 = (bf16[2,272,128]{2,1,0:T(8,128)(2,1)}, bf16[2,272,128]{2,1,0:T(8,128)(2,1)S(1)}, u32[]{:S(2)}, u32[]{:S(2)}) collective-permute-start(bf16[2,272,128]{2,1,0:T(8,128)(2,1)} %get-tuple-element.26), channel_id=1, source_target_pairs={{0,2},{2,0},{4,6},{6,4},{8,10},{10,8},{12,14},{14,12},{16,18},{18,... | collective-permute-start | bytes 417800 | tf_op jit(solution)/shard_map/ppermute | solution.py:199
  22.8 4.6 %collective-permute-start.1 = (bf16[272,128]{1,0:T(8,128)(2,1)S(1)}, bf16[272,128]{1,0:T(8,128)(2,1)S(1)}, u32[]{:S(2)}, u32[]{:S(2)}) collective-permute-start(bf16[272,128]{1,0:T(8,128)(2,1)S(1)} %fusion.39), channel_id=1, source_target_pairs={{0,4},{2,6},{4,0},{6,2},{8,12},{10,14},{12,8},{14,10},{16,20},{18,... | collective-permute-start | bytes 208904 | tf_op jit(solution)/shard_map/ppermute | solution.py:199
  24.4 8.5 %collective-permute-start.11 = (bf16[272,128]{1,0:T(8,128)(2,1)S(1)}, bf16[272,128]{1,0:T(8,128)(2,1)S(1)}, u32[]{:S(2)}, u32[]{:S(2)}) collective-permute-start(bf16[272,128]{1,0:T(8,128)(2,1)S(1)} %fusion.41), channel_id=1, source_target_pairs={{0,4},{2,6},{4,0},{6,2},{8,12},{10,14},{12,8},{14,10},{16,20},{18,... | collective-permute-start | bytes 208904 | tf_op jit(solution)/shard_map/ppermute | solution.py:199
  25.0 9.3 %collective-permute-start.19 = (bf16[272,128]{1,0:T(8,128)(2,1)S(1)}, bf16[272,128]{1,0:T(8,128)(2,1)S(1)}, u32[]{:S(2)}, u32[]{:S(2)}) collective-permute-start(bf16[272,128]{1,0:T(8,128)(2,1)S(1)} %fusion.43), channel_id=1, source_target_pairs={{0,4},{2,6},{4,0},{6,2},{8,12},{10,14},{12,8},{14,10},{16,20},{18,... | collective-permute-start | bytes 208904 | tf_op jit(solution)/shard_map/ppermute | solution.py:199
  26.6 11.0 %collective-permute-start.27 = (bf16[272,128]{1,0:T(8,128)(2,1)S(1)}, bf16[272,128]{1,0:T(8,128)(2,1)S(1)}, u32[]{:S(2)}, u32[]{:S(2)}) collective-permute-start(bf16[272,128]{1,0:T(8,128)(2,1)S(1)} %fusion.45), channel_id=1, source_target_pairs={{0,4},{2,6},{4,0},{6,2},{8,12},{10,14},{12,8},{14,10},{16,20},{18,... | collective-permute-start | bytes 208904 | tf_op jit(solution)/shard_map/ppermute | solution.py:199
  27.4 11.6 %collective-permute-start.4 = (bf16[272,128]{1,0:T(8,128)(2,1)S(1)}, bf16[272,128]{1,0:T(8,128)(2,1)S(1)}, u32[]{:S(2)}, u32[]{:S(2)}) collective-permute-start(bf16[272,128]{1,0:T(8,128)(2,1)S(1)} %add_convert_fusion.22), channel_id=1, source_target_pairs={{0,24},{2,26},{4,28},{6,30},{1,25},{3,27},{5,29},{7,31}} | collective-permute-start | bytes 208904 | tf_op jit(solution)/shard_map/ppermute | solution.py:203
  32.9 7.3 %collective-permute-start.3 = (bf16[272,128]{1,0:T(8,128)(2,1)S(1)}, bf16[272,128]{1,0:T(8,128)(2,1)S(1)}, u32[]{:S(2)}, u32[]{:S(2)}) collective-permute-start(bf16[272,128]{1,0:T(8,128)(2,1)S(1)} %add_convert_fusion.22), channel_id=1, source_target_pairs={{0,16},{2,18},{4,20},{6,22},{8,24},{10,26},{12,28},{14,30},{1,17},... | collective-permute-start | bytes 208904 | tf_op jit(solution)/shard_map/ppermute | solution.py:203
  34.3 9.4 %collective-permute-start.2 = (bf16[272,128]{1,0:T(8,128)(2,1)S(1)}, bf16[272,128]{1,0:T(8,128)(2,1)S(1)}, u32[]{:S(2)}, u32[]{:S(2)}) collective-permute-start(bf16[272,128]{1,0:T(8,128)(2,1)S(1)} %add_convert_fusion.22), channel_id=1, source_target_pairs={{0,8},{2,10},{4,12},{6,14},{8,16},{10,18},{12,20},{14,22},{16,24},... | collective-permute-start | bytes 208904 | tf_op jit(solution)/shard_map/ppermute | solution.py:203
  37.6 8.1 %collective-permute-start.14 = (bf16[272,128]{1,0:T(8,128)(2,1)S(1)}, bf16[272,128]{1,0:T(8,128)(2,1)S(1)}, u32[]{:S(2)}, u32[]{:S(2)}) collective-permute-start(bf16[272,128]{1,0:T(8,128)(2,1)S(1)} %add_convert_fusion.17), channel_id=1, source_target_pairs={{0,24},{2,26},{4,28},{6,30},{1,25},{3,27},{5,29},{7,31}} | collective-permute-start | bytes 208904 | tf_op jit(solution)/shard_map/ppermute | solution.py:203
  39.0 8.6 %collective-permute-start.13 = (bf16[272,128]{1,0:T(8,128)(2,1)S(1)}, bf16[272,128]{1,0:T(8,128)(2,1)S(1)}, u32[]{:S(2)}, u32[]{:S(2)}) collective-permute-start(bf16[272,128]{1,0:T(8,128)(2,1)S(1)} %add_convert_fusion.17), channel_id=1, source_target_pairs={{0,16},{2,18},{4,20},{6,22},{8,24},{10,26},{12,28},{14,30},{1,17},... | collective-permute-start | bytes 208904 | tf_op jit(solution)/shard_map/ppermute | solution.py:203
  40.3 9.2 %collective-permute-start.12 = (bf16[272,128]{1,0:T(8,128)(2,1)S(1)}, bf16[272,128]{1,0:T(8,128)(2,1)S(1)}, u32[]{:S(2)}, u32[]{:S(2)}) collective-permute-start(bf16[272,128]{1,0:T(8,128)(2,1)S(1)} %add_convert_fusion.17), channel_id=1, source_target_pairs={{0,8},{2,10},{4,12},{6,14},{8,16},{10,18},{12,20},{14,22},{16,24},... | collective-permute-start | bytes 208904 | tf_op jit(solution)/shard_map/ppermute | solution.py:203
  43.7 8.2 %collective-permute-start.22 = (bf16[272,128]{1,0:T(8,128)(2,1)S(1)}, bf16[272,128]{1,0:T(8,128)(2,1)S(1)}, u32[]{:S(2)}, u32[]{:S(2)}) collective-permute-start(bf16[272,128]{1,0:T(8,128)(2,1)S(1)} %add_convert_fusion.12), channel_id=1, source_target_pairs={{0,24},{2,26},{4,28},{6,30},{1,25},{3,27},{5,29},{7,31}} | collective-permute-start | bytes 208904 | tf_op jit(solution)/shard_map/ppermute | solution.py:203
  45.7 8.1 %collective-permute-start.21 = (bf16[272,128]{1,0:T(8,128)(2,1)S(1)}, bf16[272,128]{1,0:T(8,128)(2,1)S(1)}, u32[]{:S(2)}, u32[]{:S(2)}) collective-permute-start(bf16[272,128]{1,0:T(8,128)(2,1)S(1)} %add_convert_fusion.12), channel_id=1, source_target_pairs={{0,16},{2,18},{4,20},{6,22},{8,24},{10,26},{12,28},{14,30},{1,17},... | collective-permute-start | bytes 208904 | tf_op jit(solution)/shard_map/ppermute | solution.py:203
  47.6 9.2 %collective-permute-start.20 = (bf16[272,128]{1,0:T(8,128)(2,1)S(1)}, bf16[272,128]{1,0:T(8,128)(2,1)S(1)}, u32[]{:S(2)}, u32[]{:S(2)}) collective-permute-start(bf16[272,128]{1,0:T(8,128)(2,1)S(1)} %add_convert_fusion.12), channel_id=1, source_target_pairs={{0,8},{2,10},{4,12},{6,14},{8,16},{10,18},{12,20},{14,22},{16,24},... | collective-permute-start | bytes 208904 | tf_op jit(solution)/shard_map/ppermute | solution.py:203
  49.5 9.0 %collective-permute-start.30 = (bf16[272,128]{1,0:T(8,128)(2,1)S(1)}, bf16[272,128]{1,0:T(8,128)(2,1)S(1)}, u32[]{:S(2)}, u32[]{:S(2)}) collective-permute-start(bf16[272,128]{1,0:T(8,128)(2,1)S(1)} %add_convert_fusion.7), channel_id=1, source_target_pairs={{0,24},{2,26},{4,28},{6,30},{1,25},{3,27},{5,29},{7,31}} | collective-permute-start | bytes 208904 | tf_op jit(solution)/shard_map/ppermute | solution.py:203
  51.9 7.1 %collective-permute-start.29 = (bf16[272,128]{1,0:T(8,128)(2,1)S(1)}, bf16[272,128]{1,0:T(8,128)(2,1)S(1)}, u32[]{:S(2)}, u32[]{:S(2)}) collective-permute-start(bf16[272,128]{1,0:T(8,128)(2,1)S(1)} %add_convert_fusion.7), channel_id=1, source_target_pairs={{0,16},{2,18},{4,20},{6,22},{8,24},{10,26},{12,28},{14,30},{1,17},... | collective-permute-start | bytes 208904 | tf_op jit(solution)/shard_map/ppermute | solution.py:203
  53.8 6.9 %collective-permute-start.28 = (bf16[272,128]{1,0:T(8,128)(2,1)S(1)}, bf16[272,128]{1,0:T(8,128)(2,1)S(1)}, u32[]{:S(2)}, u32[]{:S(2)}) collective-permute-start(bf16[272,128]{1,0:T(8,128)(2,1)S(1)} %add_convert_fusion.7), channel_id=1, source_target_pairs={{0,8},{2,10},{4,12},{6,14},{8,16},{10,18},{12,20},{14,22},{16,24},... | collective-permute-start | bytes 208904 | tf_op jit(solution)/shard_map/ppermute | solution.py:203
  56.8 4.4 %collective-permute-start.5 = (bf16[272,128]{1,0:T(8,128)(2,1)S(1)}, bf16[272,128]{1,0:T(8,128)(2,1)S(1)}, u32[]{:S(2)}, u32[]{:S(2)}) collective-permute-start(bf16[272,128]{1,0:T(8,128)(2,1)S(1)} %get-tuple-element.30), channel_id=1, source_target_pairs={{0,4},{2,6},{4,0},{6,2},{8,12},{10,14},{12,8},{14,10},{16,20},{18,... | collective-permute-start | bytes 208904 | tf_op jit(solution)/shard_map/ppermute | solution.py:199
  58.6 4.4 %collective-permute-start.15 = (bf16[272,128]{1,0:T(8,128)(2,1)S(1)}, bf16[272,128]{1,0:T(8,128)(2,1)S(1)}, u32[]{:S(2)}, u32[]{:S(2)}) collective-permute-start(bf16[272,128]{1,0:T(8,128)(2,1)S(1)} %get-tuple-element.32), channel_id=1, source_target_pairs={{0,4},{2,6},{4,0},{6,2},{8,12},{10,14},{12,8},{14,10},{16,20},{18,... | collective-permute-start | bytes 208904 | tf_op jit(solution)/shard_map/ppermute | solution.py:199
  59.0 4.7 %collective-permute-start.23 = (bf16[272,128]{1,0:T(8,128)(2,1)S(1)}, bf16[272,128]{1,0:T(8,128)(2,1)S(1)}, u32[]{:S(2)}, u32[]{:S(2)}) collective-permute-start(bf16[272,128]{1,0:T(8,128)(2,1)S(1)} %get-tuple-element.34), channel_id=1, source_target_pairs={{0,4},{2,6},{4,0},{6,2},{8,12},{10,14},{12,8},{14,10},{16,20},{18,... | collective-permute-start | bytes 208904 | tf_op jit(solution)/shard_map/ppermute | solution.py:199
  63.6 8.9 %collective-permute-start.16 = (bf16[2,272,128]{2,1,0:T(8,128)(2,1)S(1)}, bf16[2,272,128]{2,1,0:T(8,128)(2,1)S(1)}, u32[]{:S(2)}, u32[]{:S(2)}) collective-permute-start(bf16[2,272,128]{2,1,0:T(8,128)(2,1)S(1)} %get-tuple-element.39), channel_id=1, source_target_pairs={{0,2},{2,0},{4,6},{6,4},{8,10},{10,8},{12,14},{14,12},{16,18},{18,... | collective-permute-start | bytes 417800 | tf_op jit(solution)/shard_map/ppermute | solution.py:199
  64.5 15.8 %collective-permute-start.24 = (bf16[2,272,128]{2,1,0:T(8,128)(2,1)}, bf16[2,272,128]{2,1,0:T(8,128)(2,1)S(1)}, u32[]{:S(2)}, u32[]{:S(2)}) collective-permute-start(bf16[2,272,128]{2,1,0:T(8,128)(2,1)} %get-tuple-element.41), channel_id=1, source_target_pairs={{0,2},{2,0},{4,6},{6,4},{8,10},{10,8},{12,14},{14,12},{16,18},{18,... | collective-permute-start | bytes 417800 | tf_op jit(solution)/shard_map/ppermute | solution.py:199
  65.9 21.0 %collective-permute-start.32 = (bf16[2,272,128]{2,1,0:T(8,128)(2,1)}, bf16[2,272,128]{2,1,0:T(8,128)(2,1)S(1)}, u32[]{:S(2)}, u32[]{:S(2)}) collective-permute-start(bf16[2,272,128]{2,1,0:T(8,128)(2,1)} %get-tuple-element.43), channel_id=1, source_target_pairs={{0,2},{2,0},{4,6},{6,4},{8,10},{10,8},{12,14},{14,12},{16,18},{18,... | collective-permute-start | bytes 417800 | tf_op jit(solution)/shard_map/ppermute | solution.py:199
  72.0 30.0 %collective-permute-start.7 = (bf16[512,256]{1,0:T(8,128)(2,1)}, bf16[512,256]{1,0:T(8,128)(2,1)S(1)}, u32[]{:S(2)}, u32[]{:S(2)}) collective-permute-start(bf16[512,256]{1,0:T(8,128)(2,1)} %attend.4), channel_id=1, source_target_pairs={{0,1},{1,0},{2,3},{3,2},{4,5},{5,4},{6,7},{7,6},{8,9},{9,8},{10,11... | collective-permute-start | bytes 786440 | tf_op jit(solution)/shard_map/ppermute | solution.py:199
  78.7 22.8 %collective-permute-start.17 = (bf16[512,256]{1,0:T(8,128)(2,1)}, bf16[512,256]{1,0:T(8,128)(2,1)S(1)}, u32[]{:S(2)}, u32[]{:S(2)}) collective-permute-start(bf16[512,256]{1,0:T(8,128)(2,1)} %attend.5), channel_id=1, source_target_pairs={{0,1},{1,0},{2,3},{3,2},{4,5},{5,4},{6,7},{7,6},{8,9},{9,8},{10,11... | collective-permute-start | bytes 786440 | tf_op jit(solution)/shard_map/ppermute | solution.py:199
  86.4 14.7 %collective-permute-start.25 = (bf16[512,256]{1,0:T(8,128)(2,1)}, bf16[512,256]{1,0:T(8,128)(2,1)S(1)}, u32[]{:S(2)}, u32[]{:S(2)}) collective-permute-start(bf16[512,256]{1,0:T(8,128)(2,1)} %attend.6), channel_id=1, source_target_pairs={{0,1},{1,0},{2,3},{3,2},{4,5},{5,4},{6,7},{7,6},{8,9},{9,8},{10,11... | collective-permute-start | bytes 786440 | tf_op jit(solution)/shard_map/ppermute | solution.py:199
  93.1 9.3 %collective-permute-start.33 = (bf16[512,256]{1,0:T(8,128)(2,1)}, bf16[512,256]{1,0:T(8,128)(2,1)S(1)}, u32[]{:S(2)}, u32[]{:S(2)}) collective-permute-start(bf16[512,256]{1,0:T(8,128)(2,1)} %attend.7), channel_id=1, source_target_pairs={{0,1},{1,0},{2,3},{3,2},{4,5},{5,4},{6,7},{7,6},{8,9},{9,8},{10,11... | collective-permute-start | bytes 786440 | tf_op jit(solution)/shard_map/ppermute | solution.py:199
  94.6 6.1 %collective-permute-start.9 = (bf16[512,1024]{1,0:T(8,128)(2,1)S(1)}, bf16[512,1024]{1,0:T(8,128)(2,1)S(1)}, u32[]{:S(2)}, u32[]{:S(2)}) collective-permute-start(bf16[512,1024]{1,0:T(8,128)(2,1)S(1)} %collective-permute-done.8), channel_id=1, source_target_pairs={{0,2},{2,0},{4,6},{6,4},{8,10},{10,8},{12,14},{14,12},{16,18},{18,... | collective-permute-start | bytes 3145736 | tf_op jit(solution)/shard_map/ppermute | solution.py:199
  (14 other events, 83.1 us)

commit v2 on v1

v2 whole, which is shorter than its diff:
```python
import functools
import math

import jax
import jax.numpy as jnp
from jax import lax
from jax.experimental import pallas as pl
from jax.experimental.pallas import tpu as pltpu
from jax.sharding import PartitionSpec as P

BLOCK = 512
LANES = 128
GROUPS = 4
NEVER = -1e30
F32 = jnp.float32
BF16 = jnp.bfloat16
VMEM = pl.BlockSpec(memory_space=pltpu.VMEM)
SMEM = pl.BlockSpec(memory_space=pltpu.SMEM)


def dot(a, b, contract=((1,), (0,))):
    return lax.dot_general(a, b, (contract, ((), ())), preferred_element_type=F32)


def one_hot(codes, ncodes):
    table = lax.broadcasted_iota(jnp.int32, (ncodes, codes.shape[1]), 0)
    return (table == codes).astype(BF16)


class Layout:
    def __init__(self, devices, first, heads, ncodes):
        self.first, self.heads = (first, heads)
        self.each = ncodes // LANES
        self.per = heads * self.each // 4
        self.shift = int(math.log2(256 // devices + 1))
        self.digits = 1
        while (1 << (self.shift * self.digits)) <= BLOCK:
            self.digits += 1
        self.sums = self.per * LANES
        self.tail = -(-self.digits * self.per // 16) * 16
        self.rows = self.sums + self.tail
        assert ncodes % LANES == 0 and heads * self.each % 4 == 0 and devices % 4 == 0

    def place(self, head, j):
        return divmod(head * self.each + j, self.per)


def group_sums(lay, core, row, codes_ref, vt_ref, buf, keep_ref, give_ref):
    line = lax.broadcasted_iota(jnp.int32, (lay.tail, LANES), 0)
    eye = lax.broadcasted_iota(jnp.int32, (LANES, LANES), 0) == lax.broadcasted_iota(jnp.int32, (LANES, LANES), 1)
    mask = (1 << lay.shift) - 1
    tails = [jnp.zeros((lay.tail, LANES), F32) for _ in range(4)]
    tokens = codes_ref.shape[1]
    ones = jnp.ones((tokens, LANES), BF16)
    for k in range(lay.heads):
        h = lay.first + k
        onehot = one_hot(codes_ref[h : h + 1, :], lay.each * LANES)
        both = dot(onehot, jnp.concatenate([vt_ref[h], ones], axis=1))
        for j in range(lay.each):
            piece, at = lay.place(k, j)
            here = slice(j * LANES, (j + 1) * LANES)
            buf[piece // 2 ^ core, piece % 2 ^ row, at * LANES : (at + 1) * LANES, :] = both[here, :LANES].astype(BF16)
            count = jnp.sum(jnp.where(eye, both[here, LANES:], 0.0), axis=0, keepdims=True).astype(jnp.int32)
            for d in range(lay.digits):
                digit = ((count >> (lay.shift * d)) & mask).astype(F32)
                tails[piece] = jnp.where(line == d * lay.per + at, digit, tails[piece])
    for piece in range(4):
        buf[piece // 2 ^ core, piece % 2 ^ row, lay.sums :, :] = tails[piece].astype(BF16)
    keep_ref[...] = buf[0]
    give_ref[...] = buf[1]


def sums_kernel(lays, turn, pos_ref, codes_ref, values_ref, *refs):
    buf = refs[-1]
    core, row = (pos_ref[0], pos_ref[1])
    if turn:
        vt_ref = refs[0]
        vt_ref[...] = jnp.swapaxes(values_ref[...], 0, 1)
        outs = refs[1:-1]
    else:
        vt_ref = values_ref
        outs = refs[:-1]
    for g, lay in enumerate(lays):
        view = buf.at[:, :, : lay.rows, :]
        group_sums(lay, core, row, codes_ref, vt_ref, view, outs[2 * g], outs[2 * g + 1])


def block_sums(lays, turn, pos, codes, values):
    heads, tokens = codes.shape
    width = values.shape[2]
    shapes = [jax.ShapeDtypeStruct((2, lay.rows, LANES), BF16) for lay in lays for _ in range(2)]
    if turn:
        shapes = [jax.ShapeDtypeStruct((heads, tokens, width), BF16)] + shapes
    some = sum(lay.heads for lay in lays)
    outs = pl.pallas_call(
        functools.partial(sums_kernel, lays, turn),
        out_shape=shapes,
        in_specs=[SMEM, VMEM, VMEM],
        out_specs=[VMEM] * len(shapes),
        scratch_shapes=[pltpu.VMEM((2, 2, max(lay.rows for lay in lays), LANES), BF16)],
        cost_estimate=pl.CostEstimate(
            flops=8 * some * tokens * lays[0].each * LANES * width, bytes_accessed=4 * tokens * heads * width, transcendentals=0
        ),
        name="block_sums",
    )(pos, codes, values)
    vt = outs[0] if turn else values
    outs = outs[1:] if turn else outs
    return vt, [(outs[2 * g], outs[2 * g + 1]) for g in range(len(lays))]


def turn_kernel(queries_ref, book_ref, qt_ref, bt_ref):
    qt_ref[...] = jnp.swapaxes(queries_ref[...], 0, 1)
    for h in range(book_ref.shape[0]):
        bt_ref[h] = book_ref[h].T


def turn_inputs(queries, book):
    tokens, heads, width = queries.shape
    return pl.pallas_call(
        turn_kernel,
        out_shape=[
            jax.ShapeDtypeStruct((heads, tokens, width), BF16),
            jax.ShapeDtypeStruct((heads, width, book.shape[1]), BF16),
        ],
        in_specs=[VMEM] * 2,
        out_specs=[VMEM] * 2,
        cost_estimate=pl.CostEstimate(flops=4000000000, bytes_accessed=8 * tokens * heads * width, transcendentals=0),
        name="turn_inputs",
    )(queries, book)


def lane_tiles(x):
    return [x[:, j : j + LANES] for j in range(0, x.shape[1], LANES)]


def window_kernel(lay, factor, codes_ref, qt_ref, vt_ref, bt_ref, num_ref, top_ref, den_ref):
    tokens = qt_ref.shape[1]
    ncodes = bt_ref.shape[2]
    tile = tokens // 2
    causal = lax.broadcasted_iota(jnp.int32, (tile, tile), 0) >= lax.broadcasted_iota(jnp.int32, (tile, tile), 1)
    for k in range(lay.heads):
        onehot = one_hot(codes_ref[lay.first + k : lay.first + k + 1, :], ncodes)
        keys = dot(bt_ref[k], onehot).astype(BF16)
        for r in range(2):
            rows = slice(r * tile, (r + 1) * tile)
            upto = slice(0, (r + 1) * tile)
            score = dot(qt_ref[k, rows, :], keys[:, upto])
            last = jnp.where(causal, score[:, r * tile :], NEVER)
            score = jnp.concatenate([score[:, :tile], last], axis=1) if r else last
            top = jnp.max(functools.reduce(jnp.maximum, lane_tiles(score)), axis=1, keepdims=True)
            top_ref[k, rows, :] = jnp.broadcast_to(top, (tile, LANES))
            weight = jnp.exp2((score - top) * factor)
            den = jnp.sum(sum(lane_tiles(weight)), axis=1, keepdims=True)
            den_ref[k, rows, :] = jnp.broadcast_to(den, (tile, LANES))
            num_ref[k, rows, :] = dot(weight.astype(BF16), vt_ref[k, upto, :])


def part_of(lay, x):
    first, count = (lay.first, lay.heads)
    assert first % count == 0
    return pl.BlockSpec((count,) + x.shape[1:], lambda i: (first // count, 0, 0))


def whole(x):
    return pl.BlockSpec(x.shape, lambda i: (0,) * len(x.shape))


def window(lay, codes, qt, vt, bt):
    heads, tokens, width = qt.shape
    factor = width ** (-0.5) * math.log2(math.e)
    shape = jax.ShapeDtypeStruct((lay.heads, tokens, width), F32)
    return pl.pallas_call(
        functools.partial(window_kernel, lay, factor),
        out_shape=[shape] * 3,
        grid=(1,),
        in_specs=[whole(codes), part_of(lay, qt), part_of(lay, vt), part_of(lay, bt)],
        out_specs=[whole(shape)] * 3,
        cost_estimate=pl.CostEstimate(flops=2400000000, bytes_accessed=18 * tokens * lay.heads * width, transcendentals=0),
        name="window",
    )(codes, qt, vt, bt)


def codes_kernel(lay, factor, pos_ref, qt_ref, bt_ref, num_ref, top_ref, den_ref, mine_ref, theirs_ref, out_ref, buf):
    core, row = (pos_ref[0], pos_ref[1])
    tokens, width = qt_ref.shape[1:]
    tile = tokens // 2
    buf[core] = mine_ref[...]
    buf[1 - core] = theirs_ref[...]
    tails = [buf[p // 2, p % 2 ^ row, lay.sums :, :].astype(F32) for p in range(4)]
    for k in range(lay.heads):
        sums, counts = ([], [])
        for j in range(lay.each):
            p, at = lay.place(k, j)
            sums.append(buf[p // 2, p % 2 ^ row, at * LANES : (at + 1) * LANES, :])
            count = 0.0
            for d in range(lay.digits):
                line = d * lay.per + at
                count = count + tails[p][line : line + 1] * float(1 << (lay.shift * d))
            counts.append(count)
        cache = jnp.concatenate(sums, axis=0)
        for r in range(2):
            rows = slice(r * tile, (r + 1) * tile)
            scores = lane_tiles(dot(qt_ref[k, rows, :], bt_ref[k]))
            scores = [s + jnp.where(n > 0.5, 0.0, NEVER) for s, n in zip(scores, counts)]
            early = top_ref[k, rows, :]
            top = jnp.maximum(early, jnp.max(functools.reduce(jnp.maximum, scores), axis=1, keepdims=True))
            weights = [jnp.exp2((s - top) * factor) for s in scores]
            keep = jnp.exp2((early - top) * factor)
            den = jnp.sum(sum(w * n for w, n in zip(weights, counts)), axis=1, keepdims=True)
            den = keep * den_ref[k, rows, :] + den
            num = dot(jnp.concatenate([w.astype(BF16) for w in weights], axis=1), cache)
            num = keep * num_ref[k, rows, :] + num
            out_ref[rows, k * width : (k + 1) * width] = (num * (1.0 / den)).astype(BF16)


def attend(lay, pos, qt, bt, num, top, den, mine, theirs):
    heads, tokens, width = qt.shape
    factor = width ** (-0.5) * math.log2(math.e)
    out = jax.ShapeDtypeStruct((tokens, lay.heads * width), BF16)
    return pl.pallas_call(
        functools.partial(codes_kernel, lay, factor),
        out_shape=out,
        grid=(1,),
        in_specs=[SMEM, part_of(lay, qt), part_of(lay, bt)] + [whole(x) for x in (num, top, den, mine, theirs)],
        out_specs=whole(out),
        scratch_shapes=[pltpu.VMEM((2, 2, lay.rows, LANES), BF16)],
        cost_estimate=pl.CostEstimate(flops=2000000000, bytes_accessed=14 * tokens * lay.heads * width, transcendentals=0),
        name="attend",
    )(pos, qt, bt, num, top, den, mine, theirs)


def mix_kernel(spans, *refs):
    n = len(spans)
    parts, weights, out_ref = (refs[:n], refs[n : 2 * n], refs[-1])
    base = refs[2 * n] if len(refs) == 2 * n + 2 else None
    tokens, columns = out_ref.shape
    wide = min(columns, 256)
    tile = tokens // 2
    for r in range(0, tokens, tile):
        for c in range(0, columns, wide):
            total = sum(dot(p[r : r + tile, :], w[a:b, c : c + wide]) for p, w, (a, b) in zip(parts, weights, spans))
            if base is not None:
                total = total + base[r : r + tile, c : c + wide]
            out_ref[r : r + tile, c : c + wide] = total.astype(out_ref.dtype)


def mix(terms, base, dtype):
    parts, weights, spans = zip(*terms)
    tokens, columns = (parts[0].shape[0], weights[0].shape[1])
    extra = [] if base is None else [base]
    return pl.pallas_call(
        functools.partial(mix_kernel, spans),
        out_shape=jax.ShapeDtypeStruct((tokens, columns), dtype),
        in_specs=[VMEM] * (2 * len(terms) + len(extra)),
        out_specs=VMEM,
        cost_estimate=pl.CostEstimate(flops=2 * tokens * columns * sum(p.shape[1] for p in parts), bytes_accessed=8 * tokens * columns, transcendentals=0),
        name="mix",
    )(*parts, *weights, *extra)


def swap(x, axis, k):
    return lax.ppermute(x, axis, [(i, i ^ k) for i in range(lax.axis_size(axis))])


def add(a, b):
    return (a.astype(F32) + b.astype(F32)).astype(BF16)


def prefix(keep, give, here):
    upper = lambda bit: (here & bit) != 0
    got1 = swap(give, "ctx", 1)
    mine, send = (add(keep[0], got1[0]), add(keep[1], got1[1]))
    got2 = swap(send, "ctx", 2)
    total = add(mine, got2)
    before = jnp.zeros_like(total)
    bit = 4
    while bit < lax.axis_size("ctx"):
        got = swap(total, "ctx", bit)
        before = jnp.where(upper(bit), add(before, got), before)
        total = add(total, got)
        bit *= 2
    with_low = add(before, jnp.where(upper(2), got2, mine))
    got = swap(jnp.where(upper(2), before, with_low), "ctx", 2)
    before = jnp.stack([jnp.where(upper(2), with_low, before), got])
    with_low = add(before, jnp.where(upper(1), got1, keep))
    got = swap(jnp.where(upper(1), before, with_low), "ctx", 1)
    return jnp.where(upper(1), with_low, before), got


def on_device(queries, values, codes, codebook, out_weight):
    tokens, heads, width = queries.shape
    assert tokens == BLOCK
    devices = lax.axis_size("ctx")
    assert devices & (devices - 1) == 0
    here, side = (lax.axis_index("ctx"), lax.axis_index("head"))
    sides = lax.axis_size("head")
    core, row = (here & 1, here >> 1 & 1)
    pos = jnp.stack([core, row]).astype(jnp.int32)
    count = heads // math.gcd(GROUPS, heads)
    lays = [Layout(devices, first, count, codebook.shape[1]) for first in range(0, heads, count)]
    codes = codes.T

    rows, columns = (out_weight.shape[0], out_weight.shape[1] // sides)
    half = rows // 2
    weights = {0: lax.dynamic_slice(out_weight, (0, side * columns), (rows, columns))}
    for k in range(1, sides):
        block = lax.dynamic_slice(out_weight, (core * half, (side ^ k) * columns), (half, columns))
        mine = swap(block, "head", k)
        other = swap(mine, "ctx", 1)
        first = core == 0
        weights[k] = jnp.stack([jnp.where(first, mine, other), jnp.where(first, other, mine)]).reshape(rows, columns)

    vt, pieces = block_sums(lays[:1], True, pos, codes, values)
    if lays[1:]:
        pieces += block_sums(lays[1:], False, pos, codes, vt)[1]
    qt, bt = turn_inputs(queries, codebook)
    wide = count * width
    terms = []
    for g, (lay, (keep, give)) in enumerate(zip(lays, pieces)):
        num, top, den = window(lay, codes, qt, vt, bt)
        mine, theirs = prefix(keep, give, here)
        attended = attend(lay, pos, qt, bt, num, top, den, mine, theirs)
        span = (g * wide, (g + 1) * wide)
        terms.append((attended, weights[0], span))
        terms += [(swap(attended, "head", k), weights[k], span) for k in range(1, sides)]
    late = len(terms) - (sides - 1)
    return mix(terms[late:], mix(terms[:late], None, F32), BF16)


def solution(mesh):
    return jax.shard_map(
        on_device,
        mesh=mesh,
        in_specs=(
            P("ctx", "head", None),
            P("ctx", "head", None),
            P("ctx", "head"),
            P("head", None, None),
            P("head", None),
        ),
        out_specs=P("ctx", "head"),
        check_vma=False,
    )
```

time: 105 us -> 106 us (level)
  starting transfers between devices: 46.1 us -> 29.8 us
  Pallas kernels: 38.7 us -> 53.1 us
  matrix products: 9.2 us -> 0 us
  waiting for transfers between devices: 1.48 us -> 7.96 us
  local copies, waits for them, and re-layouts: 3.98 us -> 8.49 us
  other arithmetic: 4.46 us -> 5.8 us
    ppermute x12 -> x0, starting transfers between devices: 28.8 us -> none  [ahead(): lax.ppermute(x, axis, [(i, i + k) for i in range(lax.axis_size(axis) - k)])]
    pallas_call x2 -> x9, Pallas kernels: 16.7 us -> 38.2 us  [the longest x4 15.6 us: window(): pl.pallas_call(functools.partial(window_kernel, lay, factor), out_shape=[...]
    ppermute x22 -> x30, starting transfers between devices: 17.2 us -> 29.8 us  [swap(): lax.ppermute(x, axis, [(i, i ^ k) for i in range(lax.axis_size(axis))])]
    dot_general x8 -> x0, matrix products: 9.2 us -> none  [dot(): lax.dot_general(a, b, (contract, ((), ())), preferred_element_type=F32)]
    pallas_call x4, Pallas kernels: 22 us -> 14.9 us  [attend(): pl.pallas_call(functools.partial(codes_kernel, lay, factor), out_shape=ou...]
    ppermute x22 -> x30, waiting for transfers between devices: 1.45 us -> 7.96 us  [swap(): lax.ppermute(x, axis, [(i, i ^ k) for i in range(lax.axis_size(axis))])]
    dynamic_slice x0 -> x1, local copies, waits for them, and re-layouts: none -> 3.17 us  [on_device(): lax.dynamic_slice(out_weight, (0, side * columns), (rows, columns))]
    another operation x2, other arithmetic: 0.34 us -> 1.68 us  [on_device(): jnp.stack([jnp.where(first, mine, other), jnp.where(first, other, mine)])]
  transfers between devices with their start and end apart: 34 -> 30, of which waited for: 3 -> 7; matrix products, arithmetic and copies ran while one was open for 11% -> 9% of each run, Pallas kernels for 37% -> 41%
where the time goes in v2:
time: 106 us; the launch traced here: 105 us
  Pallas kernels  53.1 us (50%)
  starting transfers between devices  29.8 us (28%)
  local copies, waits for them, and re-layouts  8.49 us (8%)
  waiting for transfers between devices  7.96 us (8%)
  other arithmetic  5.8 us (5%)
    ppermute x30, starting transfers between devices, swap(): lax.ppermute(x, axis, [(i, i ^ k) for i in range(lax.axis_size(axis))])  29.8 us
    pallas_call x4, Pallas kernels, window(): pl.pallas_call(functools.partial(window_kernel, lay, factor), out_shape=[...  15.6 us
    pallas_call x4, Pallas kernels, attend(): pl.pallas_call(functools.partial(codes_kernel, lay, factor), out_shape=ou...  14.9 us
    pallas_call x2, Pallas kernels, mix(): pl.pallas_call(functools.partial(mix_kernel, spans), out_shape=jax.ShapeD...  13.4 us
    ppermute x30, waiting for transfers between devices, swap(): lax.ppermute(x, axis, [(i, i ^ k) for i in range(lax.axis_size(axis))])  7.96 us
    pallas_call x2, Pallas kernels, block_sums(): pl.pallas_call(functools.partial(sums_kernel, lays, turn), out_shape=shap...  6 us
    unnamed x26, local copies, waits for them, and re-layouts  4.03 us
    pallas_call x1, Pallas kernels, turn_inputs(): pl.pallas_call(turn_kernel, out_shape=[jax.ShapeDtypeStruct((heads, token...  3.25 us
  transfers between devices with their start and end apart: 30, of which 7 were waited for; matrix products, arithmetic and copies ran while one was open for 9% of the time, Pallas kernels for 41%

profile of v2, /device:TPU:0, one launch (start us, length us, event | category | flops | bytes accessed | tf_op | source)
XLA Modules:
  0.0 105.3 jit_solution(10381368052963999554)
XLA Ops:
  0.7 2.9 %block_sums.2 = (bf16[8,512,128]{2,1,0:T(8,128)(2,1)}, bf16[2,272,128]{2,1,0:T(8,128)(2,1)}, bf16[2,272,128]{2,1,0:T(8,128)(2,1)}) custom-call(s32[2]{0:T(128)} %pad_add_fusion.pos_ref, s32[8,512]{1,0:T(8,128)} %bitcast.68, bf16[512,8,128]{2,1,0:T(8,128)(2,1)} %values_ref.1), custom_call_target="tpu_custom_call" | custom-call | flops 536870912 | bytes 2097152 | tf_op jit(solution)/shard_map/block_sums/pallas_call | solution.py:95
  3.6 3.1 %block_sums.3 = (bf16[2,272,128]{2,1,0:T(8,128)(2,1)}, bf16[2,272,128]{2,1,0:T(8,128)(2,1)}, bf16[2,272,128]{2,1,0:T(8,128)(2,1)}, bf16[2,272,128]{2,1,0:T(8,128...) custom-call(s32[2]{0:T(128)} %pad_add_fusion.pos_ref, s32[8,512]{1,0:T(8,128)} %bitcast.69, ...), custom_call_target="tpu_custom_call" | custom-call | flops 1610612736 | bytes 2097152 | tf_op jit(solution)/shard_map/block_sums/pallas_call | solution.py:95
  7.7 1.3 %dynamic_slice.6 = bf16[512,1024]{1,0:T(8,128)(2,1)S(1)} dynamic-slice(bf16[1024,2048]{1,0:T(8,128)(2,1)} %param.9, s32[]{:T(128)S(6)} %select_n.174, s32[]{:T(128)S(6)} %select_n.175), dynamic_slice_sizes={512,1024} | dynamic-slice | bytes 2097156 | tf_op jit(solution)/shard_map/dynamic_slice | solution.py:307
  9.0 3.0 %collective-permute-start.7 = (bf16[512,1024]{1,0:T(8,128)(2,1)S(1)}, bf16[512,1024]{1,0:T(8,128)(2,1)S(1)}, u32[]{:S(2)}, u32[]{:S(2)}) collective-permute-start(bf16[512,1024]{1,0:T(8,128)(2,1)S(1)} %dynamic_slice.6), channel_id=1, source_target_pairs={{0,1},{1,0},{2,3},{3,2},{4,5},{5,4},{6,7},{7,6},{8,9},{9,8},{10,11... | collective-permute-start | bytes 3145736 | tf_op jit(solution)/shard_map/ppermute | solution.py:262
  12.0 3.2 %turn_inputs.1 = (bf16[8,512,128]{2,1,0:T(8,128)(2,1)}, bf16[8,128,512]{2,1,0:T(8,128)(2,1)}) custom-call(bf16[512,8,128]{2,1,0:T(8,128)(2,1)} %queries_ref.1, bf16[8,512,128]{2,1,0:T(8,128)(2,1)} %book_ref.1), custom_call_target="tpu_custom_call" | custom-call | flops 4000000000 | bytes 4194304 | tf_op jit(solution)/shard_map/turn_inputs/pallas_call | solution.py:119
  15.3 3.9 %window.7 = (f32[2,512,128]{2,1,0:T(8,128)}, f32[2,512,128]{2,1,0:T(8,128)}, f32[2,512,128]{2,1,0:T(8,128)}) custom-call(s32[8,512]{1,0:T(8,128)} %bitcast.70, bf16[8,512,128]{2,1,0:T(8,128)(2,1)} %get-tuple-element.28.qt_ref, bf16[8,512,128]{2,1,0:T(8,128)(2,1)} %get-tuple-element.30.vt_ref.values_ref, bf16[8,128,512]{2,1,0:T(8,128)(2,1)} %get-tuple-element.29.bt_ref), custom_call_target="tpu_custom_call" | custom-call | flops 2400000000 | bytes 2359296 | tf_op jit(solution)/shard_map/window/pallas_call | solution.py:172
  19.2 3.9 %window.6 = (f32[2,512,128]{2,1,0:T(8,128)}, f32[2,512,128]{2,1,0:T(8,128)}, f32[2,512,128]{2,1,0:T(8,128)}) custom-call(s32[8,512]{1,0:T(8,128)} %bitcast.71, bf16[8,512,128]{2,1,0:T(8,128)(2,1)} %get-tuple-element.28.qt_ref, bf16[8,512,128]{2,1,0:T(8,128)(2,1)} %get-tuple-element.30.vt_ref.values_ref, bf16[8,128,512]{2,1,0:T(8,128)(2,1)} %get-tuple-element.29.bt_ref), custom_call_target="tpu_custom_call" | custom-call | flops 2400000000 | bytes 2359296 | tf_op jit(solution)/shard_map/window/pallas_call | solution.py:172
  23.1 3.8 %window.5 = (f32[2,512,128]{2,1,0:T(8,128)}, f32[2,512,128]{2,1,0:T(8,128)}, f32[2,512,128]{2,1,0:T(8,128)}) custom-call(s32[8,512]{1,0:T(8,128)} %bitcast.72, bf16[8,512,128]{2,1,0:T(8,128)(2,1)} %get-tuple-element.28.qt_ref, bf16[8,512,128]{2,1,0:T(8,128)(2,1)} %get-tuple-element.30.vt_ref.values_ref, bf16[8,128,512]{2,1,0:T(8,128)(2,1)} %get-tuple-element.29.bt_ref), custom_call_target="tpu_custom_call" | custom-call | flops 2400000000 | bytes 2359296 | tf_op jit(solution)/shard_map/window/pallas_call | solution.py:172
  26.9 3.9 %window.4 = (f32[2,512,128]{2,1,0:T(8,128)}, f32[2,512,128]{2,1,0:T(8,128)}, f32[2,512,128]{2,1,0:T(8,128)}) custom-call(s32[8,512]{1,0:T(8,128)} %bitcast.73, bf16[8,512,128]{2,1,0:T(8,128)(2,1)} %get-tuple-element.28.qt_ref, bf16[8,512,128]{2,1,0:T(8,128)(2,1)} %get-tuple-element.30.vt_ref.values_ref, bf16[8,128,512]{2,1,0:T(8,128)(2,1)} %get-tuple-element.29.bt_ref), custom_call_target="tpu_custom_call" | custom-call | flops 2400000000 | bytes 2359296 | tf_op jit(solution)/shard_map/window/pallas_call | solution.py:172
  30.8 3.2 %constant_dynamic-slice_fusion.refs_7_.refs_9_.refs_11_.refs_13_ = bf16[1024,1024]{1,0:T(8,128)(2,1)} fusion(bf16[1024,2048]{1,0:T(8,128)(2,1)} %param.9, s32[]{:T(128)S(6)} %select_n.202), kind=kLoop, calls=%fused_computation.76 | loop fusion | bytes 4194308 | tf_op jit(solution)/shard_map/dynamic_slice | solution.py:305
  34.0 1.6 %collective-permute-start.24 = (bf16[272,128]{1,0:T(8,128)(2,1)S(1)}, bf16[272,128]{1,0:T(8,128)(2,1)S(1)}, u32[]{:S(2)}, u32[]{:S(2)}) collective-permute-start(bf16[272,128]{1,0:T(8,128)(2,1)S(1)} %fusion.31), channel_id=1, source_target_pairs={{0,4},{2,6},{4,0},{6,2},{8,12},{10,14},{12,8},{14,10},{16,20},{18,... | collective-permute-start | bytes 208904 | tf_op jit(solution)/shard_map/ppermute | solution.py:262
  36.3 1.6 %collective-permute-start.10 = (bf16[272,128]{1,0:T(8,128)(2,1)S(1)}, bf16[272,128]{1,0:T(8,128)(2,1)S(1)}, u32[]{:S(2)}, u32[]{:S(2)}) collective-permute-start(bf16[272,128]{1,0:T(8,128)(2,1)S(1)} %fusion.27), channel_id=1, source_target_pairs={{0,4},{2,6},{4,0},{6,2},{8,12},{10,14},{12,8},{14,10},{16,20},{18,... | collective-permute-start | bytes 208904 | tf_op jit(solution)/shard_map/ppermute | solution.py:262
  39.1 1.6 %collective-permute-start.25 = (bf16[272,128]{1,0:T(8,128)(2,1)S(1)}, bf16[272,128]{1,0:T(8,128)(2,1)S(1)}, u32[]{:S(2)}, u32[]{:S(2)}) collective-permute-start(bf16[272,128]{1,0:T(8,128)(2,1)S(1)} %add_convert_fusion.7), channel_id=1, source_target_pairs={{0,8},{2,10},{4,12},{6,14},{8,0},{10,2},{12,4},{14,6},{16,24},{18,... | collective-permute-start | bytes 208904 | tf_op jit(solution)/shard_map/ppermute | solution.py:262
  40.8 1.6 %collective-permute-start.18 = (bf16[272,128]{1,0:T(8,128)(2,1)S(1)}, bf16[272,128]{1,0:T(8,128)(2,1)S(1)}, u32[]{:S(2)}, u32[]{:S(2)}) collective-permute-start(bf16[272,128]{1,0:T(8,128)(2,1)S(1)} %add_convert_fusion.13), channel_id=1, source_target_pairs={{0,8},{2,10},{4,12},{6,14},{8,0},{10,2},{12,4},{14,6},{16,24},{18,... | collective-permute-start | bytes 208904 | tf_op jit(solution)/shard_map/ppermute | solution.py:262
  42.5 1.3 %collective-permute-start.11 = (bf16[272,128]{1,0:T(8,128)(2,1)S(1)}, bf16[272,128]{1,0:T(8,128)(2,1)S(1)}, u32[]{:S(2)}, u32[]{:S(2)}) collective-permute-start(bf16[272,128]{1,0:T(8,128)(2,1)S(1)} %add_convert_fusion.19), channel_id=1, source_target_pairs={{0,8},{2,10},{4,12},{6,14},{8,0},{10,2},{12,4},{14,6},{16,24},{18,... | collective-permute-start | bytes 208904 | tf_op jit(solution)/shard_map/ppermute | solution.py:262
  44.7 2.7 %collective-permute-start.26 = (bf16[272,128]{1,0:T(8,128)(2,1)S(1)}, bf16[272,128]{1,0:T(8,128)(2,1)S(1)}, u32[]{:S(2)}, u32[]{:S(2)}) collective-permute-start(bf16[272,128]{1,0:T(8,128)(2,1)S(1)} %add_convert_fusion.6), channel_id=1, source_target_pairs={{0,16},{2,18},{4,20},{6,22},{8,24},{10,26},{12,28},{14,30},{16,0},... | collective-permute-start | bytes 208904 | tf_op jit(solution)/shard_map/ppermute | solution.py:262
  48.3 2.2 %collective-permute-start.12 = (bf16[272,128]{1,0:T(8,128)(2,1)S(1)}, bf16[272,128]{1,0:T(8,128)(2,1)S(1)}, u32[]{:S(2)}, u32[]{:S(2)}) collective-permute-start(bf16[272,128]{1,0:T(8,128)(2,1)S(1)} %add_convert_fusion.18), channel_id=1, source_target_pairs={{0,16},{2,18},{4,20},{6,22},{8,24},{10,26},{12,28},{14,30},{16,0},... | collective-permute-start | bytes 208904 | tf_op jit(solution)/shard_map/ppermute | solution.py:262
  50.5 1.1 %collective-permute-start.3 = (bf16[272,128]{1,0:T(8,128)(2,1)S(1)}, bf16[272,128]{1,0:T(8,128)(2,1)S(1)}, u32[]{:S(2)}, u32[]{:S(2)}) collective-permute-start(bf16[272,128]{1,0:T(8,128)(2,1)S(1)} %add_convert_fusion.24), channel_id=1, source_target_pairs={{0,16},{2,18},{4,20},{6,22},{8,24},{10,26},{12,28},{14,30},{16,0},... | collective-permute-start | bytes 208904 | tf_op jit(solution)/shard_map/ppermute | solution.py:262
  51.7 3.3 %collective-permute-done.26 = bf16[272,128]{1,0:T(8,128)(2,1)S(1)} collective-permute-done((bf16[272,128]{1,0:T(8,128)(2,1)S(1)}, bf16[272,128]{1,0:T(8,128)(2,1)S(1)}, u32[]{:S(2)}, u32[]{:S(2)}) %collective-permute-start.26) | collective-permute-done | bytes 69664 | tf_op jit(solution)/shard_map/ppermute | solution.py:262
  55.7 1.5 %collective-permute-done.19 = bf16[272,128]{1,0:T(8,128)(2,1)S(1)} collective-permute-done((bf16[272,128]{1,0:T(8,128)(2,1)S(1)}, bf16[272,128]{1,0:T(8,128)(2,1)S(1)}, u32[]{:S(2)}, u32[]{:S(2)}) %collective-permute-start.19) | collective-permute-done | bytes 69664 | tf_op jit(solution)/shard_map/ppermute | solution.py:262
  57.3 1.4 %collective-permute-start.20 = (bf16[272,128]{1,0:T(8,128)(2,1)S(1)}, bf16[272,128]{1,0:T(8,128)(2,1)S(1)}, u32[]{:S(2)}, u32[]{:S(2)}) collective-permute-start(bf16[272,128]{1,0:T(8,128)(2,1)S(1)} %get-tuple-element.56), channel_id=1, source_target_pairs={{0,4},{2,6},{4,0},{6,2},{8,12},{10,14},{12,8},{14,10},{16,20},{18,... | collective-permute-start | bytes 208904 | tf_op jit(solution)/shard_map/ppermute | solution.py:262
  58.8 1.1 %collective-permute-start.13 = (bf16[272,128]{1,0:T(8,128)(2,1)S(1)}, bf16[272,128]{1,0:T(8,128)(2,1)S(1)}, u32[]{:S(2)}, u32[]{:S(2)}) collective-permute-start(bf16[272,128]{1,0:T(8,128)(2,1)S(1)} %get-tuple-element.58), channel_id=1, source_target_pairs={{0,4},{2,6},{4,0},{6,2},{8,12},{10,14},{12,8},{14,10},{16,20},{18,... | collective-permute-start | bytes 208904 | tf_op jit(solution)/shard_map/ppermute | solution.py:262
  66.1 3.8 %attend.7.refs_4_ = bf16[512,256]{1,0:T(8,128)(2,1)} custom-call(s32[2]{0:T(128)} %pad_add_fusion.pos_ref, bf16[8,512,128]{2,1,0:T(8,128)(2,1)} %get-tuple-element.28.qt_ref, bf16[8,128,512]{2,1,0:T(8,128)(2,1)} %get-tuple-element.29.bt_ref, f32[2,512,128]{2,1,0:T(8,128)} %get-tuple-element.46.num_ref, f32[2,512,128]{2,1,0:T(8,128)} %get-tuple-element.47.top_ref, ...), custom_call_target="tpu_custom_call" | custom-call | flops 2000000000 | bytes 1835008 | tf_op jit(solution)/shard_map/attend/pallas_call | solution.py:220
  71.1 3.7 %attend.6.refs_2_ = bf16[512,256]{1,0:T(8,128)(2,1)} custom-call(s32[2]{0:T(128)} %pad_add_fusion.pos_ref, bf16[8,512,128]{2,1,0:T(8,128)(2,1)} %get-tuple-element.28.qt_ref, bf16[8,128,512]{2,1,0:T(8,128)(2,1)} %get-tuple-element.29.bt_ref, f32[2,512,128]{2,1,0:T(8,128)} %get-tuple-element.41.num_ref, f32[2,512,128]{2,1,0:T(8,128)} %get-tuple-element.42.top_ref, ...), custom_call_target="tpu_custom_call" | custom-call | flops 2000000000 | bytes 1835008 | tf_op jit(solution)/shard_map/attend/pallas_call | solution.py:220
  74.8 1.5 %collective-permute-start.22 = (bf16[512,256]{1,0:T(8,128)(2,1)}, bf16[512,256]{1,0:T(8,128)(2,1)S(1)}, u32[]{:S(2)}, u32[]{:S(2)}) collective-permute-start(bf16[512,256]{1,0:T(8,128)(2,1)} %attend.6.refs_2_), channel_id=1, source_target_pairs={{0,1},{1,0},{2,3},{3,2},{4,5},{5,4},{6,7},{7,6},{8,9},{9,8},{10,11... | collective-permute-start | bytes 786440 | tf_op jit(solution)/shard_map/ppermute | solution.py:262
  77.0 3.7 %attend.5.refs_0_ = bf16[512,256]{1,0:T(8,128)(2,1)} custom-call(s32[2]{0:T(128)} %pad_add_fusion.pos_ref, bf16[8,512,128]{2,1,0:T(8,128)(2,1)} %get-tuple-element.28.qt_ref, bf16[8,128,512]{2,1,0:T(8,128)(2,1)} %get-tuple-element.29.bt_ref, f32[2,512,128]{2,1,0:T(8,128)} %get-tuple-element.36.num_ref, f32[2,512,128]{2,1,0:T(8,128)} %get-tuple-element.37.top_ref, ...), custom_call_target="tpu_custom_call" | custom-call | flops 2000000000 | bytes 1835008 | tf_op jit(solution)/shard_map/attend/pallas_call | solution.py:220
  81.9 3.7 %attend.4.refs_6_ = bf16[512,256]{1,0:T(8,128)(2,1)} custom-call(s32[2]{0:T(128)} %pad_add_fusion.pos_ref, bf16[8,512,128]{2,1,0:T(8,128)(2,1)} %get-tuple-element.28.qt_ref, bf16[8,128,512]{2,1,0:T(8,128)(2,1)} %get-tuple-element.29.bt_ref, f32[2,512,128]{2,1,0:T(8,128)} %get-tuple-element.31.num_ref, f32[2,512,128]{2,1,0:T(8,128)} %get-tuple-element.32.top_ref, ...), custom_call_target="tpu_custom_call" | custom-call | flops 2000000000 | bytes 1835008 | tf_op jit(solution)/shard_map/attend/pallas_call | solution.py:220
  85.6 1.5 %collective-permute-start.6 = (bf16[512,256]{1,0:T(8,128)(2,1)}, bf16[512,256]{1,0:T(8,128)(2,1)S(1)}, u32[]{:S(2)}, u32[]{:S(2)}) collective-permute-start(bf16[512,256]{1,0:T(8,128)(2,1)} %attend.4.refs_6_), channel_id=1, source_target_pairs={{0,1},{1,0},{2,3},{3,2},{4,5},{5,4},{6,7},{7,6},{8,9},{9,8},{10,11... | collective-permute-start | bytes 786440 | tf_op jit(solution)/shard_map/ppermute | solution.py:262
  87.3 1.5 %pad_maximum_fusion = bf16[2,512,1024]{2,1,0:T(8,128)(2,1)} fusion(bf16[1,512,1024]{2,1,0:T(8,128)(2,1)S(1)} %get-tuple-element.52, bf16[1,512,1024]{2,1,0:T(8,128)(2,1)S(1)} %get-tuple-element.51), kind=kLoop, calls=%fused_computation | loop fusion | flops 1048576 | bytes 4194304 | tf_op jit(solution)/shard_map/stack | solution.py:311
  88.8 1.7 %collective-permute-done.15.refs_1_ = bf16[512,256]{1,0:T(8,128)(2,1)S(1)} collective-permute-done((bf16[512,256]{1,0:T(8,128)(2,1)}, bf16[512,256]{1,0:T(8,128)(2,1)S(1)}, u32[]{:S(2)}, u32[]{:S(2)}) %collective-permute-start.15) | collective-permute-done | bytes 262176 | tf_op jit(solution)/shard_map/ppermute | solution.py:262
  91.2 9.6 %mix.2.refs_2_ = f32[512,1024]{1,0:T(8,128)} custom-call(bf16[512,256]{1,0:T(8,128)(2,1)} %attend.5.refs_0_, bf16[512,256]{1,0:T(8,128)(2,1)} %copy-done.6, bf16[512,256]{1,0:T(8,128)(2,1)} %attend.6.refs_2_, bf16[512,256]{1,0:T(8,128)(2,1)} %copy-done.5, bf16[512,256]{1,0:T(8,128)(2,1)} %attend.7.refs_4_, bf16[512,256]{1,0:T(8,128)(2,1)} %copy-done.4, ...), custom_call_target="tpu_custom_call" | custom-call | flops 1879048192 | bytes 4194304 | tf_op jit(solution)/shard_map/mix/pallas_call | solution.py:251
  101.6 3.7 %mix.3 = bf16[512,1024]{1,0:T(8,128)(2,1)} custom-call(bf16[512,256]{1,0:T(8,128)(2,1)} %copy-done.7, bf16[1024,1024]{1,0:T(8,128)(2,1)} %bitcast.63, f32[512,1024]{1,0:T(8,128)} %mix.2.refs_2_), custom_call_target="tpu_custom_call" | custom-call | flops 268435456 | bytes 4194304 | tf_op jit(solution)/shard_map/mix/pallas_call | solution.py:251
  (92 shorter events, 17.1 us)
Async XLA Ops:
  6.7 27.4 %collective-permute-start.23 = (bf16[2,272,128]{2,1,0:T(8,128)(2,1)}, bf16[2,272,128]{2,1,0:T(8,128)(2,1)S(1)}, u32[]{:S(2)}, u32[]{:S(2)}) collective-permute-start(bf16[2,272,128]{2,1,0:T(8,128)(2,1)} %get-tuple-element.50), channel_id=1, source_target_pairs={{0,2},{2,0},{4,6},{6,4},{8,10},{10,8},{12,14},{14,12},{16,18},{18,... | collective-permute-start | bytes 417800 | tf_op jit(solution)/shard_map/ppermute | solution.py:262
  7.2 28.5 %collective-permute-start.16 = (bf16[2,272,128]{2,1,0:T(8,128)(2,1)}, bf16[2,272,128]{2,1,0:T(8,128)(2,1)S(1)}, u32[]{:S(2)}, u32[]{:S(2)}) collective-permute-start(bf16[2,272,128]{2,1,0:T(8,128)(2,1)} %get-tuple-element.45), channel_id=1, source_target_pairs={{0,2},{2,0},{4,6},{6,4},{8,10},{10,8},{12,14},{14,12},{16,18},{18,... | collective-permute-start | bytes 417800 | tf_op jit(solution)/shard_map/ppermute | solution.py:262
  7.2 29.1 %collective-permute-start.9 = (bf16[2,272,128]{2,1,0:T(8,128)(2,1)S(1)}, bf16[2,272,128]{2,1,0:T(8,128)(2,1)S(1)}, u32[]{:S(2)}, u32[]{:S(2)}) collective-permute-start(bf16[2,272,128]{2,1,0:T(8,128)(2,1)S(1)} %copy-done.8), channel_id=1, source_target_pairs={{0,2},{2,0},{4,6},{6,4},{8,10},{10,8},{12,14},{14,12},{16,18},{18,... | collective-permute-start | bytes 417800 | tf_op jit(solution)/shard_map/ppermute | solution.py:262
  7.7 30.2 %collective-permute-start = (bf16[2,272,128]{2,1,0:T(8,128)(2,1)}, bf16[2,272,128]{2,1,0:T(8,128)(2,1)S(1)}, u32[]{:S(2)}, u32[]{:S(2)}) collective-permute-start(bf16[2,272,128]{2,1,0:T(8,128)(2,1)} %get-tuple-element.35), channel_id=1, source_target_pairs={{0,2},{2,0},{4,6},{6,4},{8,10},{10,8},{12,14},{14,12},{16,18},{18,... | collective-permute-start | bytes 417800 | tf_op jit(solution)/shard_map/ppermute | solution.py:262
  9.0 54.0 %collective-permute-start.7 = (bf16[512,1024]{1,0:T(8,128)(2,1)S(1)}, bf16[512,1024]{1,0:T(8,128)(2,1)S(1)}, u32[]{:S(2)}, u32[]{:S(2)}) collective-permute-start(bf16[512,1024]{1,0:T(8,128)(2,1)S(1)} %dynamic_slice.6), channel_id=1, source_target_pairs={{0,1},{1,0},{2,3},{3,2},{4,5},{5,4},{6,7},{7,6},{8,9},{9,8},{10,11... | collective-permute-start | bytes 3145736 | tf_op jit(solution)/shard_map/ppermute | solution.py:262
  30.8 5.4 %copy-start.1 = (bf16[2,272,128]{2,1,0:T(8,128)(2,1)S(1)}, bf16[2,272,128]{2,1,0:T(8,128)(2,1)}, u32[]{:S(2)}) copy-start(bf16[2,272,128]{2,1,0:T(8,128)(2,1)} %get-tuple-element.39) | copy-start | bytes 417796
  30.8 7.0 %copy-start = (bf16[2,272,128]{2,1,0:T(8,128)(2,1)S(1)}, bf16[2,272,128]{2,1,0:T(8,128)(2,1)}, u32[]{:S(2)}) copy-start(bf16[2,272,128]{2,1,0:T(8,128)(2,1)} %get-tuple-element.34) | copy-start | bytes 417796
  34.0 5.0 %collective-permute-start.24 = (bf16[272,128]{1,0:T(8,128)(2,1)S(1)}, bf16[272,128]{1,0:T(8,128)(2,1)S(1)}, u32[]{:S(2)}, u32[]{:S(2)}) collective-permute-start(bf16[272,128]{1,0:T(8,128)(2,1)S(1)} %fusion.31), channel_id=1, source_target_pairs={{0,4},{2,6},{4,0},{6,2},{8,12},{10,14},{12,8},{14,10},{16,20},{18,... | collective-permute-start | bytes 208904 | tf_op jit(solution)/shard_map/ppermute | solution.py:262
  35.7 5.1 %collective-permute-start.17 = (bf16[272,128]{1,0:T(8,128)(2,1)S(1)}, bf16[272,128]{1,0:T(8,128)(2,1)S(1)}, u32[]{:S(2)}, u32[]{:S(2)}) collective-permute-start(bf16[272,128]{1,0:T(8,128)(2,1)S(1)} %fusion.29), channel_id=1, source_target_pairs={{0,4},{2,6},{4,0},{6,2},{8,12},{10,14},{12,8},{14,10},{16,20},{18,... | collective-permute-start | bytes 208904 | tf_op jit(solution)/shard_map/ppermute | solution.py:262
  36.3 6.2 %collective-permute-start.10 = (bf16[272,128]{1,0:T(8,128)(2,1)S(1)}, bf16[272,128]{1,0:T(8,128)(2,1)S(1)}, u32[]{:S(2)}, u32[]{:S(2)}) collective-permute-start(bf16[272,128]{1,0:T(8,128)(2,1)S(1)} %fusion.27), channel_id=1, source_target_pairs={{0,4},{2,6},{4,0},{6,2},{8,12},{10,14},{12,8},{14,10},{16,20},{18,... | collective-permute-start | bytes 208904 | tf_op jit(solution)/shard_map/ppermute | solution.py:262
  37.9 5.9 %collective-permute-start.1 = (bf16[272,128]{1,0:T(8,128)(2,1)S(1)}, bf16[272,128]{1,0:T(8,128)(2,1)S(1)}, u32[]{:S(2)}, u32[]{:S(2)}) collective-permute-start(bf16[272,128]{1,0:T(8,128)(2,1)S(1)} %fusion.25), channel_id=1, source_target_pairs={{0,4},{2,6},{4,0},{6,2},{8,12},{10,14},{12,8},{14,10},{16,20},{18,... | collective-permute-start | bytes 208904 | tf_op jit(solution)/shard_map/ppermute | solution.py:262
  39.1 5.6 %collective-permute-start.25 = (bf16[272,128]{1,0:T(8,128)(2,1)S(1)}, bf16[272,128]{1,0:T(8,128)(2,1)S(1)}, u32[]{:S(2)}, u32[]{:S(2)}) collective-permute-start(bf16[272,128]{1,0:T(8,128)(2,1)S(1)} %add_convert_fusion.7), channel_id=1, source_target_pairs={{0,8},{2,10},{4,12},{6,14},{8,0},{10,2},{12,4},{14,6},{16,24},{18,... | collective-permute-start | bytes 208904 | tf_op jit(solution)/shard_map/ppermute | solution.py:262
  40.8 6.6 %collective-permute-start.18 = (bf16[272,128]{1,0:T(8,128)(2,1)S(1)}, bf16[272,128]{1,0:T(8,128)(2,1)S(1)}, u32[]{:S(2)}, u32[]{:S(2)}) collective-permute-start(bf16[272,128]{1,0:T(8,128)(2,1)S(1)} %add_convert_fusion.13), channel_id=1, source_target_pairs={{0,8},{2,10},{4,12},{6,14},{8,0},{10,2},{12,4},{14,6},{16,24},{18,... | collective-permute-start | bytes 208904 | tf_op jit(solution)/shard_map/ppermute | solution.py:262
  42.5 5.7 %collective-permute-start.11 = (bf16[272,128]{1,0:T(8,128)(2,1)S(1)}, bf16[272,128]{1,0:T(8,128)(2,1)S(1)}, u32[]{:S(2)}, u32[]{:S(2)}) collective-permute-start(bf16[272,128]{1,0:T(8,128)(2,1)S(1)} %add_convert_fusion.19), channel_id=1, source_target_pairs={{0,8},{2,10},{4,12},{6,14},{8,0},{10,2},{12,4},{14,6},{16,24},{18,... | collective-permute-start | bytes 208904 | tf_op jit(solution)/shard_map/ppermute | solution.py:262
  43.9 6.6 %collective-permute-start.2 = (bf16[272,128]{1,0:T(8,128)(2,1)S(1)}, bf16[272,128]{1,0:T(8,128)(2,1)S(1)}, u32[]{:S(2)}, u32[]{:S(2)}) collective-permute-start(bf16[272,128]{1,0:T(8,128)(2,1)S(1)} %add_convert_fusion.25), channel_id=1, source_target_pairs={{0,8},{2,10},{4,12},{6,14},{8,0},{10,2},{12,4},{14,6},{16,24},{18,... | collective-permute-start | bytes 208904 | tf_op jit(solution)/shard_map/ppermute | solution.py:262
  44.7 10.3 %collective-permute-start.26 = (bf16[272,128]{1,0:T(8,128)(2,1)S(1)}, bf16[272,128]{1,0:T(8,128)(2,1)S(1)}, u32[]{:S(2)}, u32[]{:S(2)}) collective-permute-start(bf16[272,128]{1,0:T(8,128)(2,1)S(1)} %add_convert_fusion.6), channel_id=1, source_target_pairs={{0,16},{2,18},{4,20},{6,22},{8,24},{10,26},{12,28},{14,30},{16,0},... | collective-permute-start | bytes 208904 | tf_op jit(solution)/shard_map/ppermute | solution.py:262
  47.4 9.8 %collective-permute-start.19 = (bf16[272,128]{1,0:T(8,128)(2,1)S(1)}, bf16[272,128]{1,0:T(8,128)(2,1)S(1)}, u32[]{:S(2)}, u32[]{:S(2)}) collective-permute-start(bf16[272,128]{1,0:T(8,128)(2,1)S(1)} %add_convert_fusion.12), channel_id=1, source_target_pairs={{0,16},{2,18},{4,20},{6,22},{8,24},{10,26},{12,28},{14,30},{16,0},... | collective-permute-start | bytes 208904 | tf_op jit(solution)/shard_map/ppermute | solution.py:262
  48.3 10.5 %collective-permute-start.12 = (bf16[272,128]{1,0:T(8,128)(2,1)S(1)}, bf16[272,128]{1,0:T(8,128)(2,1)S(1)}, u32[]{:S(2)}, u32[]{:S(2)}) collective-permute-start(bf16[272,128]{1,0:T(8,128)(2,1)S(1)} %add_convert_fusion.18), channel_id=1, source_target_pairs={{0,16},{2,18},{4,20},{6,22},{8,24},{10,26},{12,28},{14,30},{16,0},... | collective-permute-start | bytes 208904 | tf_op jit(solution)/shard_map/ppermute | solution.py:262
  50.5 9.4 %collective-permute-start.3 = (bf16[272,128]{1,0:T(8,128)(2,1)S(1)}, bf16[272,128]{1,0:T(8,128)(2,1)S(1)}, u32[]{:S(2)}, u32[]{:S(2)}) collective-permute-start(bf16[272,128]{1,0:T(8,128)(2,1)S(1)} %add_convert_fusion.24), channel_id=1, source_target_pairs={{0,16},{2,18},{4,20},{6,22},{8,24},{10,26},{12,28},{14,30},{16,0},... | collective-permute-start | bytes 208904 | tf_op jit(solution)/shard_map/ppermute | solution.py:262
  55.1 6.0 %collective-permute-start.27 = (bf16[272,128]{1,0:T(8,128)(2,1)S(1)}, bf16[272,128]{1,0:T(8,128)(2,1)S(1)}, u32[]{:S(2)}, u32[]{:S(2)}) collective-permute-start(bf16[272,128]{1,0:T(8,128)(2,1)S(1)} %get-tuple-element.54), channel_id=1, source_target_pairs={{0,4},{2,6},{4,0},{6,2},{8,12},{10,14},{12,8},{14,10},{16,20},{18,... | collective-permute-start | bytes 208904 | tf_op jit(solution)/shard_map/ppermute | solution.py:262
  57.3 4.7 %collective-permute-start.20 = (bf16[272,128]{1,0:T(8,128)(2,1)S(1)}, bf16[272,128]{1,0:T(8,128)(2,1)S(1)}, u32[]{:S(2)}, u32[]{:S(2)}) collective-permute-start(bf16[272,128]{1,0:T(8,128)(2,1)S(1)} %get-tuple-element.56), channel_id=1, source_target_pairs={{0,4},{2,6},{4,0},{6,2},{8,12},{10,14},{12,8},{14,10},{16,20},{18,... | collective-permute-start | bytes 208904 | tf_op jit(solution)/shard_map/ppermute | solution.py:262
  58.8 4.7 %collective-permute-start.13 = (bf16[272,128]{1,0:T(8,128)(2,1)S(1)}, bf16[272,128]{1,0:T(8,128)(2,1)S(1)}, u32[]{:S(2)}, u32[]{:S(2)}) collective-permute-start(bf16[272,128]{1,0:T(8,128)(2,1)S(1)} %get-tuple-element.58), channel_id=1, source_target_pairs={{0,4},{2,6},{4,0},{6,2},{8,12},{10,14},{12,8},{14,10},{16,20},{18,... | collective-permute-start | bytes 208904 | tf_op jit(solution)/shard_map/ppermute | solution.py:262
  60.0 4.4 %collective-permute-start.4 = (bf16[272,128]{1,0:T(8,128)(2,1)S(1)}, bf16[272,128]{1,0:T(8,128)(2,1)S(1)}, u32[]{:S(2)}, u32[]{:S(2)}) collective-permute-start(bf16[272,128]{1,0:T(8,128)(2,1)S(1)} %get-tuple-element.60), channel_id=1, source_target_pairs={{0,4},{2,6},{4,0},{6,2},{8,12},{10,14},{12,8},{14,10},{16,20},{18,... | collective-permute-start | bytes 208904 | tf_op jit(solution)/shard_map/ppermute | solution.py:262
  61.8 3.7 %collective-permute-start.28 = (bf16[2,272,128]{2,1,0:T(8,128)(2,1)S(1)}, bf16[2,272,128]{2,1,0:T(8,128)(2,1)S(1)}, u32[]{:S(2)}, u32[]{:S(2)}) collective-permute-start(bf16[2,272,128]{2,1,0:T(8,128)(2,1)S(1)} %get-tuple-element.61), channel_id=1, source_target_pairs={{0,2},{2,0},{4,6},{6,4},{8,10},{10,8},{12,14},{14,12},{16,18},{18,... | collective-permute-start | bytes 417800 | tf_op jit(solution)/shard_map/ppermute | solution.py:262
  62.7 7.7 %collective-permute-start.21 = (bf16[2,272,128]{2,1,0:T(8,128)(2,1)S(1)}, bf16[2,272,128]{2,1,0:T(8,128)(2,1)S(1)}, u32[]{:S(2)}, u32[]{:S(2)}) collective-permute-start(bf16[2,272,128]{2,1,0:T(8,128)(2,1)S(1)} %get-tuple-element.63), channel_id=1, source_target_pairs={{0,2},{2,0},{4,6},{6,4},{8,10},{10,8},{12,14},{14,12},{16,18},{18,... | collective-permute-start | bytes 417800 | tf_op jit(solution)/shard_map/ppermute | solution.py:262
  63.0 24.1 %collective-permute-start.8 = (bf16[512,1024]{1,0:T(8,128)(2,1)S(1)}, bf16[512,1024]{1,0:T(8,128)(2,1)S(1)}, u32[]{:S(2)}, u32[]{:S(2)}) collective-permute-start(bf16[512,1024]{1,0:T(8,128)(2,1)S(1)} %collective-permute-done.7), channel_id=1, source_target_pairs={{0,2},{2,0},{4,6},{6,4},{8,10},{10,8},{12,14},{14,12},{16,18},{18,... | collective-permute-start | bytes 3145736 | tf_op jit(solution)/shard_map/ppermute | solution.py:262
  64.2 12.1 %collective-permute-start.14 = (bf16[2,272,128]{2,1,0:T(8,128)(2,1)S(1)}, bf16[2,272,128]{2,1,0:T(8,128)(2,1)S(1)}, u32[]{:S(2)}, u32[]{:S(2)}) collective-permute-start(bf16[2,272,128]{2,1,0:T(8,128)(2,1)S(1)} %get-tuple-element.65), channel_id=1, source_target_pairs={{0,2},{2,0},{4,6},{6,4},{8,10},{10,8},{12,14},{14,12},{16,18},{18,... | collective-permute-start | bytes 417800 | tf_op jit(solution)/shard_map/ppermute | solution.py:262
  65.1 16.1 %collective-permute-start.5 = (bf16[2,272,128]{2,1,0:T(8,128)(2,1)S(1)}, bf16[2,272,128]{2,1,0:T(8,128)(2,1)S(1)}, u32[]{:S(2)}, u32[]{:S(2)}) collective-permute-start(bf16[2,272,128]{2,1,0:T(8,128)(2,1)S(1)} %get-tuple-element.67), channel_id=1, source_target_pairs={{0,2},{2,0},{4,6},{6,4},{8,10},{10,8},{12,14},{14,12},{16,18},{18,... | collective-permute-start | bytes 417800 | tf_op jit(solution)/shard_map/ppermute | solution.py:262
  69.9 18.9 %collective-permute-start.29 = (bf16[512,256]{1,0:T(8,128)(2,1)}, bf16[512,256]{1,0:T(8,128)(2,1)S(1)}, u32[]{:S(2)}, u32[]{:S(2)}) collective-permute-start(bf16[512,256]{1,0:T(8,128)(2,1)} %attend.7.refs_4_), channel_id=1, source_target_pairs={{0,1},{1,0},{2,3},{3,2},{4,5},{5,4},{6,7},{7,6},{8,9},{9,8},{10,11... | collective-permute-start | bytes 786440 | tf_op jit(solution)/shard_map/ppermute | solution.py:262
  74.8 14.0 %collective-permute-start.22 = (bf16[512,256]{1,0:T(8,128)(2,1)}, bf16[512,256]{1,0:T(8,128)(2,1)S(1)}, u32[]{:S(2)}, u32[]{:S(2)}) collective-permute-start(bf16[512,256]{1,0:T(8,128)(2,1)} %attend.6.refs_2_), channel_id=1, source_target_pairs={{0,1},{1,0},{2,3},{3,2},{4,5},{5,4},{6,7},{7,6},{8,9},{9,8},{10,11... | collective-permute-start | bytes 786440 | tf_op jit(solution)/shard_map/ppermute | solution.py:262
  80.7 9.8 %collective-permute-start.15 = (bf16[512,256]{1,0:T(8,128)(2,1)}, bf16[512,256]{1,0:T(8,128)(2,1)S(1)}, u32[]{:S(2)}, u32[]{:S(2)}) collective-permute-start(bf16[512,256]{1,0:T(8,128)(2,1)} %attend.5.refs_0_), channel_id=1, source_target_pairs={{0,1},{1,0},{2,3},{3,2},{4,5},{5,4},{6,7},{7,6},{8,9},{9,8},{10,11... | collective-permute-start | bytes 786440 | tf_op jit(solution)/shard_map/ppermute | solution.py:262
  85.6 15.2 %collective-permute-start.6 = (bf16[512,256]{1,0:T(8,128)(2,1)}, bf16[512,256]{1,0:T(8,128)(2,1)S(1)}, u32[]{:S(2)}, u32[]{:S(2)}) collective-permute-start(bf16[512,256]{1,0:T(8,128)(2,1)} %attend.4.refs_6_), channel_id=1, source_target_pairs={{0,1},{1,0},{2,3},{3,2},{4,5},{5,4},{6,7},{7,6},{8,9},{9,8},{10,11... | collective-permute-start | bytes 786440 | tf_op jit(solution)/shard_map/ppermute | solution.py:262
  (11 other events, 19.1 us)

commit v3 on v2

--- a/solution.py
+++ b/solution.py
@@ -10,12 +10,15 @@
 
 BLOCK = 512
 LANES = 128
-GROUPS = 4
+SIZES = (2, 2, 2, 2)
+LIMIT = 20 << 20
 NEVER = -1e30
 F32 = jnp.float32
 BF16 = jnp.bfloat16
 VMEM = pl.BlockSpec(memory_space=pltpu.VMEM)
 SMEM = pl.BlockSpec(memory_space=pltpu.SMEM)
+ANY = pl.BlockSpec(memory_space=pl.ANY)
+PARAMS = pltpu.CompilerParams(vmem_limit_bytes=LIMIT)
 
 
 def dot(a, b, contract=((1,), (0,))):
@@ -98,6 +101,7 @@
         in_specs=[SMEM, VMEM, VMEM],
         out_specs=[VMEM] * len(shapes),
         scratch_shapes=[pltpu.VMEM((2, 2, max(lay.rows for lay in lays), LANES), BF16)],
+        compiler_params=PARAMS,
         cost_estimate=pl.CostEstimate(
             flops=8 * some * tokens * lays[0].each * LANES * width, bytes_accessed=4 * tokens * heads * width, transcendentals=0
         ),
@@ -108,13 +112,14 @@
     return vt, [(outs[2 * g], outs[2 * g + 1]) for g in range(len(lays))]
 
 
-def turn_kernel(queries_ref, book_ref, qt_ref, bt_ref):
+def turn_kernel(after_ref, queries_ref, book_ref, qt_ref, bt_ref):
+    del after_ref
     qt_ref[...] = jnp.swapaxes(queries_ref[...], 0, 1)
     for h in range(book_ref.shape[0]):
         bt_ref[h] = book_ref[h].T
 
 
-def turn_inputs(queries, book):
+def turn_inputs(after, queries, book):
     tokens, heads, width = queries.shape
     return pl.pallas_call(
         turn_kernel,
@@ -122,29 +127,32 @@
             jax.ShapeDtypeStruct((heads, tokens, width), BF16),
             jax.ShapeDtypeStruct((heads, width, book.shape[1]), BF16),
         ],
-        in_specs=[VMEM] * 2,
+        in_specs=[ANY, VMEM, VMEM],
         out_specs=[VMEM] * 2,
+        compiler_params=PARAMS,
         cost_estimate=pl.CostEstimate(flops=4000000000, bytes_accessed=8 * tokens * heads * width, transcendentals=0),
         name="turn_inputs",
-    )(queries, book)
+    )(after, queries, book)
 
 
 def lane_tiles(x):
     return [x[:, j : j + LANES] for j in range(0, x.shape[1], LANES)]
 
 
-def window_kernel(lay, factor, codes_ref, qt_ref, vt_ref, bt_ref, num_ref, top_ref, den_ref):
+def window_kernel(lay, factor, after_ref, codes_ref, qt_ref, vt_ref, bt_ref, num_ref, top_ref, den_ref):
+    del after_ref
     tokens = qt_ref.shape[1]
     ncodes = bt_ref.shape[2]
     tile = tokens // 2
     causal = lax.broadcasted_iota(jnp.int32, (tile, tile), 0) >= lax.broadcasted_iota(jnp.int32, (tile, tile), 1)
     for k in range(lay.heads):
-        onehot = one_hot(codes_ref[lay.first + k : lay.first + k + 1, :], ncodes)
-        keys = dot(bt_ref[k], onehot).astype(BF16)
+        h = lay.first + k
+        onehot = one_hot(codes_ref[h : h + 1, :], ncodes)
+        keys = dot(bt_ref[h], onehot).astype(BF16)
         for r in range(2):
             rows = slice(r * tile, (r + 1) * tile)
             upto = slice(0, (r + 1) * tile)
-            score = dot(qt_ref[k, rows, :], keys[:, upto])
+            score = dot(qt_ref[h, rows, :], keys[:, upto])
             last = jnp.where(causal, score[:, r * tile :], NEVER)
             score = jnp.concatenate([score[:, :tile], last], axis=1) if r else last
             top = jnp.max(functools.reduce(jnp.maximum, lane_tiles(score)), axis=1, keepdims=True)
@@ -152,32 +160,22 @@
             weight = jnp.exp2((score - top) * factor)
             den = jnp.sum(sum(lane_tiles(weight)), axis=1, keepdims=True)
             den_ref[k, rows, :] = jnp.broadcast_to(den, (tile, LANES))
-            num_ref[k, rows, :] = dot(weight.astype(BF16), vt_ref[k, upto, :])
-
-
-def part_of(lay, x):
-    first, count = (lay.first, lay.heads)
-    assert first % count == 0
-    return pl.BlockSpec((count,) + x.shape[1:], lambda i: (first // count, 0, 0))
-
-
-def whole(x):
-    return pl.BlockSpec(x.shape, lambda i: (0,) * len(x.shape))
-
-
-def window(lay, codes, qt, vt, bt):
+            num_ref[k, rows, :] = dot(weight.astype(BF16), vt_ref[h, upto, :])
+
+
+def window(lay, after, codes, qt, vt, bt):
     heads, tokens, width = qt.shape
     factor = width ** (-0.5) * math.log2(math.e)
     shape = jax.ShapeDtypeStruct((lay.heads, tokens, width), F32)
     return pl.pallas_call(
         functools.partial(window_kernel, lay, factor),
         out_shape=[shape] * 3,
-        grid=(1,),
-        in_specs=[whole(codes), part_of(lay, qt), part_of(lay, vt), part_of(lay, bt)],
-        out_specs=[whole(shape)] * 3,
+        in_specs=[ANY] + [VMEM] * 4,
+        out_specs=[VMEM] * 3,
+        compiler_params=PARAMS,
         cost_estimate=pl.CostEstimate(flops=2400000000, bytes_accessed=18 * tokens * lay.heads * width, transcendentals=0),
         name="window",
-    )(codes, qt, vt, bt)
+    )(after, codes, qt, vt, bt)
 
 
 def codes_kernel(lay, factor, pos_ref, qt_ref, bt_ref, num_ref, top_ref, den_ref, mine_ref, theirs_ref, out_ref, buf):
@@ -200,7 +198,7 @@
         cache = jnp.concatenate(sums, axis=0)
         for r in range(2):
             rows = slice(r * tile, (r + 1) * tile)
-            scores = lane_tiles(dot(qt_ref[k, rows, :], bt_ref[k]))
+            scores = lane_tiles(dot(qt_ref[lay.first + k, rows, :], bt_ref[lay.first + k]))
             scores = [s + jnp.where(n > 0.5, 0.0, NEVER) for s, n in zip(scores, counts)]
             early = top_ref[k, rows, :]
             top = jnp.maximum(early, jnp.max(functools.reduce(jnp.maximum, scores), axis=1, keepdims=True))
@@ -220,42 +218,47 @@
     return pl.pallas_call(
         functools.partial(codes_kernel, lay, factor),
         out_shape=out,
-        grid=(1,),
-        in_specs=[SMEM, part_of(lay, qt), part_of(lay, bt)] + [whole(x) for x in (num, top, den, mine, theirs)],
-        out_specs=whole(out),
+        in_specs=[SMEM] + [VMEM] * 7,
+        out_specs=VMEM,
         scratch_shapes=[pltpu.VMEM((2, 2, lay.rows, LANES), BF16)],
+        compiler_params=PARAMS,
         cost_estimate=pl.CostEstimate(flops=2000000000, bytes_accessed=14 * tokens * lay.heads * width, transcendentals=0),
         name="attend",
     )(pos, qt, bt, num, top, den, mine, theirs)
 
 
-def mix_kernel(spans, *refs):
-    n = len(spans)
-    parts, weights, out_ref = (refs[:n], refs[n : 2 * n], refs[-1])
-    base = refs[2 * n] if len(refs) == 2 * n + 2 else None
+def mix_kernel(terms, parts, extra, *refs):
+    weights, out_ref = (refs[parts:-1], refs[-1])
     tokens, columns = out_ref.shape
     wide = min(columns, 256)
     tile = tokens // 2
     for r in range(0, tokens, tile):
         for c in range(0, columns, wide):
-            total = sum(dot(p[r : r + tile, :], w[a:b, c : c + wide]) for p, w, (a, b) in zip(parts, weights, spans))
-            if base is not None:
-                total = total + base[r : r + tile, c : c + wide]
+            total = sum(
+                dot(refs[n][r : r + tile, :], weights[w][a:b, c : c + wide]) for n, (w, a, b) in enumerate(terms)
+            )
+            if extra:
+                total = total + refs[-2][r : r + tile, c : c + wide]
             out_ref[r : r + tile, c : c + wide] = total.astype(out_ref.dtype)
 
 
-def mix(terms, base, dtype):
-    parts, weights, spans = zip(*terms)
+def mix(terms, weights, base, dtype):
+    parts = [term[0] for term in terms]
+    used = sorted({term[1] for term in terms})
+    spans = [(used.index(w), a, b) for _, w, a, b in terms]
     tokens, columns = (parts[0].shape[0], weights[0].shape[1])
     extra = [] if base is None else [base]
     return pl.pallas_call(
-        functools.partial(mix_kernel, spans),
+        functools.partial(mix_kernel, spans, len(parts), len(extra)),
         out_shape=jax.ShapeDtypeStruct((tokens, columns), dtype),
-        in_specs=[VMEM] * (2 * len(terms) + len(extra)),
+        in_specs=[VMEM] * (len(parts) + len(used) + len(extra)),
         out_specs=VMEM,
-        cost_estimate=pl.CostEstimate(flops=2 * tokens * columns * sum(p.shape[1] for p in parts), bytes_accessed=8 * tokens * columns, transcendentals=0),
+        compiler_params=PARAMS,
+        cost_estimate=pl.CostEstimate(
+            flops=2 * tokens * columns * sum(p.shape[1] for p in parts), bytes_accessed=8 * tokens * columns, transcendentals=0
+        ),
         name="mix",
-    )(*parts, *weights, *extra)
+    )(*parts, *[weights[w] for w in used], *extra)
 
 
 def swap(x, axis, k):
@@ -266,25 +269,49 @@
     return (a.astype(F32) + b.astype(F32)).astype(BF16)
 
 
-def prefix(keep, give, here):
-    upper = lambda bit: (here & bit) != 0
-    got1 = swap(give, "ctx", 1)
-    mine, send = (add(keep[0], got1[0]), add(keep[1], got1[1]))
-    got2 = swap(send, "ctx", 2)
-    total = add(mine, got2)
-    before = jnp.zeros_like(total)
-    bit = 4
-    while bit < lax.axis_size("ctx"):
-        got = swap(total, "ctx", bit)
-        before = jnp.where(upper(bit), add(before, got), before)
-        total = add(total, got)
-        bit *= 2
-    with_low = add(before, jnp.where(upper(2), got2, mine))
-    got = swap(jnp.where(upper(2), before, with_low), "ctx", 2)
-    before = jnp.stack([jnp.where(upper(2), with_low, before), got])
-    with_low = add(before, jnp.where(upper(1), got1, keep))
-    got = swap(jnp.where(upper(1), before, with_low), "ctx", 1)
-    return jnp.where(upper(1), with_low, before), got
+class Prefix:
+    def __init__(self, keep, give, here):
+        self.keep, self.here = (keep, here)
+        self.got1 = swap(give, "ctx", 1)
+
+    def upper(self, bit):
+        return (self.here & bit) != 0
+
+    def reduce(self):
+        keep, got1 = (self.keep, self.got1)
+        self.mine, send = (add(keep[0], got1[0]), add(keep[1], got1[1]))
+        self.got2 = swap(send, "ctx", 2)
+        return send
+
+    def start(self):
+        self.total = add(self.mine, self.got2)
+        self.before = jnp.zeros_like(self.total)
+
+    def step(self, bit):
+        sent = self.total
+        got = swap(sent, "ctx", bit)
+        self.before = jnp.where(self.upper(bit), add(self.before, got), self.before)
+        self.total = add(self.total, got)
+        return sent
+
+    def spread(self):
+        before, got2 = (self.before, self.got2)
+        with_low = add(before, jnp.where(self.upper(2), got2, self.mine))
+        got = swap(jnp.where(self.upper(2), before, with_low), "ctx", 2)
+        self.before = jnp.stack([jnp.where(self.upper(2), with_low, before), got])
+
+    def finish(self):
+        before, got1 = (self.before, self.got1)
+        with_low = add(before, jnp.where(self.upper(1), got1, self.keep))
+        got = swap(jnp.where(self.upper(1), before, with_low), "ctx", 1)
+        return jnp.where(self.upper(1), with_low, before), got
+
+
+def group_sizes(heads):
+    total = sum(SIZES)
+    ends = [max(n + 1, heads * sum(SIZES[: n + 1]) // total) for n in range(len(SIZES))]
+    ends = sorted({min(end, heads) for end in ends})
+    return [b - a for a, b in zip([0] + ends, ends)]
 
 
 def on_device(queries, values, codes, codebook, out_weight):
@@ -296,9 +323,16 @@
     sides = lax.axis_size("head")
     core, row = (here & 1, here >> 1 & 1)
     pos = jnp.stack([core, row]).astype(jnp.int32)
-    count = heads // math.gcd(GROUPS, heads)
-    lays = [Layout(devices, first, count, codebook.shape[1]) for first in range(0, heads, count)]
+    lays, first = ([], 0)
+    for count in group_sizes(heads):
+        lays.append(Layout(devices, first, count, codebook.shape[1]))
+        first += count
     codes = codes.T
+
+    vt, pieces = block_sums(lays[:1], True, pos, codes, values)
+    runs = [Prefix(*pieces[0], here)]
+    if lays[1:]:
+        runs += [Prefix(*piece, here) for piece in block_sums(lays[1:], False, pos, codes, vt)[1]]
 
     rows, columns = (out_weight.shape[0], out_weight.shape[1] // sides)
     half = rows // 2
@@ -310,21 +344,27 @@
         first = core == 0
         weights[k] = jnp.stack([jnp.where(first, mine, other), jnp.where(first, other, mine)]).reshape(rows, columns)
 
-    vt, pieces = block_sums(lays[:1], True, pos, codes, values)
-    if lays[1:]:
-        pieces += block_sums(lays[1:], False, pos, codes, vt)[1]
-    qt, bt = turn_inputs(queries, codebook)
-    wide = count * width
+    sent = [run.reduce() for run in runs]
+    qt, bt = turn_inputs(sent[-1], queries, codebook)
+    for run in runs:
+        run.start()
+    bit = 4
+    while bit < devices:
+        sent = [run.step(bit) for run in runs]
+        bit *= 2
+    windows = [window(lay, sent[0], codes, qt, vt, bt) for lay in lays]
+    for run in runs:
+        run.spread()
     terms = []
-    for g, (lay, (keep, give)) in enumerate(zip(lays, pieces)):
-        num, top, den = window(lay, codes, qt, vt, bt)
-        mine, theirs = prefix(keep, give, here)
+    for lay, run, (num, top, den) in zip(lays, runs, windows):
+        mine, theirs = run.finish()
         attended = attend(lay, pos, qt, bt, num, top, den, mine, theirs)
-        span = (g * wide, (g + 1) * wide)
-        terms.append((attended, weights[0], span))
-        terms += [(swap(attended, "head", k), weights[k], span) for k in range(1, sides)]
+        span = (lay.first * width, (lay.first + lay.heads) * width)
+        terms.append((attended, 0, *span))
+        terms += [(swap(attended, "head", k), k, *span) for k in range(1, sides)]
     late = len(terms) - (sides - 1)
-    return mix(terms[late:], mix(terms[:late], None, F32), BF16)
+    base = mix(terms[:late], weights, None, F32)
+    return mix(terms[late:], weights, base, BF16)
 
 
 def solution(mesh):

time: 106 us -> 84.2 us (0.79)
  Pallas kernels: 53.1 us -> 21.7 us
  waiting for transfers between devices: 7.96 us -> 20.6 us
  local copies, waits for them, and re-layouts: 8.49 us -> 6.13 us
  starting transfers between devices: 29.8 us -> 28.4 us
    ppermute x30, waiting for transfers between devices: 7.96 us -> 20.6 us  [swap(): lax.ppermute(x, axis, [(i, i ^ k) for i in range(lax.axis_size(axis))])]
    pallas_call x2, Pallas kernels: 13.4 us -> 3.53 us  [mix(): pl.pallas_call(functools.partial(mix_kernel, spans, len(parts), len(extra...]
    pallas_call x4, Pallas kernels: 15.6 us -> 6.91 us  [window(): pl.pallas_call(functools.partial(window_kernel, lay, factor), out_shape=[...]
    pallas_call x4, Pallas kernels: 14.9 us -> 7.85 us  [attend(): pl.pallas_call(functools.partial(codes_kernel, lay, factor), out_shape=ou...]
    convert_element_type x12, other arithmetic: 0.3 us -> 3.84 us  [add(): return (a.astype(F32) + b.astype(F32)).astype(BF16)]
    pallas_call x2, Pallas kernels: 6 us -> 2.87 us  [block_sums(): pl.pallas_call(functools.partial(sums_kernel, lays, turn), out_shape=shap...]
    pallas_call x1, Pallas kernels: 3.25 us -> 0.52 us  [turn_inputs(): pl.pallas_call(turn_kernel, out_shape=[jax.ShapeDtypeStruct((heads, token...]
    select_n x4, other arithmetic: 2.87 us -> 0.23 us  [finish(): got = swap(jnp.where(self.upper(1), before, with_low), 'ctx', 1)]
  transfers between devices with their start and end apart: 30 -> 30, of which waited for: 7 -> 8; matrix products, arithmetic and copies ran while one was open for 9% -> 13% of each run, Pallas kernels for 41% -> 21%
where the time goes in v3:
time: 84.2 us; the launch traced here: 83.6 us
  starting transfers between devices  28.4 us (34%)
  Pallas kernels  21.7 us (26%)
  waiting for transfers between devices  20.6 us (24%)
  other arithmetic  6.55 us (8%)
  local copies, waits for them, and re-layouts  6.13 us (7%)
    ppermute x30, starting transfers between devices, swap(): lax.ppermute(x, axis, [(i, i ^ k) for i in range(lax.axis_size(axis))])  28.4 us
    ppermute x30, waiting for transfers between devices, swap(): lax.ppermute(x, axis, [(i, i ^ k) for i in range(lax.axis_size(axis))])  20.6 us
    pallas_call x4, Pallas kernels, attend(): pl.pallas_call(functools.partial(codes_kernel, lay, factor), out_shape=ou...  7.85 us
    pallas_call x4, Pallas kernels, window(): pl.pallas_call(functools.partial(window_kernel, lay, factor), out_shape=[...  6.91 us
    convert_element_type x12, other arithmetic, add(): return (a.astype(F32) + b.astype(F32)).astype(BF16)  3.84 us
    pallas_call x2, Pallas kernels, mix(): pl.pallas_call(functools.partial(mix_kernel, spans, len(parts), len(extra...  3.53 us
    pallas_call x2, Pallas kernels, block_sums(): pl.pallas_call(functools.partial(sums_kernel, lays, turn), out_shape=shap...  2.87 us
    dynamic_slice x1, local copies, waits for them, and re-layouts, on_device(): lax.dynamic_slice(out_weight, (core * half, (side ^ k) * columns), (half,...  2.26 us
  transfers between devices with their start and end apart: 30, of which 8 were waited for; matrix products, arithmetic and copies ran while one was open for 13% of the time, Pallas kernels for 21%

profile of v3, /device:TPU:0, one launch (start us, length us, event | category | flops | bytes accessed | tf_op | source)
XLA Modules:
  0.0 83.6 jit_solution(1082390092539504329)
XLA Ops:
  0.1 1.2 %copy-done = bf16[512,8,128]{2,1,0:T(8,128)(2,1)S(1)} copy-done((bf16[512,8,128]{2,1,0:T(8,128)(2,1)S(1)}, bf16[512,8,128]{2,1,0:T(8,128)(2,1)}, u32[]{:S(2)}) %copy-start) | copy-done | bytes 1048600
  3.2 1.7 %block_sums.3 = (bf16[2,272,128]{2,1,0:T(8,128)(2,1)S(1)}, bf16[2,272,128]{2,1,0:T(8,128)(2,1)S(1)}, bf16[2,272,128]{2,1,0:T(8,128)(2,1)S(1)}, bf16[2,272,128]{2...) custom-call(s32[2]{0:T(128)S(1)} %pad_add_fusion.pos_ref, ...), custom_call_target="tpu_custom_call" | custom-call | flops 1610612736 | bytes 2097152 | tf_op jit(solution)/shard_map/block_sums/pallas_call | solution.py:98
  6.1 2.3 %dynamic_slice.6 = bf16[512,1024]{1,0:T(8,128)(2,1)} dynamic-slice(bf16[1024,2048]{1,0:T(8,128)(2,1)} %param.9, s32[]{:T(128)S(6)} %select_n.174, s32[]{:T(128)S(6)} %select_n.175), dynamic_slice_sizes={512,1024} | dynamic-slice | bytes 2097156 | tf_op jit(solution)/shard_map/dynamic_slice | solution.py:341
  8.3 2.9 %collective-permute-start.10 = (bf16[512,1024]{1,0:T(8,128)(2,1)}, bf16[512,1024]{1,0:T(8,128)(2,1)S(1)}, u32[]{:S(2)}, u32[]{:S(2)}) collective-permute-start(bf16[512,1024]{1,0:T(8,128)(2,1)} %dynamic_slice.6), channel_id=1, source_target_pairs={{0,1},{1,0},{2,3},{3,2},{4,5},{5,4},{6,7},{7,6},{8,9},{9,8},{10,11... | collective-permute-start | bytes 3145736 | tf_op jit(solution)/shard_map/ppermute | solution.py:265
  11.2 1.9 %constant_dynamic-slice_fusion.refs_7_ = bf16[1024,1024]{1,0:T(8,128)(2,1)S(1)} fusion(bf16[1024,2048]{1,0:T(8,128)(2,1)} %param.9, s32[]{:T(128)S(6)} %select_n.202), kind=kLoop, calls=%fused_computation.76 | loop fusion | bytes 4194308 | tf_op jit(solution)/shard_map/dynamic_slice | solution.py:339
  14.1 1.6 %collective-permute-start.24 = (bf16[272,128]{1,0:T(8,128)(2,1)S(1)}, bf16[272,128]{1,0:T(8,128)(2,1)S(1)}, u32[]{:S(2)}, u32[]{:S(2)}) collective-permute-start(bf16[272,128]{1,0:T(8,128)(2,1)S(1)} %fusion.31), channel_id=1, source_target_pairs={{0,4},{2,6},{4,0},{6,2},{8,12},{10,14},{12,8},{14,10},{16,20},{18,... | collective-permute-start | bytes 208904 | tf_op jit(solution)/shard_map/ppermute | solution.py:265
  17.2 1.6 %collective-permute-start.17 = (bf16[272,128]{1,0:T(8,128)(2,1)S(1)}, bf16[272,128]{1,0:T(8,128)(2,1)S(1)}, u32[]{:S(2)}, u32[]{:S(2)}) collective-permute-start(bf16[272,128]{1,0:T(8,128)(2,1)S(1)} %fusion.29), channel_id=1, source_target_pairs={{0,4},{2,6},{4,0},{6,2},{8,12},{10,14},{12,8},{14,10},{16,20},{18,... | collective-permute-start | bytes 208904 | tf_op jit(solution)/shard_map/ppermute | solution.py:265
  20.8 1.6 %collective-permute-start.25 = (bf16[272,128]{1,0:T(8,128)(2,1)S(1)}, bf16[272,128]{1,0:T(8,128)(2,1)S(1)}, u32[]{:S(2)}, u32[]{:S(2)}) collective-permute-start(bf16[272,128]{1,0:T(8,128)(2,1)S(1)} %add_convert_fusion.7), channel_id=1, source_target_pairs={{0,8},{2,10},{4,12},{6,14},{8,0},{10,2},{12,4},{14,6},{16,24},{18,... | collective-permute-start | bytes 208904 | tf_op jit(solution)/shard_map/ppermute | solution.py:265
  23.9 1.6 %collective-permute-start.18 = (bf16[272,128]{1,0:T(8,128)(2,1)S(1)}, bf16[272,128]{1,0:T(8,128)(2,1)S(1)}, u32[]{:S(2)}, u32[]{:S(2)}) collective-permute-start(bf16[272,128]{1,0:T(8,128)(2,1)S(1)} %add_convert_fusion.13), channel_id=1, source_target_pairs={{0,8},{2,10},{4,12},{6,14},{8,0},{10,2},{12,4},{14,6},{16,24},{18,... | collective-permute-start | bytes 208904 | tf_op jit(solution)/shard_map/ppermute | solution.py:265
  26.1 1.5 %collective-permute-done.3 = bf16[272,128]{1,0:T(8,128)(2,1)S(1)} collective-permute-done((bf16[272,128]{1,0:T(8,128)(2,1)S(1)}, bf16[272,128]{1,0:T(8,128)(2,1)S(1)}, u32[]{:S(2)}, u32[]{:S(2)}) %collective-permute-start.3) | collective-permute-done | bytes 69664 | tf_op jit(solution)/shard_map/ppermute | solution.py:265
  27.6 1.7 %window.7 = (f32[2,512,128]{2,1,0:T(8,128)S(1)}, f32[2,512,128]{2,1,0:T(8,128)S(1)}, f32[2,512,128]{2,1,0:T(8,128)S(1)}) custom-call(bf16[272,128]{1,0:T(8,128)(2,1)S(1)} %add_convert_fusion.23.after_ref, s32[8,512]{1,0:T(8,128)S(1)} %bitcast.64, bf16[8,512,128]{2,1,0:T(8,128)(2,1)S(1)} %get-tuple-element.31.qt_ref, ...), custom_call_target="tpu_custom_call" | custom-call | flops 2400000000 | bytes 2359296 | tf_op jit(solution)/shard_map/window/pallas_call | solution.py:170
  29.4 1.7 %window.6 = (f32[2,512,128]{2,1,0:T(8,128)S(1)}, f32[2,512,128]{2,1,0:T(8,128)S(1)}, f32[2,512,128]{2,1,0:T(8,128)S(1)}) custom-call(bf16[272,128]{1,0:T(8,128)(2,1)S(1)} %add_convert_fusion.23.after_ref, s32[8,512]{1,0:T(8,128)S(1)} %bitcast.65, bf16[8,512,128]{2,1,0:T(8,128)(2,1)S(1)} %get-tuple-element.31.qt_ref, ...), custom_call_target="tpu_custom_call" | custom-call | flops 2400000000 | bytes 2359296 | tf_op jit(solution)/shard_map/window/pallas_call | solution.py:170
  31.1 2.7 %collective-permute-start.12 = (bf16[272,128]{1,0:T(8,128)(2,1)S(1)}, bf16[272,128]{1,0:T(8,128)(2,1)S(1)}, u32[]{:S(2)}, u32[]{:S(2)}) collective-permute-start(bf16[272,128]{1,0:T(8,128)(2,1)S(1)} %add_convert_fusion.23.after_ref), channel_id=1, source_target_pairs={{0,16},{2,18},{4,20},{6,22},{8,24},{10,26},{12,28},{14,30},{16,0},... | collective-permute-start | bytes 208904 | tf_op jit(solution)/shard_map/ppermute | solution.py:265
  33.8 1.7 %window.5 = (f32[2,512,128]{2,1,0:T(8,128)S(1)}, f32[2,512,128]{2,1,0:T(8,128)S(1)}, f32[2,512,128]{2,1,0:T(8,128)S(1)}) custom-call(bf16[272,128]{1,0:T(8,128)(2,1)S(1)} %add_convert_fusion.23.after_ref, s32[8,512]{1,0:T(8,128)S(1)} %bitcast.66, bf16[8,512,128]{2,1,0:T(8,128)(2,1)S(1)} %get-tuple-element.31.qt_ref, ...), custom_call_target="tpu_custom_call" | custom-call | flops 2400000000 | bytes 2359296 | tf_op jit(solution)/shard_map/window/pallas_call | solution.py:170
  35.5 1.7 %window.4 = (f32[2,512,128]{2,1,0:T(8,128)S(1)}, f32[2,512,128]{2,1,0:T(8,128)S(1)}, f32[2,512,128]{2,1,0:T(8,128)S(1)}) custom-call(bf16[272,128]{1,0:T(8,128)(2,1)S(1)} %add_convert_fusion.23.after_ref, s32[8,512]{1,0:T(8,128)S(1)} %bitcast.67, bf16[8,512,128]{2,1,0:T(8,128)(2,1)S(1)} %get-tuple-element.31.qt_ref, ...), custom_call_target="tpu_custom_call" | custom-call | flops 2400000000 | bytes 2359296 | tf_op jit(solution)/shard_map/window/pallas_call | solution.py:170
  37.7 2.7 %collective-permute-start.19 = (bf16[272,128]{1,0:T(8,128)(2,1)S(1)}, bf16[272,128]{1,0:T(8,128)(2,1)S(1)}, u32[]{:S(2)}, u32[]{:S(2)}) collective-permute-start(bf16[272,128]{1,0:T(8,128)(2,1)S(1)} %add_convert_fusion.12), channel_id=1, source_target_pairs={{0,16},{2,18},{4,20},{6,22},{8,24},{10,26},{12,28},{14,30},{16,0},... | collective-permute-start | bytes 208904 | tf_op jit(solution)/shard_map/ppermute | solution.py:265
  40.8 3.3 %collective-permute-done.26 = bf16[272,128]{1,0:T(8,128)(2,1)S(1)} collective-permute-done((bf16[272,128]{1,0:T(8,128)(2,1)S(1)}, bf16[272,128]{1,0:T(8,128)(2,1)S(1)}, u32[]{:S(2)}, u32[]{:S(2)}) %collective-permute-start.26) | collective-permute-done | bytes 69664 | tf_op jit(solution)/shard_map/ppermute | solution.py:265
  45.1 1.6 %collective-permute-start.27 = (bf16[272,128]{1,0:T(8,128)(2,1)S(1)}, bf16[272,128]{1,0:T(8,128)(2,1)S(1)}, u32[]{:S(2)}, u32[]{:S(2)}) collective-permute-start(bf16[272,128]{1,0:T(8,128)(2,1)S(1)} %get-tuple-element.54), channel_id=1, source_target_pairs={{0,4},{2,6},{4,0},{6,2},{8,12},{10,14},{12,8},{14,10},{16,20},{18,... | collective-permute-start | bytes 208904 | tf_op jit(solution)/shard_map/ppermute | solution.py:265
  48.3 1.6 %collective-permute-start.13 = (bf16[272,128]{1,0:T(8,128)(2,1)S(1)}, bf16[272,128]{1,0:T(8,128)(2,1)S(1)}, u32[]{:S(2)}, u32[]{:S(2)}) collective-permute-start(bf16[272,128]{1,0:T(8,128)(2,1)S(1)} %get-tuple-element.58), channel_id=1, source_target_pairs={{0,4},{2,6},{4,0},{6,2},{8,12},{10,14},{12,8},{14,10},{16,20},{18,... | collective-permute-start | bytes 208904 | tf_op jit(solution)/shard_map/ppermute | solution.py:265
  50.6 1.3 %collective-permute-done.20 = bf16[272,128]{1,0:T(8,128)(2,1)S(1)} collective-permute-done((bf16[272,128]{1,0:T(8,128)(2,1)S(1)}, bf16[272,128]{1,0:T(8,128)(2,1)S(1)}, u32[]{:S(2)}, u32[]{:S(2)}) %collective-permute-start.20) | collective-permute-done | bytes 69664 | tf_op jit(solution)/shard_map/ppermute | solution.py:265
  52.9 1.4 %collective-permute-done.7 = bf16[272,128]{1,0:T(8,128)(2,1)S(1)} collective-permute-done((bf16[272,128]{1,0:T(8,128)(2,1)S(1)}, bf16[272,128]{1,0:T(8,128)(2,1)S(1)}, u32[]{:S(2)}, u32[]{:S(2)}) %collective-permute-start.7) | collective-permute-done | bytes 69664 | tf_op jit(solution)/shard_map/ppermute | solution.py:265
  54.4 2.0 %attend.7.refs_4_ = bf16[512,256]{1,0:T(8,128)(2,1)S(1)} custom-call(s32[2]{0:T(128)S(1)} %pad_add_fusion.pos_ref, bf16[8,512,128]{2,1,0:T(8,128)(2,1)S(1)} %get-tuple-element.31.qt_ref, bf16[8,128,512]{2,1,0:T(8,128)(2,1)S(1)} %get-tuple-element.32.bt_ref, f32[2,512,128]{2,1,0:T(8,128)S(1)} %get-tuple-element.46.num_ref, ...), custom_call_target="tpu_custom_call" | custom-call | flops 2000000000 | bytes 1835008 | tf_op jit(solution)/shard_map/attend/pallas_call | solution.py:218
  57.2 2.0 %attend.6.refs_2_ = bf16[512,256]{1,0:T(8,128)(2,1)S(1)} custom-call(s32[2]{0:T(128)S(1)} %pad_add_fusion.pos_ref, bf16[8,512,128]{2,1,0:T(8,128)(2,1)S(1)} %get-tuple-element.31.qt_ref, bf16[8,128,512]{2,1,0:T(8,128)(2,1)S(1)} %get-tuple-element.32.bt_ref, f32[2,512,128]{2,1,0:T(8,128)S(1)} %get-tuple-element.41.num_ref, ...), custom_call_target="tpu_custom_call" | custom-call | flops 2000000000 | bytes 1835008 | tf_op jit(solution)/shard_map/attend/pallas_call | solution.py:218
  59.2 1.6 %collective-permute-start.22 = (bf16[512,256]{1,0:T(8,128)(2,1)S(1)}, bf16[512,256]{1,0:T(8,128)(2,1)S(1)}, u32[]{:S(2)}, u32[]{:S(2)}) collective-permute-start(bf16[512,256]{1,0:T(8,128)(2,1)S(1)} %attend.6.refs_2_), channel_id=1, source_target_pairs={{0,1},{1,0},{2,3},{3,2},{4,5},{5,4},{6,7},{7,6},{8,9},{9,8},{10,11... | collective-permute-start | bytes 786440 | tf_op jit(solution)/shard_map/ppermute | solution.py:265
  60.7 2.0 %attend.5.refs_0_ = bf16[512,256]{1,0:T(8,128)(2,1)S(1)} custom-call(s32[2]{0:T(128)S(1)} %pad_add_fusion.pos_ref, bf16[8,512,128]{2,1,0:T(8,128)(2,1)S(1)} %get-tuple-element.31.qt_ref, bf16[8,128,512]{2,1,0:T(8,128)(2,1)S(1)} %get-tuple-element.32.bt_ref, f32[2,512,128]{2,1,0:T(8,128)S(1)} %get-tuple-element.38.num_ref, ...), custom_call_target="tpu_custom_call" | custom-call | flops 2000000000 | bytes 1835008 | tf_op jit(solution)/shard_map/attend/pallas_call | solution.py:218
  63.3 1.9 %attend.4.refs_6_ = bf16[512,256]{1,0:T(8,128)(2,1)S(1)} custom-call(s32[2]{0:T(128)S(1)} %pad_add_fusion.pos_ref, bf16[8,512,128]{2,1,0:T(8,128)(2,1)S(1)} %get-tuple-element.31.qt_ref, bf16[8,128,512]{2,1,0:T(8,128)(2,1)S(1)} %get-tuple-element.32.bt_ref, f32[2,512,128]{2,1,0:T(8,128)S(1)} %get-tuple-element.35.num_ref, ...), custom_call_target="tpu_custom_call" | custom-call | flops 2000000000 | bytes 1835008 | tf_op jit(solution)/shard_map/attend/pallas_call | solution.py:218
  65.3 1.6 %collective-permute-start.9 = (bf16[512,256]{1,0:T(8,128)(2,1)S(1)}, bf16[512,256]{1,0:T(8,128)(2,1)S(1)}, u32[]{:S(2)}, u32[]{:S(2)}) collective-permute-start(bf16[512,256]{1,0:T(8,128)(2,1)S(1)} %attend.4.refs_6_), channel_id=1, source_target_pairs={{0,1},{1,0},{2,3},{3,2},{4,5},{5,4},{6,7},{7,6},{8,9},{9,8},{10,11... | collective-permute-start | bytes 786440 | tf_op jit(solution)/shard_map/ppermute | solution.py:265
  67.2 4.3 %collective-permute-done.22.refs_3_ = bf16[512,256]{1,0:T(8,128)(2,1)S(1)} collective-permute-done((bf16[512,256]{1,0:T(8,128)(2,1)S(1)}, bf16[512,256]{1,0:T(8,128)(2,1)S(1)}, u32[]{:S(2)}, u32[]{:S(2)}) %collective-permute-start.22) | collective-permute-done | bytes 262176 | tf_op jit(solution)/shard_map/ppermute | solution.py:265
  71.5 5.6 %collective-permute-done.15.refs_1_ = bf16[512,256]{1,0:T(8,128)(2,1)S(1)} collective-permute-done((bf16[512,256]{1,0:T(8,128)(2,1)S(1)}, bf16[512,256]{1,0:T(8,128)(2,1)S(1)}, u32[]{:S(2)}, u32[]{:S(2)}) %collective-permute-start.15) | collective-permute-done | bytes 262176 | tf_op jit(solution)/shard_map/ppermute | solution.py:265
  77.1 2.1 %mix.2.refs_2_ = f32[512,1024]{1,0:T(8,128)S(1)} custom-call(bf16[512,256]{1,0:T(8,128)(2,1)S(1)} %attend.5.refs_0_, bf16[512,256]{1,0:T(8,128)(2,1)S(1)} %collective-permute-done.15.refs_1_, bf16[512,256]{1,0:T(8,128)(2,1)S(1)} %attend.6.refs_2_, bf16[512,256]{1,0:T(8,128)(2,1)S(1)} %collective-permute-done.22.refs_3_, bf16[512,256]{1,0:T(8,128)(2,1)S(1)} %attend.7.refs_4_, ...), custom_call_target="tpu_custom_call" | custom-call | flops 1879048192 | bytes 4194304 | tf_op jit(solution)/shard_map/mix/pallas_call | solution.py:251
  79.2 3.0 %collective-permute-done.9.refs_0_ = bf16[512,256]{1,0:T(8,128)(2,1)S(1)} collective-permute-done((bf16[512,256]{1,0:T(8,128)(2,1)S(1)}, bf16[512,256]{1,0:T(8,128)(2,1)S(1)}, u32[]{:S(2)}, u32[]{:S(2)}) %collective-permute-start.9) | collective-permute-done | bytes 262176 | tf_op jit(solution)/shard_map/ppermute | solution.py:265
  82.2 1.4 %mix.3 = bf16[512,1024]{1,0:T(8,128)(2,1)} custom-call(bf16[512,256]{1,0:T(8,128)(2,1)S(1)} %collective-permute-done.9.refs_0_, bf16[1024,1024]{1,0:T(8,128)(2,1)S(1)} %bitcast.61, f32[512,1024]{1,0:T(8,128)S(1)} %mix.2.refs_2_), custom_call_target="tpu_custom_call" | custom-call | flops 268435456 | bytes 4194304 | tf_op jit(solution)/shard_map/mix/pallas_call | solution.py:251
  (76 shorter events, 16.6 us)
Async XLA Ops:
  4.9 8.2 %collective-permute-start.23 = (bf16[2,272,128]{2,1,0:T(8,128)(2,1)S(1)}, bf16[2,272,128]{2,1,0:T(8,128)(2,1)}, u32[]{:S(2)}, u32[]{:S(2)}) collective-permute-start(bf16[2,272,128]{2,1,0:T(8,128)(2,1)S(1)} %get-tuple-element.50), channel_id=1, source_target_pairs={{0,2},{2,0},{4,6},{6,4},{8,10},{10,8},{12,14},{14,12},{16,18},{18,... | collective-permute-start | bytes 417800 | tf_op jit(solution)/shard_map/ppermute | solution.py:265
  5.5 10.2 %collective-permute-start.1 = (bf16[2,272,128]{2,1,0:T(8,128)(2,1)S(1)}, bf16[2,272,128]{2,1,0:T(8,128)(2,1)S(1)}, u32[]{:S(2)}, u32[]{:S(2)}) collective-permute-start(bf16[2,272,128]{2,1,0:T(8,128)(2,1)S(1)} %get-tuple-element.34), channel_id=1, source_target_pairs={{0,2},{2,0},{4,6},{6,4},{8,10},{10,8},{12,14},{14,12},{16,18},{18,... | collective-permute-start | bytes 417800 | tf_op jit(solution)/shard_map/ppermute | solution.py:265
  5.5 13.2 %collective-permute-start = (bf16[2,272,128]{2,1,0:T(8,128)(2,1)S(1)}, bf16[2,272,128]{2,1,0:T(8,128)(2,1)S(1)}, u32[]{:S(2)}, u32[]{:S(2)}) collective-permute-start(bf16[2,272,128]{2,1,0:T(8,128)(2,1)S(1)} %get-tuple-element.30), channel_id=1, source_target_pairs={{0,2},{2,0},{4,6},{6,4},{8,10},{10,8},{12,14},{14,12},{16,18},{18,... | collective-permute-start | bytes 417800 | tf_op jit(solution)/shard_map/ppermute | solution.py:265
  6.0 10.3 %collective-permute-start.16 = (bf16[2,272,128]{2,1,0:T(8,128)(2,1)S(1)}, bf16[2,272,128]{2,1,0:T(8,128)(2,1)}, u32[]{:S(2)}, u32[]{:S(2)}) collective-permute-start(bf16[2,272,128]{2,1,0:T(8,128)(2,1)S(1)} %get-tuple-element.45), channel_id=1, source_target_pairs={{0,2},{2,0},{4,6},{6,4},{8,10},{10,8},{12,14},{14,12},{16,18},{18,... | collective-permute-start | bytes 417800 | tf_op jit(solution)/shard_map/ppermute | solution.py:265
  8.3 43.9 %collective-permute-start.10 = (bf16[512,1024]{1,0:T(8,128)(2,1)}, bf16[512,1024]{1,0:T(8,128)(2,1)S(1)}, u32[]{:S(2)}, u32[]{:S(2)}) collective-permute-start(bf16[512,1024]{1,0:T(8,128)(2,1)} %dynamic_slice.6), channel_id=1, source_target_pairs={{0,1},{1,0},{2,3},{3,2},{4,5},{5,4},{6,7},{7,6},{8,9},{9,8},{10,11... | collective-permute-start | bytes 3145736 | tf_op jit(solution)/shard_map/ppermute | solution.py:265
  11.2 8.1 %copy-start.2 = (bf16[8,512,128]{2,1,0:T(8,128)(2,1)S(1)}, bf16[8,512,128]{2,1,0:T(8,128)(2,1)}, u32[]{:S(2)}) copy-start(bf16[8,512,128]{2,1,0:T(8,128)(2,1)} %book_ref.1) | copy-start | bytes 3145732
  14.1 5.8 %collective-permute-start.24 = (bf16[272,128]{1,0:T(8,128)(2,1)S(1)}, bf16[272,128]{1,0:T(8,128)(2,1)S(1)}, u32[]{:S(2)}, u32[]{:S(2)}) collective-permute-start(bf16[272,128]{1,0:T(8,128)(2,1)S(1)} %fusion.31), channel_id=1, source_target_pairs={{0,4},{2,6},{4,0},{6,2},{8,12},{10,14},{12,8},{14,10},{16,20},{18,... | collective-permute-start | bytes 208904 | tf_op jit(solution)/shard_map/ppermute | solution.py:265
  15.7 6.8 %collective-permute-start.2 = (bf16[272,128]{1,0:T(8,128)(2,1)S(1)}, bf16[272,128]{1,0:T(8,128)(2,1)S(1)}, u32[]{:S(2)}, u32[]{:S(2)}) collective-permute-start(bf16[272,128]{1,0:T(8,128)(2,1)S(1)} %fusion.26), channel_id=1, source_target_pairs={{0,4},{2,6},{4,0},{6,2},{8,12},{10,14},{12,8},{14,10},{16,20},{18,... | collective-permute-start | bytes 208904 | tf_op jit(solution)/shard_map/ppermute | solution.py:265
  17.2 5.9 %collective-permute-start.17 = (bf16[272,128]{1,0:T(8,128)(2,1)S(1)}, bf16[272,128]{1,0:T(8,128)(2,1)S(1)}, u32[]{:S(2)}, u32[]{:S(2)}) collective-permute-start(bf16[272,128]{1,0:T(8,128)(2,1)S(1)} %fusion.29), channel_id=1, source_target_pairs={{0,4},{2,6},{4,0},{6,2},{8,12},{10,14},{12,8},{14,10},{16,20},{18,... | collective-permute-start | bytes 208904 | tf_op jit(solution)/shard_map/ppermute | solution.py:265
  18.8 8.9 %copy-start.4 = (s32[512,8]{0,1:T(8,128)S(1)}, s32[512,8]{0,1:T(8,128)}, u32[]{:S(2)}) copy-start(s32[512,8]{0,1:T(8,128)} %param.7) | copy-start | bytes 49156
  18.8 6.8 %collective-permute-start.4 = (bf16[272,128]{1,0:T(8,128)(2,1)S(1)}, bf16[272,128]{1,0:T(8,128)(2,1)S(1)}, u32[]{:S(2)}, u32[]{:S(2)}) collective-permute-start(bf16[272,128]{1,0:T(8,128)(2,1)S(1)} %fusion.24.after_ref), channel_id=1, source_target_pairs={{0,4},{2,6},{4,0},{6,2},{8,12},{10,14},{12,8},{14,10},{16,20},{18,... | collective-permute-start | bytes 208904 | tf_op jit(solution)/shard_map/ppermute | solution.py:265
  20.8 14.7 %collective-permute-start.25 = (bf16[272,128]{1,0:T(8,128)(2,1)S(1)}, bf16[272,128]{1,0:T(8,128)(2,1)S(1)}, u32[]{:S(2)}, u32[]{:S(2)}) collective-permute-start(bf16[272,128]{1,0:T(8,128)(2,1)S(1)} %add_convert_fusion.7), channel_id=1, source_target_pairs={{0,8},{2,10},{4,12},{6,14},{8,0},{10,2},{12,4},{14,6},{16,24},{18,... | collective-permute-start | bytes 208904 | tf_op jit(solution)/shard_map/ppermute | solution.py:265
  22.5 5.1 %collective-permute-start.3 = (bf16[272,128]{1,0:T(8,128)(2,1)S(1)}, bf16[272,128]{1,0:T(8,128)(2,1)S(1)}, u32[]{:S(2)}, u32[]{:S(2)}) collective-permute-start(bf16[272,128]{1,0:T(8,128)(2,1)S(1)} %add_convert_fusion.24), channel_id=1, source_target_pairs={{0,8},{2,10},{4,12},{6,14},{8,0},{10,2},{12,4},{14,6},{16,24},{18,... | collective-permute-start | bytes 208904 | tf_op jit(solution)/shard_map/ppermute | solution.py:265
  23.9 13.7 %collective-permute-start.18 = (bf16[272,128]{1,0:T(8,128)(2,1)S(1)}, bf16[272,128]{1,0:T(8,128)(2,1)S(1)}, u32[]{:S(2)}, u32[]{:S(2)}) collective-permute-start(bf16[272,128]{1,0:T(8,128)(2,1)S(1)} %add_convert_fusion.13), channel_id=1, source_target_pairs={{0,8},{2,10},{4,12},{6,14},{8,0},{10,2},{12,4},{14,6},{16,24},{18,... | collective-permute-start | bytes 208904 | tf_op jit(solution)/shard_map/ppermute | solution.py:265
  25.6 14.8 %collective-permute-start.5 = (bf16[272,128]{1,0:T(8,128)(2,1)S(1)}, bf16[272,128]{1,0:T(8,128)(2,1)S(1)}, u32[]{:S(2)}, u32[]{:S(2)}) collective-permute-start(bf16[272,128]{1,0:T(8,128)(2,1)S(1)} %add_convert_fusion.21), channel_id=1, source_target_pairs={{0,8},{2,10},{4,12},{6,14},{8,0},{10,2},{12,4},{14,6},{16,24},{18,... | collective-permute-start | bytes 208904 | tf_op jit(solution)/shard_map/ppermute | solution.py:265
  31.1 17.1 %collective-permute-start.12 = (bf16[272,128]{1,0:T(8,128)(2,1)S(1)}, bf16[272,128]{1,0:T(8,128)(2,1)S(1)}, u32[]{:S(2)}, u32[]{:S(2)}) collective-permute-start(bf16[272,128]{1,0:T(8,128)(2,1)S(1)} %add_convert_fusion.23.after_ref), channel_id=1, source_target_pairs={{0,16},{2,18},{4,20},{6,22},{8,24},{10,26},{12,28},{14,30},{16,0},... | collective-permute-start | bytes 208904 | tf_op jit(solution)/shard_map/ppermute | solution.py:265
  37.3 6.8 %collective-permute-start.26 = (bf16[272,128]{1,0:T(8,128)(2,1)S(1)}, bf16[272,128]{1,0:T(8,128)(2,1)S(1)}, u32[]{:S(2)}, u32[]{:S(2)}) collective-permute-start(bf16[272,128]{1,0:T(8,128)(2,1)S(1)} %add_convert_fusion.6), channel_id=1, source_target_pairs={{0,16},{2,18},{4,20},{6,22},{8,24},{10,26},{12,28},{14,30},{16,0},... | collective-permute-start | bytes 208904 | tf_op jit(solution)/shard_map/ppermute | solution.py:265
  37.7 8.9 %collective-permute-start.19 = (bf16[272,128]{1,0:T(8,128)(2,1)S(1)}, bf16[272,128]{1,0:T(8,128)(2,1)S(1)}, u32[]{:S(2)}, u32[]{:S(2)}) collective-permute-start(bf16[272,128]{1,0:T(8,128)(2,1)S(1)} %add_convert_fusion.12), channel_id=1, source_target_pairs={{0,16},{2,18},{4,20},{6,22},{8,24},{10,26},{12,28},{14,30},{16,0},... | collective-permute-start | bytes 208904 | tf_op jit(solution)/shard_map/ppermute | solution.py:265
  40.4 9.4 %collective-permute-start.6 = (bf16[272,128]{1,0:T(8,128)(2,1)S(1)}, bf16[272,128]{1,0:T(8,128)(2,1)S(1)}, u32[]{:S(2)}, u32[]{:S(2)}) collective-permute-start(bf16[272,128]{1,0:T(8,128)(2,1)S(1)} %add_convert_fusion.20), channel_id=1, source_target_pairs={{0,16},{2,18},{4,20},{6,22},{8,24},{10,26},{12,28},{14,30},{16,0},... | collective-permute-start | bytes 208904 | tf_op jit(solution)/shard_map/ppermute | solution.py:265
  45.1 5.4 %collective-permute-start.27 = (bf16[272,128]{1,0:T(8,128)(2,1)S(1)}, bf16[272,128]{1,0:T(8,128)(2,1)S(1)}, u32[]{:S(2)}, u32[]{:S(2)}) collective-permute-start(bf16[272,128]{1,0:T(8,128)(2,1)S(1)} %get-tuple-element.54), channel_id=1, source_target_pairs={{0,4},{2,6},{4,0},{6,2},{8,12},{10,14},{12,8},{14,10},{16,20},{18,... | collective-permute-start | bytes 208904 | tf_op jit(solution)/shard_map/ppermute | solution.py:265
  47.6 4.4 %collective-permute-start.20 = (bf16[272,128]{1,0:T(8,128)(2,1)S(1)}, bf16[272,128]{1,0:T(8,128)(2,1)S(1)}, u32[]{:S(2)}, u32[]{:S(2)}) collective-permute-start(bf16[272,128]{1,0:T(8,128)(2,1)S(1)} %get-tuple-element.56), channel_id=1, source_target_pairs={{0,4},{2,6},{4,0},{6,2},{8,12},{10,14},{12,8},{14,10},{16,20},{18,... | collective-permute-start | bytes 208904 | tf_op jit(solution)/shard_map/ppermute | solution.py:265
  48.3 4.5 %collective-permute-start.13 = (bf16[272,128]{1,0:T(8,128)(2,1)S(1)}, bf16[272,128]{1,0:T(8,128)(2,1)S(1)}, u32[]{:S(2)}, u32[]{:S(2)}) collective-permute-start(bf16[272,128]{1,0:T(8,128)(2,1)S(1)} %get-tuple-element.58), channel_id=1, source_target_pairs={{0,4},{2,6},{4,0},{6,2},{8,12},{10,14},{12,8},{14,10},{16,20},{18,... | collective-permute-start | bytes 208904 | tf_op jit(solution)/shard_map/ppermute | solution.py:265
  49.9 4.4 %collective-permute-start.7 = (bf16[272,128]{1,0:T(8,128)(2,1)S(1)}, bf16[272,128]{1,0:T(8,128)(2,1)S(1)}, u32[]{:S(2)}, u32[]{:S(2)}) collective-permute-start(bf16[272,128]{1,0:T(8,128)(2,1)S(1)} %get-tuple-element.60), channel_id=1, source_target_pairs={{0,4},{2,6},{4,0},{6,2},{8,12},{10,14},{12,8},{14,10},{16,20},{18,... | collective-permute-start | bytes 208904 | tf_op jit(solution)/shard_map/ppermute | solution.py:265
  50.6 3.9 %collective-permute-start.28 = (bf16[2,272,128]{2,1,0:T(8,128)(2,1)S(1)}, bf16[2,272,128]{2,1,0:T(8,128)(2,1)S(1)}, u32[]{:S(2)}, u32[]{:S(2)}) collective-permute-start(bf16[2,272,128]{2,1,0:T(8,128)(2,1)S(1)} %get-tuple-element.61), channel_id=1, source_target_pairs={{0,2},{2,0},{4,6},{6,4},{8,10},{10,8},{12,14},{14,12},{16,18},{18,... | collective-permute-start | bytes 417800 | tf_op jit(solution)/shard_map/ppermute | solution.py:265
  52.0 5.2 %collective-permute-start.21 = (bf16[2,272,128]{2,1,0:T(8,128)(2,1)S(1)}, bf16[2,272,128]{2,1,0:T(8,128)(2,1)S(1)}, u32[]{:S(2)}, u32[]{:S(2)}) collective-permute-start(bf16[2,272,128]{2,1,0:T(8,128)(2,1)S(1)} %get-tuple-element.63), channel_id=1, source_target_pairs={{0,2},{2,0},{4,6},{6,4},{8,10},{10,8},{12,14},{14,12},{16,18},{18,... | collective-permute-start | bytes 417800 | tf_op jit(solution)/shard_map/ppermute | solution.py:265
  52.2 14.7 %collective-permute-start.11 = (bf16[512,1024]{1,0:T(8,128)(2,1)S(1)}, bf16[512,1024]{1,0:T(8,128)(2,1)S(1)}, u32[]{:S(2)}, u32[]{:S(2)}) collective-permute-start(bf16[512,1024]{1,0:T(8,128)(2,1)S(1)} %collective-permute-done.10), channel_id=1, source_target_pairs={{0,2},{2,0},{4,6},{6,4},{8,10},{10,8},{12,14},{14,12},{16,18},{18,... | collective-permute-start | bytes 3145736 | tf_op jit(solution)/shard_map/ppermute | solution.py:265
  52.8 7.9 %collective-permute-start.14 = (bf16[2,272,128]{2,1,0:T(8,128)(2,1)S(1)}, bf16[2,272,128]{2,1,0:T(8,128)(2,1)S(1)}, u32[]{:S(2)}, u32[]{:S(2)}) collective-permute-start(bf16[2,272,128]{2,1,0:T(8,128)(2,1)S(1)} %get-tuple-element.65), channel_id=1, source_target_pairs={{0,2},{2,0},{4,6},{6,4},{8,10},{10,8},{12,14},{14,12},{16,18},{18,... | collective-permute-start | bytes 417800 | tf_op jit(solution)/shard_map/ppermute | solution.py:265
  54.4 9.0 %collective-permute-start.8 = (bf16[2,272,128]{2,1,0:T(8,128)(2,1)S(1)}, bf16[2,272,128]{2,1,0:T(8,128)(2,1)S(1)}, u32[]{:S(2)}, u32[]{:S(2)}) collective-permute-start(bf16[2,272,128]{2,1,0:T(8,128)(2,1)S(1)} %get-tuple-element.67), channel_id=1, source_target_pairs={{0,2},{2,0},{4,6},{6,4},{8,10},{10,8},{12,14},{14,12},{16,18},{18,... | collective-permute-start | bytes 417800 | tf_op jit(solution)/shard_map/ppermute | solution.py:265
  56.4 10.8 %collective-permute-start.29 = (bf16[512,256]{1,0:T(8,128)(2,1)S(1)}, bf16[512,256]{1,0:T(8,128)(2,1)S(1)}, u32[]{:S(2)}, u32[]{:S(2)}) collective-permute-start(bf16[512,256]{1,0:T(8,128)(2,1)S(1)} %attend.7.refs_4_), channel_id=1, source_target_pairs={{0,1},{1,0},{2,3},{3,2},{4,5},{5,4},{6,7},{7,6},{8,9},{9,8},{10,11... | collective-permute-start | bytes 786440 | tf_op jit(solution)/shard_map/ppermute | solution.py:265
  59.2 12.3 %collective-permute-start.22 = (bf16[512,256]{1,0:T(8,128)(2,1)S(1)}, bf16[512,256]{1,0:T(8,128)(2,1)S(1)}, u32[]{:S(2)}, u32[]{:S(2)}) collective-permute-start(bf16[512,256]{1,0:T(8,128)(2,1)S(1)} %attend.6.refs_2_), channel_id=1, source_target_pairs={{0,1},{1,0},{2,3},{3,2},{4,5},{5,4},{6,7},{7,6},{8,9},{9,8},{10,11... | collective-permute-start | bytes 786440 | tf_op jit(solution)/shard_map/ppermute | solution.py:265
  62.7 14.4 %collective-permute-start.15 = (bf16[512,256]{1,0:T(8,128)(2,1)S(1)}, bf16[512,256]{1,0:T(8,128)(2,1)S(1)}, u32[]{:S(2)}, u32[]{:S(2)}) collective-permute-start(bf16[512,256]{1,0:T(8,128)(2,1)S(1)} %attend.5.refs_0_), channel_id=1, source_target_pairs={{0,1},{1,0},{2,3},{3,2},{4,5},{5,4},{6,7},{7,6},{8,9},{9,8},{10,11... | collective-permute-start | bytes 786440 | tf_op jit(solution)/shard_map/ppermute | solution.py:265
  65.3 16.9 %collective-permute-start.9 = (bf16[512,256]{1,0:T(8,128)(2,1)S(1)}, bf16[512,256]{1,0:T(8,128)(2,1)S(1)}, u32[]{:S(2)}, u32[]{:S(2)}) collective-permute-start(bf16[512,256]{1,0:T(8,128)(2,1)S(1)} %attend.4.refs_6_), channel_id=1, source_target_pairs={{0,1},{1,0},{2,3},{3,2},{4,5},{5,4},{6,7},{7,6},{8,9},{9,8},{10,11... | collective-permute-start | bytes 786440 | tf_op jit(solution)/shard_map/ppermute | solution.py:265
  (3 other events, 10.1 us)

commit v4 on v0

v4 whole, which is shorter than its diff:
```python
import functools
import math

import jax
import jax.numpy as jnp
from jax import lax
from jax.experimental import pallas as pl
from jax.experimental.pallas import tpu as pltpu
from jax.sharding import PartitionSpec as P

BLOCK = 512
LANES = 128
SIZES = (2, 2, 2, 2)
LIMIT = 20 << 20
NEVER = -1e30
F32 = jnp.float32
BF16 = jnp.bfloat16
VMEM = pl.BlockSpec(memory_space=pltpu.VMEM)
ANY = pl.BlockSpec(memory_space=pl.ANY)
HBM = pl.BlockSpec(memory_space=pltpu.HBM)
PARAMS = pltpu.CompilerParams(vmem_limit_bytes=LIMIT)


def dot(a, b, contract=((1,), (0,))):
    return lax.dot_general(a, b, (contract, ((), ())), preferred_element_type=F32)


def one_hot(codes, ncodes):
    table = lax.broadcasted_iota(jnp.int32, (ncodes, codes.shape[1]), 0)
    return (table == codes).astype(BF16)


class Layout:
    def __init__(self, devices, first, heads, ncodes):
        self.first, self.heads, self.half = (first, heads, heads // 2)
        self.each = ncodes // LANES
        self.per = self.half * self.each // 2
        self.shift = int(math.log2(256 // devices + 1))
        self.digits = 1
        while (1 << (self.shift * self.digits)) <= BLOCK:
            self.digits += 1
        self.sums = self.per * LANES
        self.tail = -(-self.digits * self.per // 16) * 16
        self.rows = self.sums + self.tail
        assert ncodes % (2 * LANES) == 0 and heads % 2 == 0 and devices % 4 == 0

    def place(self, k, j):
        piece, at = divmod(j, self.each // 2)
        return (piece, k * (self.each // 2) + at)


class Chain:
    def __init__(self):
        self.last = None

    def __call__(self, kernel, shapes, args, in_hbm=(), scratch=(), name=None, flops=1000000000):
        first = [] if self.last is None else [self.last]

        def run(*refs):
            return kernel(*refs[len(first) :])

        outs = pl.pallas_call(
            run,
            out_shape=shapes,
            in_specs=[ANY] * len(first) + [HBM if n in in_hbm else VMEM for n in range(len(args))],
            out_specs=jax.tree.map(lambda _: VMEM, shapes),
            scratch_shapes=list(scratch),
            compiler_params=PARAMS,
            cost_estimate=pl.CostEstimate(flops=flops, bytes_accessed=1000000, transcendentals=0),
            name=name,
        )(*first, *args)
        self.last = jax.tree.leaves(outs)[0]
        return outs


def bit_of(bit):
    return (lax.axis_index("ctx") & bit) != 0


def shape_of(*dims, dtype=BF16):
    return jax.ShapeDtypeStruct(dims, dtype)


def turn(chain, queries, values, book, out_weight):
    tokens, heads, width = queries.shape
    sides = lax.axis_size("head")
    rows, columns = (out_weight.shape[0], out_weight.shape[1] // sides)
    half = rows // 2
    peers = range(1, sides)

    def kernel(queries_ref, values_ref, book_ref, weight_ref, vt_ref, qt_ref, bt_ref, *refs):
        blocks, sems = (refs[:-1], refs[-1])
        core, side = (lax.axis_index("ctx") & 1, lax.axis_index("head"))
        copies = []
        for n, k in enumerate(peers):
            part = weight_ref.at[
                pl.ds(pl.multiple_of(core * half, half), half), pl.ds(pl.multiple_of((side ^ k) * columns, columns), columns)
            ]
            copies.append(pltpu.make_async_copy(part, blocks[n], sems.at[n]))
            copies[-1].start()
        vt_ref[...] = jnp.swapaxes(values_ref[...], 0, 1)
        qt_ref[...] = jnp.swapaxes(queries_ref[...], 0, 1)
        for h in range(heads):
            bt_ref[h] = book_ref[h].T
        for copy in copies:
            copy.wait()

    shapes = [shape_of(heads, tokens, width), shape_of(heads, tokens, width), shape_of(heads, width, book.shape[1])]
    shapes += [shape_of(half, columns) for _ in peers]
    outs = chain(
        kernel, shapes, (queries, values, book, out_weight), in_hbm=(3,),
        scratch=[pltpu.SemaphoreType.DMA((max(1, len(peers)),))], name="turn",
    )
    return outs[0], outs[1], outs[2], outs[3:]


def block_sums(chain, lay, codes, codes2, vt, values2, turned):
    heads, tokens = codes.shape

    def kernel(codes_ref, codes2_ref, vt_ref, values2_ref, mine_ref, send_ref, low_ref, *refs):
        buf = refs[-1]
        if turned:
            vt2_ref = values2_ref
        else:
            vt2_ref = refs[0]
            vt2_ref[...] = jnp.swapaxes(values2_ref[...], 0, 1)
        core, row = (bit_of(1), bit_of(2).astype(jnp.int32))
        line = lax.broadcasted_iota(jnp.int32, (lay.tail, LANES), 0)
        eye = lax.broadcasted_iota(jnp.int32, (LANES, LANES), 0) == lax.broadcasted_iota(jnp.int32, (LANES, LANES), 1)
        mask = (1 << lay.shift) - 1
        ones = jnp.ones((tokens, LANES), BF16)
        tails = [[jnp.zeros((lay.tail, LANES), F32) for _ in range(2)] for _ in range(2)]
        for k in range(lay.half):
            h = lay.first + core.astype(jnp.int32) * lay.half + k
            own, other = [
                dot(one_hot(c[pl.ds(h, 1), :], lay.each * LANES), jnp.concatenate([v[h], ones], axis=1))
                for c, v in ((codes_ref, vt_ref), (codes2_ref, vt2_ref))
            ]
            for to, ref, both in ((0, buf, own + other), (1, low_ref, jnp.where(core, other, own))):
                for j in range(lay.each):
                    piece, at = lay.place(k, j)
                    here = slice(j * LANES, (j + 1) * LANES)
                    ref[piece ^ row, at * LANES : (at + 1) * LANES, :] = both[here, :LANES].astype(BF16)
                    count = jnp.sum(jnp.where(eye, both[here, LANES:], 0.0), axis=0, keepdims=True).astype(jnp.int32)
                    for d in range(lay.digits):
                        digit = ((count >> (lay.shift * d)) & mask).astype(F32)
                        tails[to][piece] = jnp.where(line == d * lay.per + at, digit, tails[to][piece])
        for to, ref in ((0, buf), (1, low_ref)):
            for piece in range(2):
                ref[piece ^ row, lay.sums :, :] = tails[to][piece].astype(BF16)
        mine_ref[...] = buf[0]
        send_ref[...] = buf[1]

    shapes = [shape_of(lay.rows, LANES)] * 2 + [shape_of(2, lay.rows, LANES)]
    if not turned:
        shapes.append(shape_of(*vt.shape))
    return chain(
        kernel, shapes, (codes, codes2, vt, values2), scratch=[pltpu.VMEM((2, lay.rows, LANES), BF16)], name="block_sums"
    )


def plus(chain, a, b):
    def kernel(a_ref, b_ref, out_ref):
        out_ref[...] = (a_ref[...].astype(F32) + b_ref[...].astype(F32)).astype(BF16)

    return chain(kernel, shape_of(*a.shape), (a, b), name="plus")


def with_low(before, low, flag):
    more = (before + low.astype(F32)).astype(BF16)
    before = before.astype(BF16)
    return jnp.where(flag, more, before), jnp.where(flag, before, more)


def spread(chain, got, bits, got2, mine):
    def kernel(*refs):
        got_refs, (got2_ref, mine_ref, own_ref, send_ref) = (refs[:-4], refs[-4:])
        before = 0.0
        for ref, bit in zip(got_refs, bits):
            before = before + jnp.where(bit_of(bit), ref[...].astype(F32), 0.0)
        low = jnp.where(bit_of(2), got2_ref[...].astype(F32), mine_ref[...].astype(F32))
        own_ref[...], send_ref[...] = with_low(before, low, bit_of(2))

    return chain(kernel, [shape_of(*mine.shape)] * 2, (*got, got2, mine), name="spread")


def share(chain, own, got, low):
    def kernel(own_ref, got_ref, low_ref, mine_ref, send_ref):
        for n, ref in enumerate((own_ref, got_ref)):
            mine_ref[n], send_ref[n] = with_low(ref[...].astype(F32), low_ref[n], bit_of(1))

    return chain(kernel, [shape_of(*low.shape)] * 2, (own, got, low), name="share")


def lane_tiles(x):
    return [x[:, j : j + LANES] for j in range(0, x.shape[1], LANES)]


def window(chain, lay, codes, qt, vt, bt, out_weight=None):
    heads, tokens, width = qt.shape
    factor = width ** (-0.5) * math.log2(math.e)
    tile = tokens // 2
    columns = out_weight.shape[1] // lax.axis_size("head") if out_weight is not None else 0

    def kernel(codes_ref, qt_ref, vt_ref, bt_ref, *refs):
        if columns:
            weight_ref, num_ref, top_ref, den_ref, own_ref, sem = refs
            at = pl.multiple_of(lax.axis_index("head") * columns, columns)
            copy = pltpu.make_async_copy(weight_ref.at[:, pl.ds(at, columns)], own_ref, sem.at[0])
            copy.start()
        else:
            num_ref, top_ref, den_ref = refs
        causal = lax.broadcasted_iota(jnp.int32, (tile, tile), 0) >= lax.broadcasted_iota(jnp.int32, (tile, tile), 1)
        for k in range(lay.heads):
            h = lay.first + k
            keys = dot(bt_ref[h], one_hot(codes_ref[h : h + 1, :], bt_ref.shape[2])).astype(BF16)
            for r in range(2):
                rows = slice(r * tile, (r + 1) * tile)
                upto = slice(0, (r + 1) * tile)
                score = dot(qt_ref[h, rows, :], keys[:, upto])
                last = jnp.where(causal, score[:, r * tile :], NEVER)
                score = jnp.concatenate([score[:, :tile], last], axis=1) if r else last
                top = jnp.max(functools.reduce(jnp.maximum, lane_tiles(score)), axis=1, keepdims=True)
                top_ref[k, rows, :] = jnp.broadcast_to(top, (tile, LANES))
                weight = jnp.exp2((score - top) * factor)
                den = jnp.sum(sum(lane_tiles(weight)), axis=1, keepdims=True)
                den_ref[k, rows, :] = jnp.broadcast_to(den, (tile, LANES))
                num_ref[k, rows, :] = dot(weight.astype(BF16), vt_ref[h, upto, :])
        if columns:
            copy.wait()

    shapes = [shape_of(lay.heads, tokens, n, dtype=F32) for n in (width, LANES, LANES)]
    args, scratch = ([codes, qt, vt, bt], [])
    if columns:
        args.append(out_weight)
        shapes.append(shape_of(out_weight.shape[0], columns))
        scratch = [pltpu.SemaphoreType.DMA((1,))]
    return chain(kernel, shapes, args, in_hbm=(4,), scratch=scratch, name="window", flops=200000000)


def attend(chain, lay, qt, bt, num, top, den, mine, theirs):
    heads, tokens, width = qt.shape
    factor = width ** (-0.5) * math.log2(math.e)
    tile = tokens // 2

    def kernel(qt_ref, bt_ref, num_ref, top_ref, den_ref, mine_ref, theirs_ref, out_ref, buf):
        core, row = (bit_of(1).astype(jnp.int32), bit_of(2).astype(jnp.int32))
        buf[core] = mine_ref[...]
        buf[1 - core] = theirs_ref[...]
        tails = [[buf[c, p ^ row, lay.sums :, :].astype(F32) for p in range(2)] for c in range(2)]
        for k in range(lay.heads):
            h = lay.first + k
            owner, within = divmod(k, lay.half)
            sums, counts = ([], [])
            for j in range(lay.each):
                p, at = lay.place(within, j)
                sums.append(buf[owner, p ^ row, at * LANES : (at + 1) * LANES, :])
                count = 0.0
                for d in range(lay.digits):
                    line = d * lay.per + at
                    count = count + tails[owner][p][line : line + 1] * float(1 << (lay.shift * d))
                counts.append(count)
            cache = jnp.concatenate(sums, axis=0)
            for r in range(2):
                rows = slice(r * tile, (r + 1) * tile)
                scores = lane_tiles(dot(qt_ref[h, rows, :], bt_ref[h]))
                scores = [s + jnp.where(n > 0.5, 0.0, NEVER) for s, n in zip(scores, counts)]
                early = top_ref[k, rows, :]
                top = jnp.maximum(early, jnp.max(functools.reduce(jnp.maximum, scores), axis=1, keepdims=True))
                weights = [jnp.exp2((s - top) * factor) for s in scores]
                keep = jnp.exp2((early - top) * factor)
                den = jnp.sum(sum(w * n for w, n in zip(weights, counts)), axis=1, keepdims=True)
                den = keep * den_ref[k, rows, :] + den
                num = dot(jnp.concatenate([w.astype(BF16) for w in weights], axis=1), cache)
                num = keep * num_ref[k, rows, :] + num
                out_ref[rows, k * width : (k + 1) * width] = (num * (1.0 / den)).astype(BF16)

    return chain(
        kernel, shape_of(tokens, lay.heads * width), (qt, bt, num, top, den, mine, theirs),
        scratch=[pltpu.VMEM((2, 2, lay.rows, LANES), BF16)], name="attend",
    )


def mix(chain, terms, weights, base, dtype):
    parts = [term[0] for term in terms]
    used = sorted({term[1] for term in terms})
    spans = [(used.index(w), a, b) for _, w, a, b in terms]
    tokens, columns = (parts[0].shape[0], weights[0].shape[1])
    extra = [] if base is None else [base]
    wide, tile = (min(columns, 256), tokens // 2)

    def kernel(*refs):
        out_ref = refs[-1]
        for r in range(0, tokens, tile):
            for c in range(0, columns, wide):
                total = sum(
                    dot(refs[n][r : r + tile, :], refs[len(parts) + w][a:b, c : c + wide])
                    for n, (w, a, b) in enumerate(spans)
                )
                if extra:
                    total = total + refs[-2][r : r + tile, c : c + wide]
                out_ref[r : r + tile, c : c + wide] = total.astype(out_ref.dtype)

    return chain(kernel, shape_of(tokens, columns, dtype=dtype), (*parts, *[weights[w] for w in used], *extra), name="mix")


def swap(x, axis, k):
    return lax.ppermute(x, axis, [(i, i ^ k) for i in range(lax.axis_size(axis))])


def group_sizes(heads):
    ends = [max(n + 1, heads // 2 * sum(SIZES[: n + 1]) // sum(SIZES)) for n in range(len(SIZES))]
    ends = sorted({min(end, heads // 2) for end in ends})
    return [2 * (b - a) for a, b in zip([0] + ends, ends)]


def on_device(queries, values, codes, codebook, out_weight):
    tokens, heads, width = queries.shape
    assert tokens == BLOCK
    devices, sides = (lax.axis_size("ctx"), lax.axis_size("head"))
    assert devices & (devices - 1) == 0 and sides & (sides - 1) == 0
    lays, first = ([], 0)
    for count in group_sizes(heads):
        lays.append(Layout(devices, first, count, codebook.shape[1]))
        first += count
    codes = codes.T
    chain = Chain()

    values2, codes2 = (swap(values, "ctx", 1), swap(codes, "ctx", 1))
    vt, qt, bt, blocks = turn(chain, queries, values, codebook, out_weight)
    blocks = [swap(block, "head", k + 1) for k, block in enumerate(blocks)]

    runs = []
    for n, lay in enumerate(lays):
        outs = block_sums(chain, lay, codes, codes2, vt, values2, n > 0)
        if n == 0:
            values2 = outs[3]
        runs.append((*outs[:3], swap(outs[1], "ctx", 2)))
    totals = []
    for mine, send, low, got2 in runs:
        totals.append(plus(chain, mine, got2))
    bits = [1 << n for n in range(2, devices.bit_length() - 1)]
    windows = [window(chain, lays[0], codes, qt, vt, bt, out_weight)]
    got = [[] for _ in runs]
    for bit in bits:
        arrived = [swap(total, "ctx", bit) for total in totals]
        for g, part in enumerate(arrived):
            got[g].append(part)
        if bit != bits[-1]:
            totals = [plus(chain, total, part) for total, part in zip(totals, arrived)]
    windows += [window(chain, lay, codes, qt, vt, bt) for lay in lays[1:]]
    pairs = [spread(chain, got[g], bits, run[3], run[0]) for g, run in enumerate(runs)]
    pairs = [(own, swap(send, "ctx", 2)) for own, send in pairs]
    pairs = [share(chain, own, other, run[2]) for run, (own, other) in zip(runs, pairs)]
    pairs = [(mine, swap(send, "ctx", 1)) for mine, send in pairs]

    weights = {0: windows[0][3]}
    core = lax.axis_index("ctx") & 1
    for k, mine in enumerate(blocks):
        other = swap(mine, "ctx", 1)
        both = jnp.stack([jnp.where(core == 0, mine, other), jnp.where(core == 0, other, mine)])
        weights[k + 1] = both.reshape(-1, mine.shape[1])
    terms = []
    for lay, pair, (num, top, den, *_) in zip(lays, pairs, windows):
        attended = attend(chain, lay, qt, bt, num, top, den, *pair)
        span = (lay.first * width, (lay.first + lay.heads) * width)
        terms.append((attended, 0, *span))
        terms += [(swap(attended, "head", k), k, *span) for k in range(1, sides)]
    late = len(terms) - (sides - 1)
    base = mix(chain, terms[:late], weights, None, F32)
    return mix(chain, terms[late:], weights, base, BF16)


def solution(mesh):
    return jax.shard_map(
        on_device,
        mesh=mesh,
        in_specs=(
            P("ctx", "head", None),
            P("ctx", "head", None),
            P("ctx", "head"),
            P("head", None, None),
            P("head", None),
        ),
        out_specs=P("ctx", "head"),
        check_vma=False,
    )
```

time: 358 us -> 91.8 us (0.26)
  blocking collectives: 132 us -> 0 us
  other arithmetic: 59.6 us -> 1.56 us
  local copies, waits for them, and re-layouts: 55.6 us -> 5.87 us
  matrix products: 41.2 us -> 0 us
  Pallas kernels: 0 us -> 22.7 us
  between operations: 13.7 us -> 0.26 us
  starting transfers between devices: 18 us -> 28.5 us
    all_gather x1 -> x0, blocking collectives: 132 us -> none  [prefix(): everything = jax.tree.map(lambda part: lax.all_gather(part, axis), x)]
    select_n x32 -> x0, other arithmetic: 48.5 us -> none  [turn(): return jax.tree.map(lambda a, b: jnp.where(reached, a, b), new, before)]
    dot_general x8 -> x0, matrix products: 41.2 us -> none  [the longest x1 9.17 us: attend(): jnp.dot(code_weight, cache_sum, precision=lax.Precision.HIGHEST)]
    gather x1 -> x0, local copies, waits for them, and re-layouts: 40.2 us -> none  [on_device(): book[index]]
    all_gather x2 -> x0, waiting for transfers between devices: 35 us -> none  [the longest x1 31.1 us: on_device(): lax.all_gather(attended_all, 'head', axis=1, tiled=True)]
    ppermute x4 -> x28, waiting for transfers between devices: 0.01 us -> 32.6 us  [swap(): lax.ppermute(x, axis, [(i, i ^ k) for i in range(lax.axis_size(axis))])]
    pallas_call x0 -> x31, Pallas kernels: none -> 22.7 us  [__call__(): pl.pallas_call(run, out_shape=shapes, in_specs=[ANY] * len(first) + [HBM...]
    ppermute x4 -> x28, starting transfers between devices: 12.4 us -> 28.5 us  [swap(): lax.ppermute(x, axis, [(i, i ^ k) for i in range(lax.axis_size(axis))])]
  transfers between devices with their start and end apart: 7 -> 28, of which waited for: 2 -> 7; matrix products, arithmetic and copies ran while one was open for 40% -> 2% of each run, Pallas kernels for 0% -> 23%
where the time goes in v4:
time: 91.8 us; the launch traced here: 91.5 us
  waiting for transfers between devices  32.6 us (36%)
  starting transfers between devices  28.5 us (31%)
  Pallas kernels  22.7 us (25%)
  local copies, waits for them, and re-layouts  5.87 us (6%)
  other arithmetic  1.56 us (2%)
    ppermute x28, waiting for transfers between devices, swap(): lax.ppermute(x, axis, [(i, i ^ k) for i in range(lax.axis_size(axis))])  32.6 us
    ppermute x28, starting transfers between devices, swap(): lax.ppermute(x, axis, [(i, i ^ k) for i in range(lax.axis_size(axis))])  28.5 us
    pallas_call x31, Pallas kernels, __call__(): pl.pallas_call(run, out_shape=shapes, in_specs=[ANY] * len(first) + [HBM...  22.7 us
    unnamed x12, local copies, waits for them, and re-layouts  5.87 us
  transfers between devices with their start and end apart: 28, of which 7 were waited for; matrix products, arithmetic and copies ran while one was open for 2% of the time, Pallas kernels for 23%

profile of v4, /device:TPU:0, one launch (start us, length us, event | category | flops | bytes accessed | tf_op | source)
XLA Modules:
  0.0 91.5 jit_solution(14494476573219672435)
XLA Ops:
  0.5 2.2 %copy-done = bf16[1024,2048]{1,0:T(8,128)(2,1)S(1)} copy-done((bf16[1024,2048]{1,0:T(8,128)(2,1)S(1)}, bf16[1024,2048]{1,0:T(8,128)(2,1)}, u32[]{:S(2)}) %copy-start) | copy-done | bytes 4194328
  2.7 1.2 %copy-done.2 = bf16[512,8,128]{2,1,0:T(8,128)(2,1)S(1)} copy-done((bf16[512,8,128]{2,1,0:T(8,128)(2,1)S(1)}, bf16[512,8,128]{2,1,0:T(8,128)(2,1)}, u32[]{:S(2)}) %copy-start.2) | copy-done | bytes 1048600
  5.1 1.2 %copy-done.4 = bf16[512,8,128]{2,1,0:T(8,128)(2,1)S(1)} copy-done((bf16[512,8,128]{2,1,0:T(8,128)(2,1)S(1)}, bf16[512,8,128]{2,1,0:T(8,128)(2,1)}, u32[]{:S(2)}) %copy-start.4) | copy-done | bytes 1048600
  6.4 2.0 %turn.1 = (bf16[8,512,128]{2,1,0:T(8,128)(2,1)S(1)}, bf16[8,512,128]{2,1,0:T(8,128)(2,1)S(1)}, bf16[8,128,512]{2,1,0:T(8,128)(2,1)S(1)}, bf16[512,1024]{1,0:T(8,128)(2,1)}) custom-call(bf16[512,8,128]{2,1,0:T(8,128)(2,1)S(1)} %copy-done.2, bf16[512,8,128]{2,1,0:T(8,128)(2,1)S(1)} %copy-done.4, bf16[8,512,128]{2,1,0:T(8,128)(2,1)S(1)} %copy-done.3, ...), custom_call_target="tpu_custom_call" | custom-call | flops 1000000000 | bytes 1000000 | tf_op jit(solution)/shard_map/turn/pallas_call | solution.py:62
  8.3 2.5 %collective-permute-start.25 = (bf16[512,1024]{1,0:T(8,128)(2,1)}, bf16[512,1024]{1,0:T(8,128)(2,1)}, u32[]{:S(2)}, u32[]{:S(2)}) collective-permute-start(bf16[512,1024]{1,0:T(8,128)(2,1)} %get-tuple-element.96), channel_id=1, source_target_pairs={{0,1},{1,0},{2,3},{3,2},{4,5},{5,4},{6,7},{7,6},{8,9},{9,8},{10,11... | collective-permute-start | bytes 3145736 | tf_op jit(solution)/shard_map/ppermute | solution.py:308
  12.1 1.9 %block_sums.4 = (bf16[272,128]{1,0:T(8,128)(2,1)S(1)}, bf16[272,128]{1,0:T(8,128)(2,1)S(1)}, bf16[2,272,128]{2,1,0:T(8,128)(2,1)S(1)}, bf16[8,512,128]{2,1,0:T(8,128)(2,1)S(1)}) custom-call(bf16[8,512,128]{2,1,0:T(8,128)(2,1)S(1)} %get-tuple-element.51.refs_0_.refs_3_, s32[8,512]{1,0:T(8,128)S(1)} %bitcast.9, s32[8,512]{1,0:T(8,128)S(1)} %collective-permute-done.refs_2_, ...), custom_call_target="tpu_custom_call" | custom-call | flops 1000000000 | bytes 1000000 | tf_op jit(solution)/shard_map/block_sums/pallas_call | solution.py:62
  14.0 1.6 %collective-permute-start.2 = (bf16[272,128]{1,0:T(8,128)(2,1)S(1)}, bf16[272,128]{1,0:T(8,128)(2,1)S(1)}, u32[]{:S(2)}, u32[]{:S(2)}) collective-permute-start(bf16[272,128]{1,0:T(8,128)(2,1)S(1)} %get-tuple-element.57), channel_id=1, source_target_pairs={{0,4},{2,6},{4,0},{6,2},{8,12},{10,14},{12,8},{14,10},{16,20},{18,... | collective-permute-start | bytes 208904 | tf_op jit(solution)/shard_map/ppermute | solution.py:308
  17.1 1.6 %collective-permute-start.4 = (bf16[272,128]{1,0:T(8,128)(2,1)S(1)}, bf16[272,128]{1,0:T(8,128)(2,1)S(1)}, u32[]{:S(2)}, u32[]{:S(2)}) collective-permute-start(bf16[272,128]{1,0:T(8,128)(2,1)S(1)} %get-tuple-element.59), channel_id=1, source_target_pairs={{0,4},{2,6},{4,0},{6,2},{8,12},{10,14},{12,8},{14,10},{16,20},{18,... | collective-permute-start | bytes 208904 | tf_op jit(solution)/shard_map/ppermute | solution.py:308
  19.7 15.3 %collective-permute-done.25 = bf16[512,1024]{1,0:T(8,128)(2,1)} collective-permute-done((bf16[512,1024]{1,0:T(8,128)(2,1)}, bf16[512,1024]{1,0:T(8,128)(2,1)}, u32[]{:S(2)}, u32[]{:S(2)}) %collective-permute-start.25) | collective-permute-done | bytes 1048608 | tf_op jit(solution)/shard_map/ppermute | solution.py:308
  35.1 1.9 %collective-permute-start.6 = (bf16[272,128]{1,0:T(8,128)(2,1)S(1)}, bf16[272,128]{1,0:T(8,128)(2,1)S(1)}, u32[]{:S(2)}, u32[]{:S(2)}) collective-permute-start(bf16[272,128]{1,0:T(8,128)(2,1)S(1)} %plus.8.refs_0_.refs_1_), channel_id=1, source_target_pairs={{0,8},{2,10},{4,12},{6,14},{8,0},{10,2},{12,4},{14,6},{16,24},{18,... | collective-permute-start | bytes 208904 | tf_op jit(solution)/shard_map/ppermute | solution.py:308
  37.3 1.9 %collective-permute-start.8 = (bf16[272,128]{1,0:T(8,128)(2,1)S(1)}, bf16[272,128]{1,0:T(8,128)(2,1)S(1)}, u32[]{:S(2)}, u32[]{:S(2)}) collective-permute-start(bf16[272,128]{1,0:T(8,128)(2,1)S(1)} %plus.10.refs_0_.refs_1_), channel_id=1, source_target_pairs={{0,8},{2,10},{4,12},{6,14},{8,0},{10,2},{12,4},{14,6},{16,24},{18,... | collective-permute-start | bytes 208904 | tf_op jit(solution)/shard_map/ppermute | solution.py:308
  39.5 2.3 %window.4 = (f32[2,512,128]{2,1,0:T(8,128)S(1)}, f32[2,512,128]{2,1,0:T(8,128)S(1)}, f32[2,512,128]{2,1,0:T(8,128)S(1)}, bf16[1024,1024]{1,0:T(8,128)(2,1)S(1)}) custom-call(bf16[272,128]{1,0:T(8,128)(2,1)S(1)} %plus.11.refs_0_.refs_1_, s32[8,512]{1,0:T(8,128)S(1)} %bitcast.13, bf16[8,512,128]{2,1,0:T(8,128)(2,1)S(1)} %get-tuple-element.61.refs_2_.refs_1_, ...), custom_call_target="tpu_custom_call" | custom-call | flops 200000000 | bytes 1000000 | tf_op jit(solution)/shard_map/window/pallas_call | solution.py:62
  41.8 2.9 %collective-permute-start.10 = (bf16[272,128]{1,0:T(8,128)(2,1)S(1)}, bf16[272,128]{1,0:T(8,128)(2,1)S(1)}, u32[]{:S(2)}, u32[]{:S(2)}) collective-permute-start(bf16[272,128]{1,0:T(8,128)(2,1)S(1)} %plus.12.refs_0_), channel_id=1, source_target_pairs={{0,16},{2,18},{4,20},{6,22},{8,24},{10,26},{12,28},{14,30},{16,0},... | collective-permute-start | bytes 208904 | tf_op jit(solution)/shard_map/ppermute | solution.py:308
  44.9 2.9 %collective-permute-start.12 = (bf16[272,128]{1,0:T(8,128)(2,1)S(1)}, bf16[272,128]{1,0:T(8,128)(2,1)S(1)}, u32[]{:S(2)}, u32[]{:S(2)}) collective-permute-start(bf16[272,128]{1,0:T(8,128)(2,1)S(1)} %plus.14.refs_0_), channel_id=1, source_target_pairs={{0,16},{2,18},{4,20},{6,22},{8,24},{10,26},{12,28},{14,30},{16,0},... | collective-permute-start | bytes 208904 | tf_op jit(solution)/shard_map/ppermute | solution.py:308
  48.0 1.7 %window.5 = (f32[2,512,128]{2,1,0:T(8,128)S(1)}, f32[2,512,128]{2,1,0:T(8,128)S(1)}, f32[2,512,128]{2,1,0:T(8,128)S(1)}) custom-call(bf16[272,128]{1,0:T(8,128)(2,1)S(1)} %plus.15.refs_0_, s32[8,512]{1,0:T(8,128)S(1)} %bitcast.14, bf16[8,512,128]{2,1,0:T(8,128)(2,1)S(1)} %get-tuple-element.61.refs_2_.refs_1_, ...), custom_call_target="tpu_custom_call" | custom-call | flops 200000000 | bytes 1000000 | tf_op jit(solution)/shard_map/window/pallas_call | solution.py:62
  49.7 1.7 %window.6 = (f32[2,512,128]{2,1,0:T(8,128)S(1)}, f32[2,512,128]{2,1,0:T(8,128)S(1)}, f32[2,512,128]{2,1,0:T(8,128)S(1)}) custom-call(f32[2,512,128]{2,1,0:T(8,128)S(1)} %get-tuple-element.64.refs_0_.refs_3_, s32[8,512]{1,0:T(8,128)S(1)} %bitcast.15, bf16[8,512,128]{2,1,0:T(8,128)(2,1)S(1)} %get-tuple-element.61.refs_2_.refs_1_, ...), custom_call_target="tpu_custom_call" | custom-call | flops 200000000 | bytes 1000000 | tf_op jit(solution)/shard_map/window/pallas_call | solution.py:62
  51.5 1.7 %window.7 = (f32[2,512,128]{2,1,0:T(8,128)S(1)}, f32[2,512,128]{2,1,0:T(8,128)S(1)}, f32[2,512,128]{2,1,0:T(8,128)S(1)}) custom-call(f32[2,512,128]{2,1,0:T(8,128)S(1)} %get-tuple-element.65.refs_0_.refs_3_, s32[8,512]{1,0:T(8,128)S(1)} %bitcast.16, bf16[8,512,128]{2,1,0:T(8,128)(2,1)S(1)} %get-tuple-element.61.refs_2_.refs_1_, ...), custom_call_target="tpu_custom_call" | custom-call | flops 200000000 | bytes 1000000 | tf_op jit(solution)/shard_map/window/pallas_call | solution.py:62
  53.3 1.8 %collective-permute-start.14 = (bf16[272,128]{1,0:T(8,128)(2,1)S(1)}, bf16[272,128]{1,0:T(8,128)(2,1)S(1)}, u32[]{:S(2)}, u32[]{:S(2)}) collective-permute-start(bf16[272,128]{1,0:T(8,128)(2,1)S(1)} %get-tuple-element.71), channel_id=1, source_target_pairs={{0,4},{2,6},{4,0},{6,2},{8,12},{10,14},{12,8},{14,10},{16,20},{18,... | collective-permute-start | bytes 208904 | tf_op jit(solution)/shard_map/ppermute | solution.py:308
  55.2 1.7 %collective-permute-start.15 = (bf16[272,128]{1,0:T(8,128)(2,1)S(1)}, bf16[272,128]{1,0:T(8,128)(2,1)S(1)}, u32[]{:S(2)}, u32[]{:S(2)}) collective-permute-start(bf16[272,128]{1,0:T(8,128)(2,1)S(1)} %get-tuple-element.74), channel_id=1, source_target_pairs={{0,4},{2,6},{4,0},{6,2},{8,12},{10,14},{12,8},{14,10},{16,20},{18,... | collective-permute-start | bytes 208904 | tf_op jit(solution)/shard_map/ppermute | solution.py:308
  57.0 1.4 %collective-permute-start.16 = (bf16[272,128]{1,0:T(8,128)(2,1)S(1)}, bf16[272,128]{1,0:T(8,128)(2,1)S(1)}, u32[]{:S(2)}, u32[]{:S(2)}) collective-permute-start(bf16[272,128]{1,0:T(8,128)(2,1)S(1)} %get-tuple-element.77), channel_id=1, source_target_pairs={{0,4},{2,6},{4,0},{6,2},{8,12},{10,14},{12,8},{14,10},{16,20},{18,... | collective-permute-start | bytes 208904 | tf_op jit(solution)/shard_map/ppermute | solution.py:308
  60.2 1.3 %collective-permute-done.16.refs_2_ = bf16[272,128]{1,0:T(8,128)(2,1)S(1)} collective-permute-done((bf16[272,128]{1,0:T(8,128)(2,1)S(1)}, bf16[272,128]{1,0:T(8,128)(2,1)S(1)}, u32[]{:S(2)}, u32[]{:S(2)}) %collective-permute-start.16) | collective-permute-done | bytes 69664 | tf_op jit(solution)/shard_map/ppermute | solution.py:308
  63.0 1.4 %attend.4.refs_0_.refs_1_ = bf16[512,256]{1,0:T(8,128)(2,1)S(1)} custom-call(bf16[2,272,128]{2,1,0:T(8,128)(2,1)S(1)} %get-tuple-element.82.refs_0_.refs_6_, bf16[8,512,128]{2,1,0:T(8,128)(2,1)S(1)} %get-tuple-element.61.refs_2_.refs_1_, bf16[8,128,512]{2,1,0:T(8,128)(2,1)S(1)} %get-tuple-element.62.refs_4_.refs_2_, ...), custom_call_target="tpu_custom_call" | custom-call | flops 1000000000 | bytes 1000000 | tf_op jit(solution)/shard_map/attend/pallas_call | solution.py:62
  64.4 1.5 %collective-permute-start.22 = (bf16[512,256]{1,0:T(8,128)(2,1)S(1)}, bf16[512,256]{1,0:T(8,128)(2,1)S(1)}, u32[]{:S(2)}, u32[]{:S(2)}) collective-permute-start(bf16[512,256]{1,0:T(8,128)(2,1)S(1)} %attend.4.refs_0_.refs_1_), channel_id=1, source_target_pairs={{0,1},{1,0},{2,3},{3,2},{4,5},{5,4},{6,7},{7,6},{8,9},{9,8},{10,11... | collective-permute-start | bytes 786440 | tf_op jit(solution)/shard_map/ppermute | solution.py:308
  65.9 1.4 %attend.5.refs_0_.refs_3_ = bf16[512,256]{1,0:T(8,128)(2,1)S(1)} custom-call(bf16[512,256]{1,0:T(8,128)(2,1)S(1)} %attend.4.refs_0_.refs_1_, bf16[8,512,128]{2,1,0:T(8,128)(2,1)S(1)} %get-tuple-element.61.refs_2_.refs_1_, bf16[8,128,512]{2,1,0:T(8,128)(2,1)S(1)} %get-tuple-element.62.refs_4_.refs_2_, f32[2,512,128]{2,1,0:T(8,128)S(1)} %get-tuple-element.64.refs_0_.refs_3_, ...), custom_call_target="tpu_custom_call" | custom-call | flops 1000000000 | bytes 1000000 | tf_op jit(solution)/shard_map/attend/pallas_call | solution.py:62
  68.0 1.4 %attend.6.refs_0_.refs_5_ = bf16[512,256]{1,0:T(8,128)(2,1)S(1)} custom-call(bf16[512,256]{1,0:T(8,128)(2,1)S(1)} %attend.5.refs_0_.refs_3_, bf16[8,512,128]{2,1,0:T(8,128)(2,1)S(1)} %get-tuple-element.61.refs_2_.refs_1_, bf16[8,128,512]{2,1,0:T(8,128)(2,1)S(1)} %get-tuple-element.62.refs_4_.refs_2_, f32[2,512,128]{2,1,0:T(8,128)S(1)} %get-tuple-element.65.refs_0_.refs_3_, ...), custom_call_target="tpu_custom_call" | custom-call | flops 1000000000 | bytes 1000000 | tf_op jit(solution)/shard_map/attend/pallas_call | solution.py:62
  69.4 1.5 %collective-permute-start.24 = (bf16[512,256]{1,0:T(8,128)(2,1)S(1)}, bf16[512,256]{1,0:T(8,128)(2,1)S(1)}, u32[]{:S(2)}, u32[]{:S(2)}) collective-permute-start(bf16[512,256]{1,0:T(8,128)(2,1)S(1)} %attend.6.refs_0_.refs_5_), channel_id=1, source_target_pairs={{0,1},{1,0},{2,3},{3,2},{4,5},{5,4},{6,7},{7,6},{8,9},{9,8},{10,11... | collective-permute-start | bytes 786440 | tf_op jit(solution)/shard_map/ppermute | solution.py:308
  71.0 1.4 %attend.7.refs_0_.refs_7_ = bf16[512,256]{1,0:T(8,128)(2,1)S(1)} custom-call(bf16[512,256]{1,0:T(8,128)(2,1)S(1)} %attend.6.refs_0_.refs_5_, bf16[8,512,128]{2,1,0:T(8,128)(2,1)S(1)} %get-tuple-element.61.refs_2_.refs_1_, bf16[8,128,512]{2,1,0:T(8,128)(2,1)S(1)} %get-tuple-element.62.refs_4_.refs_2_, f32[2,512,128]{2,1,0:T(8,128)S(1)} %get-tuple-element.66.refs_0_.refs_3_, ...), custom_call_target="tpu_custom_call" | custom-call | flops 1000000000 | bytes 1000000 | tf_op jit(solution)/shard_map/attend/pallas_call | solution.py:62
  73.0 1.4 %select_bitcast_fusion.1 = (bf16[1,512,1024]{2,1,0:T(8,128)(2,1)S(1)}, bf16[1,512,1024]{2,1,0:T(8,128)(2,1)S(1)}) fusion(bf16[512,1024]{1,0:T(8,128)(2,1)} %collective-permute-done.25, bf16[512,1024]{1,0:T(8,128)(2,1)S(1)} %collective-permute-done.26, pred[]{:T(512)S(6)} %eq.4), kind=kLoop, calls=%fused_computation.2 | loop fusion | flops 1048576 | bytes 4194305 | tf_op jit(solution)/shard_map/stack | solution.py:361
  74.6 10.3 %collective-permute-done.24.refs_6_ = bf16[512,256]{1,0:T(8,128)(2,1)S(1)} collective-permute-done((bf16[512,256]{1,0:T(8,128)(2,1)S(1)}, bf16[512,256]{1,0:T(8,128)(2,1)S(1)}, u32[]{:S(2)}, u32[]{:S(2)}) %collective-permute-start.24) | collective-permute-done | bytes 262176 | tf_op jit(solution)/shard_map/ppermute | solution.py:308
  84.9 2.1 %mix.2.refs_0_.refs_3_ = f32[512,1024]{1,0:T(8,128)S(1)} custom-call(bf16[512,256]{1,0:T(8,128)(2,1)S(1)} %attend.7.refs_0_.refs_7_, bf16[512,256]{1,0:T(8,128)(2,1)S(1)} %attend.4.refs_0_.refs_1_, bf16[512,256]{1,0:T(8,128)(2,1)S(1)} %collective-permute-done.22.refs_2_, bf16[512,256]{1,0:T(8,128)(2,1)S(1)} %attend.5.refs_0_.refs_3_, ...), custom_call_target="tpu_custom_call" | custom-call | flops 1000000000 | bytes 1000000 | tf_op jit(solution)/shard_map/mix/pallas_call | solution.py:62
  87.0 3.1 %collective-permute-done.27.refs_1_ = bf16[512,256]{1,0:T(8,128)(2,1)S(1)} collective-permute-done((bf16[512,256]{1,0:T(8,128)(2,1)S(1)}, bf16[512,256]{1,0:T(8,128)(2,1)S(1)}, u32[]{:S(2)}, u32[]{:S(2)}) %collective-permute-start.27) | collective-permute-done | bytes 262176 | tf_op jit(solution)/shard_map/ppermute | solution.py:308
  90.0 1.4 %mix.3 = bf16[512,1024]{1,0:T(8,128)(2,1)} custom-call(f32[512,1024]{1,0:T(8,128)S(1)} %mix.2.refs_0_.refs_3_, bf16[512,256]{1,0:T(8,128)(2,1)S(1)} %collective-permute-done.27.refs_1_, bf16[1024,1024]{1,0:T(8,128)(2,1)S(1)} %bitcast.7, f32[512,1024]{1,0:T(8,128)S(1)} %mix.2.refs_0_.refs_3_), custom_call_target="tpu_custom_call" | custom-call | flops 1000000000 | bytes 1000000 | tf_op jit(solution)/shard_map/mix/pallas_call | solution.py:62
  (69 shorter events, 11.4 us)
Async XLA Ops:
  0.0 12.1 %collective-permute-start.1 = (bf16[512,8,128]{2,1,0:T(8,128)(2,1)}, bf16[512,8,128]{2,1,0:T(8,128)(2,1)}, u32[]{:S(2)}, u32[]{:S(2)}) collective-permute-start(bf16[512,8,128]{2,1,0:T(8,128)(2,1)} %refs_1_.1), channel_id=1, source_target_pairs={{0,2},{2,0},{4,6},{6,4},{8,10},{10,8},{12,14},{14,12},{16,18},{18,... | collective-permute-start | bytes 3145736 | tf_op jit(solution)/shard_map/ppermute | solution.py:308
  0.5 2.2 %copy-start = (bf16[1024,2048]{1,0:T(8,128)(2,1)S(1)}, bf16[1024,2048]{1,0:T(8,128)(2,1)}, u32[]{:S(2)}) copy-start(bf16[1024,2048]{1,0:T(8,128)(2,1)} %refs_5_.1) | copy-start | bytes 12582916
  2.7 1.2 %copy-start.2 = (bf16[512,8,128]{2,1,0:T(8,128)(2,1)S(1)}, bf16[512,8,128]{2,1,0:T(8,128)(2,1)}, u32[]{:S(2)}) copy-start(bf16[512,8,128]{2,1,0:T(8,128)(2,1)} %refs_0_.1) | copy-start | bytes 3145732
  6.4 4.5 %copy-start.5 = (s32[512,8]{0,1:T(8,128)S(1)}, s32[512,8]{0,1:T(8,128)}, u32[]{:S(2)}) copy-start(s32[512,8]{0,1:T(8,128)} %param.7) | copy-start | bytes 49156
  8.3 26.7 %collective-permute-start.25 = (bf16[512,1024]{1,0:T(8,128)(2,1)}, bf16[512,1024]{1,0:T(8,128)(2,1)}, u32[]{:S(2)}, u32[]{:S(2)}) collective-permute-start(bf16[512,1024]{1,0:T(8,128)(2,1)} %get-tuple-element.96), channel_id=1, source_target_pairs={{0,1},{1,0},{2,3},{3,2},{4,5},{5,4},{6,7},{7,6},{8,9},{9,8},{10,11... | collective-permute-start | bytes 3145736 | tf_op jit(solution)/shard_map/ppermute | solution.py:308
  10.9 1.2 %collective-permute-start = (s32[8,512]{1,0:T(8,128)S(1)}, s32[8,512]{1,0:T(8,128)S(1)}, u32[]{:S(2)}, u32[]{:S(2)}) collective-permute-start(s32[8,512]{1,0:T(8,128)S(1)} %bitcast.8), channel_id=1, source_target_pairs={{0,2},{2,0},{4,6},{6,4},{8,10},{10,8},{12,14},{14,12},{16,18},{18,... | collective-permute-start | bytes 49160 | tf_op jit(solution)/shard_map/ppermute | solution.py:308
  14.0 21.1 %collective-permute-start.2 = (bf16[272,128]{1,0:T(8,128)(2,1)S(1)}, bf16[272,128]{1,0:T(8,128)(2,1)S(1)}, u32[]{:S(2)}, u32[]{:S(2)}) collective-permute-start(bf16[272,128]{1,0:T(8,128)(2,1)S(1)} %get-tuple-element.57), channel_id=1, source_target_pairs={{0,4},{2,6},{4,0},{6,2},{8,12},{10,14},{12,8},{14,10},{16,20},{18,... | collective-permute-start | bytes 208904 | tf_op jit(solution)/shard_map/ppermute | solution.py:308
  16.0 20.9 %collective-permute-start.3 = (bf16[272,128]{1,0:T(8,128)(2,1)S(1)}, bf16[272,128]{1,0:T(8,128)(2,1)S(1)}, u32[]{:S(2)}, u32[]{:S(2)}) collective-permute-start(bf16[272,128]{1,0:T(8,128)(2,1)S(1)} %get-tuple-element.58), channel_id=1, source_target_pairs={{0,4},{2,6},{4,0},{6,2},{8,12},{10,14},{12,8},{14,10},{16,20},{18,... | collective-permute-start | bytes 208904 | tf_op jit(solution)/shard_map/ppermute | solution.py:308
  17.1 20.2 %collective-permute-start.4 = (bf16[272,128]{1,0:T(8,128)(2,1)S(1)}, bf16[272,128]{1,0:T(8,128)(2,1)S(1)}, u32[]{:S(2)}, u32[]{:S(2)}) collective-permute-start(bf16[272,128]{1,0:T(8,128)(2,1)S(1)} %get-tuple-element.59), channel_id=1, source_target_pairs={{0,4},{2,6},{4,0},{6,2},{8,12},{10,14},{12,8},{14,10},{16,20},{18,... | collective-permute-start | bytes 208904 | tf_op jit(solution)/shard_map/ppermute | solution.py:308
  19.1 20.0 %collective-permute-start.5 = (bf16[272,128]{1,0:T(8,128)(2,1)S(1)}, bf16[272,128]{1,0:T(8,128)(2,1)S(1)}, u32[]{:S(2)}, u32[]{:S(2)}) collective-permute-start(bf16[272,128]{1,0:T(8,128)(2,1)S(1)} %get-tuple-element.60), channel_id=1, source_target_pairs={{0,4},{2,6},{4,0},{6,2},{8,12},{10,14},{12,8},{14,10},{16,20},{18,... | collective-permute-start | bytes 208904 | tf_op jit(solution)/shard_map/ppermute | solution.py:308
  35.0 38.0 %collective-permute-start.26 = (bf16[512,1024]{1,0:T(8,128)(2,1)}, bf16[512,1024]{1,0:T(8,128)(2,1)S(1)}, u32[]{:S(2)}, u32[]{:S(2)}) collective-permute-start(bf16[512,1024]{1,0:T(8,128)(2,1)} %collective-permute-done.25), channel_id=1, source_target_pairs={{0,2},{2,0},{4,6},{6,4},{8,10},{10,8},{12,14},{14,12},{16,18},{18,... | collective-permute-start | bytes 3145736 | tf_op jit(solution)/shard_map/ppermute | solution.py:308
  35.1 6.7 %collective-permute-start.6 = (bf16[272,128]{1,0:T(8,128)(2,1)S(1)}, bf16[272,128]{1,0:T(8,128)(2,1)S(1)}, u32[]{:S(2)}, u32[]{:S(2)}) collective-permute-start(bf16[272,128]{1,0:T(8,128)(2,1)S(1)} %plus.8.refs_0_.refs_1_), channel_id=1, source_target_pairs={{0,8},{2,10},{4,12},{6,14},{8,0},{10,2},{12,4},{14,6},{16,24},{18,... | collective-permute-start | bytes 208904 | tf_op jit(solution)/shard_map/ppermute | solution.py:308
  37.0 7.7 %collective-permute-start.7 = (bf16[272,128]{1,0:T(8,128)(2,1)S(1)}, bf16[272,128]{1,0:T(8,128)(2,1)S(1)}, u32[]{:S(2)}, u32[]{:S(2)}) collective-permute-start(bf16[272,128]{1,0:T(8,128)(2,1)S(1)} %plus.9.refs_0_.refs_1_), channel_id=1, source_target_pairs={{0,8},{2,10},{4,12},{6,14},{8,0},{10,2},{12,4},{14,6},{16,24},{18,... | collective-permute-start | bytes 208904 | tf_op jit(solution)/shard_map/ppermute | solution.py:308
  37.3 2.2 %copy-start.1 = (bf16[1024,2048]{1,0:T(8,128)(2,1)S(1)}, bf16[1024,2048]{1,0:T(8,128)(2,1)}, u32[]{:S(2)}) copy-start(bf16[1024,2048]{1,0:T(8,128)(2,1)} %refs_5_.1) | copy-start | bytes 12582916
  37.3 7.6 %collective-permute-start.8 = (bf16[272,128]{1,0:T(8,128)(2,1)S(1)}, bf16[272,128]{1,0:T(8,128)(2,1)S(1)}, u32[]{:S(2)}, u32[]{:S(2)}) collective-permute-start(bf16[272,128]{1,0:T(8,128)(2,1)S(1)} %plus.10.refs_0_.refs_1_), channel_id=1, source_target_pairs={{0,8},{2,10},{4,12},{6,14},{8,0},{10,2},{12,4},{14,6},{16,24},{18,... | collective-permute-start | bytes 208904 | tf_op jit(solution)/shard_map/ppermute | solution.py:308
  39.2 8.6 %collective-permute-start.9 = (bf16[272,128]{1,0:T(8,128)(2,1)S(1)}, bf16[272,128]{1,0:T(8,128)(2,1)S(1)}, u32[]{:S(2)}, u32[]{:S(2)}) collective-permute-start(bf16[272,128]{1,0:T(8,128)(2,1)S(1)} %plus.11.refs_0_.refs_1_), channel_id=1, source_target_pairs={{0,8},{2,10},{4,12},{6,14},{8,0},{10,2},{12,4},{14,6},{16,24},{18,... | collective-permute-start | bytes 208904 | tf_op jit(solution)/shard_map/ppermute | solution.py:308
  41.8 11.4 %collective-permute-start.10 = (bf16[272,128]{1,0:T(8,128)(2,1)S(1)}, bf16[272,128]{1,0:T(8,128)(2,1)S(1)}, u32[]{:S(2)}, u32[]{:S(2)}) collective-permute-start(bf16[272,128]{1,0:T(8,128)(2,1)S(1)} %plus.12.refs_0_), channel_id=1, source_target_pairs={{0,16},{2,18},{4,20},{6,22},{8,24},{10,26},{12,28},{14,30},{16,0},... | collective-permute-start | bytes 208904 | tf_op jit(solution)/shard_map/ppermute | solution.py:308
  44.7 10.4 %collective-permute-start.11 = (bf16[272,128]{1,0:T(8,128)(2,1)S(1)}, bf16[272,128]{1,0:T(8,128)(2,1)S(1)}, u32[]{:S(2)}, u32[]{:S(2)}) collective-permute-start(bf16[272,128]{1,0:T(8,128)(2,1)S(1)} %plus.13.refs_0_), channel_id=1, source_target_pairs={{0,16},{2,18},{4,20},{6,22},{8,24},{10,26},{12,28},{14,30},{16,0},... | collective-permute-start | bytes 208904 | tf_op jit(solution)/shard_map/ppermute | solution.py:308
  44.9 12.0 %collective-permute-start.12 = (bf16[272,128]{1,0:T(8,128)(2,1)S(1)}, bf16[272,128]{1,0:T(8,128)(2,1)S(1)}, u32[]{:S(2)}, u32[]{:S(2)}) collective-permute-start(bf16[272,128]{1,0:T(8,128)(2,1)S(1)} %plus.14.refs_0_), channel_id=1, source_target_pairs={{0,16},{2,18},{4,20},{6,22},{8,24},{10,26},{12,28},{14,30},{16,0},... | collective-permute-start | bytes 208904 | tf_op jit(solution)/shard_map/ppermute | solution.py:308
  47.8 10.5 %collective-permute-start.13 = (bf16[272,128]{1,0:T(8,128)(2,1)S(1)}, bf16[272,128]{1,0:T(8,128)(2,1)S(1)}, u32[]{:S(2)}, u32[]{:S(2)}) collective-permute-start(bf16[272,128]{1,0:T(8,128)(2,1)S(1)} %plus.15.refs_0_), channel_id=1, source_target_pairs={{0,16},{2,18},{4,20},{6,22},{8,24},{10,26},{12,28},{14,30},{16,0},... | collective-permute-start | bytes 208904 | tf_op jit(solution)/shard_map/ppermute | solution.py:308
  53.3 6.1 %collective-permute-start.14 = (bf16[272,128]{1,0:T(8,128)(2,1)S(1)}, bf16[272,128]{1,0:T(8,128)(2,1)S(1)}, u32[]{:S(2)}, u32[]{:S(2)}) collective-permute-start(bf16[272,128]{1,0:T(8,128)(2,1)S(1)} %get-tuple-element.71), channel_id=1, source_target_pairs={{0,4},{2,6},{4,0},{6,2},{8,12},{10,14},{12,8},{14,10},{16,20},{18,... | collective-permute-start | bytes 208904 | tf_op jit(solution)/shard_map/ppermute | solution.py:308
  55.2 4.8 %collective-permute-start.15 = (bf16[272,128]{1,0:T(8,128)(2,1)S(1)}, bf16[272,128]{1,0:T(8,128)(2,1)S(1)}, u32[]{:S(2)}, u32[]{:S(2)}) collective-permute-start(bf16[272,128]{1,0:T(8,128)(2,1)S(1)} %get-tuple-element.74), channel_id=1, source_target_pairs={{0,4},{2,6},{4,0},{6,2},{8,12},{10,14},{12,8},{14,10},{16,20},{18,... | collective-permute-start | bytes 208904 | tf_op jit(solution)/shard_map/ppermute | solution.py:308
  57.0 4.6 %collective-permute-start.16 = (bf16[272,128]{1,0:T(8,128)(2,1)S(1)}, bf16[272,128]{1,0:T(8,128)(2,1)S(1)}, u32[]{:S(2)}, u32[]{:S(2)}) collective-permute-start(bf16[272,128]{1,0:T(8,128)(2,1)S(1)} %get-tuple-element.77), channel_id=1, source_target_pairs={{0,4},{2,6},{4,0},{6,2},{8,12},{10,14},{12,8},{14,10},{16,20},{18,... | collective-permute-start | bytes 208904 | tf_op jit(solution)/shard_map/ppermute | solution.py:308
  58.5 4.4 %collective-permute-start.17 = (bf16[272,128]{1,0:T(8,128)(2,1)S(1)}, bf16[272,128]{1,0:T(8,128)(2,1)S(1)}, u32[]{:S(2)}, u32[]{:S(2)}) collective-permute-start(bf16[272,128]{1,0:T(8,128)(2,1)S(1)} %get-tuple-element.80), channel_id=1, source_target_pairs={{0,4},{2,6},{4,0},{6,2},{8,12},{10,14},{12,8},{14,10},{16,20},{18,... | collective-permute-start | bytes 208904 | tf_op jit(solution)/shard_map/ppermute | solution.py:308
  59.5 3.5 %collective-permute-start.18 = (bf16[2,272,128]{2,1,0:T(8,128)(2,1)S(1)}, bf16[2,272,128]{2,1,0:T(8,128)(2,1)S(1)}, u32[]{:S(2)}, u32[]{:S(2)}) collective-permute-start(bf16[2,272,128]{2,1,0:T(8,128)(2,1)S(1)} %get-tuple-element.85), channel_id=1, source_target_pairs={{0,2},{2,0},{4,6},{6,4},{8,10},{10,8},{12,14},{14,12},{16,18},{18,... | collective-permute-start | bytes 417800 | tf_op jit(solution)/shard_map/ppermute | solution.py:308
  60.1 5.8 %collective-permute-start.19 = (bf16[2,272,128]{2,1,0:T(8,128)(2,1)S(1)}, bf16[2,272,128]{2,1,0:T(8,128)(2,1)S(1)}, u32[]{:S(2)}, u32[]{:S(2)}) collective-permute-start(bf16[2,272,128]{2,1,0:T(8,128)(2,1)S(1)} %get-tuple-element.88), channel_id=1, source_target_pairs={{0,2},{2,0},{4,6},{6,4},{8,10},{10,8},{12,14},{14,12},{16,18},{18,... | collective-permute-start | bytes 417800 | tf_op jit(solution)/shard_map/ppermute | solution.py:308
  61.6 6.4 %collective-permute-start.20 = (bf16[2,272,128]{2,1,0:T(8,128)(2,1)S(1)}, bf16[2,272,128]{2,1,0:T(8,128)(2,1)S(1)}, u32[]{:S(2)}, u32[]{:S(2)}) collective-permute-start(bf16[2,272,128]{2,1,0:T(8,128)(2,1)S(1)} %get-tuple-element.91), channel_id=1, source_target_pairs={{0,2},{2,0},{4,6},{6,4},{8,10},{10,8},{12,14},{14,12},{16,18},{18,... | collective-permute-start | bytes 417800 | tf_op jit(solution)/shard_map/ppermute | solution.py:308
  62.9 8.1 %collective-permute-start.21 = (bf16[2,272,128]{2,1,0:T(8,128)(2,1)S(1)}, bf16[2,272,128]{2,1,0:T(8,128)(2,1)S(1)}, u32[]{:S(2)}, u32[]{:S(2)}) collective-permute-start(bf16[2,272,128]{2,1,0:T(8,128)(2,1)S(1)} %get-tuple-element.94), channel_id=1, source_target_pairs={{0,2},{2,0},{4,6},{6,4},{8,10},{10,8},{12,14},{14,12},{16,18},{18,... | collective-permute-start | bytes 417800 | tf_op jit(solution)/shard_map/ppermute | solution.py:308
  64.4 20.5 %collective-permute-start.22 = (bf16[512,256]{1,0:T(8,128)(2,1)S(1)}, bf16[512,256]{1,0:T(8,128)(2,1)S(1)}, u32[]{:S(2)}, u32[]{:S(2)}) collective-permute-start(bf16[512,256]{1,0:T(8,128)(2,1)S(1)} %attend.4.refs_0_.refs_1_), channel_id=1, source_target_pairs={{0,1},{1,0},{2,3},{3,2},{4,5},{5,4},{6,7},{7,6},{8,9},{9,8},{10,11... | collective-permute-start | bytes 786440 | tf_op jit(solution)/shard_map/ppermute | solution.py:308
  67.4 17.5 %collective-permute-start.23 = (bf16[512,256]{1,0:T(8,128)(2,1)S(1)}, bf16[512,256]{1,0:T(8,128)(2,1)S(1)}, u32[]{:S(2)}, u32[]{:S(2)}) collective-permute-start(bf16[512,256]{1,0:T(8,128)(2,1)S(1)} %attend.5.refs_0_.refs_3_), channel_id=1, source_target_pairs={{0,1},{1,0},{2,3},{3,2},{4,5},{5,4},{6,7},{7,6},{8,9},{9,8},{10,11... | collective-permute-start | bytes 786440 | tf_op jit(solution)/shard_map/ppermute | solution.py:308
  69.4 15.4 %collective-permute-start.24 = (bf16[512,256]{1,0:T(8,128)(2,1)S(1)}, bf16[512,256]{1,0:T(8,128)(2,1)S(1)}, u32[]{:S(2)}, u32[]{:S(2)}) collective-permute-start(bf16[512,256]{1,0:T(8,128)(2,1)S(1)} %attend.6.refs_0_.refs_5_), channel_id=1, source_target_pairs={{0,1},{1,0},{2,3},{3,2},{4,5},{5,4},{6,7},{7,6},{8,9},{9,8},{10,11... | collective-permute-start | bytes 786440 | tf_op jit(solution)/shard_map/ppermute | solution.py:308
  72.4 17.6 %collective-permute-start.27 = (bf16[512,256]{1,0:T(8,128)(2,1)S(1)}, bf16[512,256]{1,0:T(8,128)(2,1)S(1)}, u32[]{:S(2)}, u32[]{:S(2)}) collective-permute-start(bf16[512,256]{1,0:T(8,128)(2,1)S(1)} %attend.7.refs_0_.refs_7_), channel_id=1, source_target_pairs={{0,1},{1,0},{2,3},{3,2},{4,5},{5,4},{6,7},{7,6},{8,9},{9,8},{10,11... | collective-permute-start | bytes 786440 | tf_op jit(solution)/shard_map/ppermute | solution.py:308
  (2 other events, 2.4 us)
